TPU v7x, 128 devices: a whole 4x4x4 slice. The times are simulated.
128 devices in a mesh: dp: 1, tp: 16 (over z, y), sp: 8 (over x, core).
Axes of the slice: x: 4, y: 4, z: 4, core: 2. Of those that a mesh axis runs over, the one named last changes fastest.
Arguments:
- x_seq: bfloat16 [16384, 4608], P(('dp', 'sp', 'tp'))
- w_query: bfloat16 [4608, 32, 128], P(None, 'tp')
- w_key: bfloat16 [4608, 16, 128], P(None, 'tp')
- w_value: bfloat16 [4608, 16, 128], P(None, 'tp')
- w_out: bfloat16 [32, 128, 4608], P('tp')
Outputs:
- output: bfloat16 [16384, 4608], P(('dp', 'sp', 'tp'))
All inputs are finite; a program needn't handle non-finite values.
Results may differ from a plain program's by a relative error of at most 0.00875352.
Values are sent between devices in bfloat16 or wider.
A program may use at most 1 GiB of HBM per device.

v0:
```python
import jax
import jax.numpy as jnp
from jax import lax
from jax.sharding import PartitionSpec as P

WINDOW = 4096
NEG_BIG = -1e30


def block_update(soft_state, q_blk, k_blk, v_blk, chunk_gap, score_scale):
    row_max, row_sum, acc_sum = soft_state
    chunk_len = q_blk.shape[0]
    scores = jnp.einsum("qhgd,khd->hgqk", q_blk, k_blk, preferred_element_type=jnp.float32) * score_scale
    offset = chunk_gap * chunk_len + lax.broadcasted_iota(jnp.int32, (chunk_len, chunk_len), 0) - lax.broadcasted_iota(jnp.int32, (chunk_len, chunk_len), 1)
    visible = (offset >= 0) & (offset < WINDOW)
    scores = jnp.where(visible, scores, NEG_BIG)
    new_max = jnp.maximum(row_max, jnp.max(scores, axis=-1))
    prob_blk = jnp.where(visible, jnp.exp(scores - new_max[..., None]), 0.0)
    rescale = jnp.exp(row_max - new_max)
    new_sum = row_sum * rescale + jnp.sum(prob_blk, axis=-1)
    new_acc = acc_sum * rescale[..., None] + jnp.einsum("hgqk,khd->hgqd", prob_blk.astype(jnp.bfloat16), v_blk, preferred_element_type=jnp.float32)
    return new_max, new_sum, new_acc


def pair_update(soft_state, q_blk, k_blk, v_blk, q_id, k_id, score_scale):
    chunk_len = q_blk.shape[0]
    chunk_gap = q_id - k_id
    needed = (chunk_gap >= 0) & (chunk_gap * chunk_len - chunk_len + 1 < WINDOW)
    return lax.cond(needed, lambda cur_state: block_update(cur_state, q_blk, k_blk, v_blk, chunk_gap, score_scale), lambda cur_state: cur_state, soft_state)


def solution(mesh):
    sp_size = mesh.shape["sp"]
    next_pairs = [(src_idx, (src_idx + 1) % sp_size) for src_idx in range(sp_size)]

    def local_attn(x_part, w_query, w_key, w_value, w_out):
        x_block = lax.all_gather(x_part, "tp", axis=0, tiled=True)
        block_rows, d_model = x_block.shape
        chunk_len = block_rows // 2
        heads_loc, head_dim = w_query.shape[1], w_query.shape[2]
        kv_loc = w_key.shape[1]
        group_size = heads_loc // kv_loc
        score_scale = head_dim ** -0.5
        q_loc = jnp.dot(x_block, w_query.reshape(d_model, heads_loc * head_dim), preferred_element_type=jnp.float32).astype(jnp.bfloat16).reshape(2, chunk_len, kv_loc, group_size, head_dim)
        k_loc = jnp.dot(x_block, w_key.reshape(d_model, kv_loc * head_dim), preferred_element_type=jnp.float32).astype(jnp.bfloat16).reshape(2, chunk_len, kv_loc, head_dim)
        v_loc = jnp.dot(x_block, w_value.reshape(d_model, kv_loc * head_dim), preferred_element_type=jnp.float32).astype(jnp.bfloat16).reshape(2, chunk_len, kv_loc, head_dim)
        sp_rank = lax.axis_index("sp")
        own_ids = (sp_rank, 2 * sp_size - 1 - sp_rank)

        def fresh_state():
            return (jnp.full((kv_loc, group_size, chunk_len), NEG_BIG, jnp.float32), jnp.zeros((kv_loc, group_size, chunk_len), jnp.float32), jnp.zeros((kv_loc, group_size, chunk_len, head_dim), jnp.float32))

        def absorb(states, k_blocks, v_blocks, src_rank):
            key_ids = (src_rank, 2 * sp_size - 1 - src_rank)
            updated = []
            for q_half in range(2):
                cur_state = states[q_half]
                for k_half in range(2):
                    cur_state = pair_update(cur_state, q_loc[q_half], k_blocks[k_half], v_blocks[k_half], own_ids[q_half], key_ids[k_half], score_scale)
                updated.append(cur_state)
            return tuple(updated)

        states = absorb((fresh_state(), fresh_state()), k_loc, v_loc, sp_rank)

        def ring_free_step(step_idx, carry):
            k_blocks, v_blocks, cur_states = carry
            k_blocks, v_blocks = lax.ppermute((k_blocks, v_blocks), "sp", next_pairs)
            src_rank = (sp_rank - step_idx) % sp_size
            return k_blocks, v_blocks, absorb(cur_states, k_blocks, v_blocks, src_rank)

        carry_out = lax.fori_loop(1, sp_size, ring_free_step, (k_loc, v_loc, states))
        states = carry_out[2]
        outs_norm = jnp.stack([(soft_state[2] / soft_state[1][..., None]).astype(jnp.bfloat16) for soft_state in states])
        part_sum = jnp.einsum("ahgqd,hgde->aqe", outs_norm, w_out.reshape(kv_loc, group_size, head_dim, d_model), preferred_element_type=jnp.float32).reshape(block_rows, d_model)
        y_rows = lax.psum_scatter(part_sum, "tp", scatter_dimension=0, tiled=True)
        return y_rows.astype(jnp.bfloat16)

    return jax.shard_map(local_attn, mesh=mesh, in_specs=(P(("dp", "sp", "tp"), None), P(None, "tp", None), P(None, "tp", None), P(None, "tp", None), P("tp", None, None)), out_specs=P(("dp", "sp", "tp"), None), check_vma=False)
```

profile of v0, /device:TPU:1, one launch (start us, length us, event | category | flops | bytes accessed | tf_op | source)
XLA Modules:
  0.0 688.8 jit_solution(10622907385313878778)
XLA Ops:
  7.7 126.8 %all-gather.2.cloned.1.call-done = bf16[2048,4608]{1,0:T(8,128)(2,1)} async-done(((bf16[128,4608]{1,0:T(8,128)(2,1)}), bf16[2048,4608]{1,0:T(8,128)(2,1)}) %all-gather.2.cloned.1.call-update) | async-done | bytes 18874384 | tf_op jit(solution)/shard_map/all_gather | solution.py:37
  134.5 10.5 %convolution_convert_fusion = bf16[2048,256]{0,1:T(8,128)(2,1)} fusion(bf16[2048,4608]{1,0:T(8,128)(2,1)} %all-gather.2.cloned.1.call-done, bf16[576,8,2,128]{3,2,1,0:T(2,128)(2,1)} %bitcast.465), kind=kOutput, calls=%fused_computation.181 | convolution fusion | flops 4832362496 | bytes 22282240 | tf_op jit(solution)/shard_map/dot_general | solution.py:44
  144.9 2.6 reshape.333
  147.5 2.2 fusion.196
  149.8 3.7 copy.22
  153.5 11.4 %convolution_convert_fusion.1 = bf16[2048,128]{1,0:T(8,128)(2,1)S(1)} fusion(bf16[2048,4608]{1,0:T(8,128)(2,1)} %all-gather.2.cloned.1.call-done, bf16[4608,1,128]{2,0,1:T(8,128)(2,1)} %param.22), kind=kOutput, calls=%fused_computation.182 | convolution fusion | flops 2416181248 | bytes 20578304 | tf_op jit(solution)/shard_map/dot_general | solution.py:46
  165.8 5.1 convolution_convert_fusion.2
  173.2 6.6 fusion.143
  181.2 7.2 %fusion.170 = f32[1,2,1024,128]{3,2,1,0:T(8,128)} fusion(f32[1024,1024,2]{1,0,2:T(8,128)} %copy-done.1, f32[2,1024]{1,0:T(2,128)S(1)} %get-tuple-element.770, pred[1024,1024]{0,1:T(8,128)(4,1)S(1)} %fusion.156, f32[2,1024]{1,0:T(2,128)S(1)} %get-tuple-element.768, bf16[2048,128]{1,0:T(8,128)(2,1)} %copy-done.20), kind=kOutput, calls=%fused_computation.189 | convolution fusion | flops 547618816 | bytes 10764288 | tf_op jit(solution)/shard_map/cond/branch_1_fun/hgqk,khd->hgqd/dot_general | solution.py:21
  188.4 1.4 copy-done.3
  189.7 4.1 fusion.147
  193.9 5.0 fusion.164
  198.9 231.0 %while.32 = (s32[]{:T(128)}, bf16[2,1024,1,128]{3,1,2,0:T(8,128)(2,1)}, bf16[2,1024,1,128]{3,1,2,0:T(8,128)(2,1)}, f32[1,2,1024]{2,1,0:T(2,128)S(1)}, f32[1,2,10...) while((s32[]{:T(128)}, ...), condition=%wide.region_29.30_spmd, body=%wide.region_12.29_spmd.sunk | while | flops 4422922240 | bytes 178816432 | solution.py:71
  213.3 2.0 collective-permute-start.1
  215.3 2.2 slice_bitcast_fusion.10
  217.5 3.8 collective-permute-done.1
  222.2 4.8 collective-permute-done
  227.8 11.0 %conditional.12 = ((f32[1,2,1024]{2,1,0:T(2,128)S(1)}, f32[1,2,1024]{2,1,0:T(2,128)S(1)}, f32[1,2,1024,128]{3,2,1,0:T(8,128)})) conditional(s32[]{:T(128)} %convert_element_type.194, (f32[1,2,1024]{2,1,0:T(2,128)S(1)}, f32[1,2,1024]{2,1,0:T(2,128)S(1)}, f32[1,2,1024,128]{3,2,1,0:T(8,128)}) %tuple.137, (s32[]{:T(128)}, ...), branch_computations={%region_13.13_spmd, %region_14.16_spmd} | conditional | flops 1105730560 | bytes 42082436 | solution.py:29
  229.0 3.0 fusion.46
  232.1 2.3 fusion.48
  234.3 3.5 fusion.59
  240.4 2.5 collective-permute-start.1
  242.9 2.2 slice_bitcast_fusion.10
  245.2 3.8 collective-permute-done.1
  249.8 4.8 collective-permute-done
  257.1 13.5 %collective-permute-start.1 = (bf16[2,1024,1,128]{3,1,2,0:T(8,128)(2,1)}, bf16[2,1024,1,128]{3,1,2,0:T(8,128)(2,1)S(1)}, u32[]{:S(2)}, u32[]{:S(2)}) collective-permute-start(bf16[2,1024,1,128]{3,1,2,0:T(8,128)(2,1)} %get-tuple-element.941), channel_id=1, source_target_pairs={{0,1},{1,2},{2,3},{3,4},{4,5},{5,6},{6,7},{7,0},{8,9},{9,10},{10,1... | collective-permute-start | bytes 1572872 | tf_op jit(solution)/shard_map/while/body/eval_jaxpr/ppermute | solution.py:67
  270.6 1.6 collective-permute-start
  272.2 2.2 slice_bitcast_fusion.10
  274.4 3.5 collective-permute-done.1
  278.7 3.5 collective-permute-done
  284.7 3.5 collective-permute-start.1
  288.2 22.6 %collective-permute-start = (bf16[2,1024,1,128]{3,1,2,0:T(8,128)(2,1)}, bf16[2,1024,1,128]{3,1,2,0:T(8,128)(2,1)S(1)}, u32[]{:S(2)}, u32[]{:S(2)}) collective-permute-start(bf16[2,1024,1,128]{3,1,2,0:T(8,128)(2,1)} %get-tuple-element.940), channel_id=1, source_target_pairs={{0,1},{1,2},{2,3},{3,4},{4,5},{5,6},{6,7},{7,0},{8,9},{9,10},{10,1... | collective-permute-start | bytes 1572872 | tf_op jit(solution)/shard_map/while/body/eval_jaxpr/ppermute | solution.py:67
  310.8 2.2 slice_bitcast_fusion.10
  314.9 2.1 collective-permute-done
  317.7 9.9 %conditional.15 = ((f32[1,2,1024]{2,1,0:T(2,128)S(1)}, f32[1,2,1024]{2,1,0:T(2,128)S(1)}, f32[1,2,1024,128]{3,2,1,0:T(8,128)})) conditional(s32[]{:T(128)} %convert_element_type.195, (f32[1,2,1024]{2,1,0:T(2,128)S(1)}, f32[1,2,1024]{2,1,0:T(2,128)S(1)}, f32[1,2,1024,128]{3,2,1,0:T(8,128)}) %get-tuple-element.982, (s32[]{:T(128)}, ...), branch_computations={%region_25.25_spmd, %region_26.0_spmd} | conditional | flops 1105730560 | bytes 42082436 | solution.py:29
  318.9 2.9 fusion.118
  321.9 3.5 fusion.131
  325.4 2.3 fusion.120
  329.4 2.5 collective-permute-start.1
  331.9 5.6 collective-permute-start
  337.5 2.2 slice_bitcast_fusion.10
  339.7 20.4 %collective-permute-done.1 = bf16[2,1024,1,128]{3,1,2,0:T(8,128)(2,1)S(1)} collective-permute-done((bf16[2,1024,1,128]{3,1,2,0:T(8,128)(2,1)}, bf16[2,1024,1,128]{3,1,2,0:T(8,128)(2,1)S(1)}, u32[]{:S(2)}, u32[]{:S(2)}) %collective-permute-start.1) | collective-permute-done | bytes 524320 | tf_op jit(solution)/shard_map/while/body/eval_jaxpr/ppermute | solution.py:67
  361.8 9.9 %conditional.15 = ((f32[1,2,1024]{2,1,0:T(2,128)S(1)}, f32[1,2,1024]{2,1,0:T(2,128)S(1)}, f32[1,2,1024,128]{3,2,1,0:T(8,128)})) conditional(s32[]{:T(128)} %convert_element_type.195, (f32[1,2,1024]{2,1,0:T(2,128)S(1)}, f32[1,2,1024]{2,1,0:T(2,128)S(1)}, f32[1,2,1024,128]{3,2,1,0:T(8,128)}) %get-tuple-element.982, (s32[]{:T(128)}, ...), branch_computations={%region_25.25_spmd, %region_26.0_spmd} | conditional | flops 1105730560 | bytes 42082436 | solution.py:29
  363.0 2.9 fusion.118
  365.9 3.5 fusion.131
  369.4 2.3 fusion.120
  373.5 2.2 slice_bitcast_fusion.10
  375.8 12.2 %collective-permute-done.1 = bf16[2,1024,1,128]{3,1,2,0:T(8,128)(2,1)S(1)} collective-permute-done((bf16[2,1024,1,128]{3,1,2,0:T(8,128)(2,1)}, bf16[2,1024,1,128]{3,1,2,0:T(8,128)(2,1)S(1)}, u32[]{:S(2)}, u32[]{:S(2)}) %collective-permute-start.1) | collective-permute-done | bytes 524320 | tf_op jit(solution)/shard_map/while/body/eval_jaxpr/ppermute | solution.py:67
  389.7 9.9 %conditional.15 = ((f32[1,2,1024]{2,1,0:T(2,128)S(1)}, f32[1,2,1024]{2,1,0:T(2,128)S(1)}, f32[1,2,1024,128]{3,2,1,0:T(8,128)})) conditional(s32[]{:T(128)} %convert_element_type.195, (f32[1,2,1024]{2,1,0:T(2,128)S(1)}, f32[1,2,1024]{2,1,0:T(2,128)S(1)}, f32[1,2,1024,128]{3,2,1,0:T(8,128)}) %get-tuple-element.982, (s32[]{:T(128)}, ...), branch_computations={%region_25.25_spmd, %region_26.0_spmd} | conditional | flops 1105730560 | bytes 42082436 | solution.py:29
  390.8 2.9 fusion.118
  393.8 3.5 fusion.131
  397.3 2.3 fusion.120
  402.6 8.6 %collective-permute-start = (bf16[2,1024,1,128]{3,1,2,0:T(8,128)(2,1)}, bf16[2,1024,1,128]{3,1,2,0:T(8,128)(2,1)S(1)}, u32[]{:S(2)}, u32[]{:S(2)}) collective-permute-start(bf16[2,1024,1,128]{3,1,2,0:T(8,128)(2,1)} %get-tuple-element.940), channel_id=1, source_target_pairs={{0,1},{1,2},{2,3},{3,4},{4,5},{5,6},{6,7},{7,0},{8,9},{9,10},{10,1... | collective-permute-start | bytes 1572872 | tf_op jit(solution)/shard_map/while/body/eval_jaxpr/ppermute | solution.py:67
  411.2 2.2 slice_bitcast_fusion.10
  413.4 2.5 collective-permute-done.1
  418.1 9.9 %conditional.15 = ((f32[1,2,1024]{2,1,0:T(2,128)S(1)}, f32[1,2,1024]{2,1,0:T(2,128)S(1)}, f32[1,2,1024,128]{3,2,1,0:T(8,128)})) conditional(s32[]{:T(128)} %convert_element_type.195, (f32[1,2,1024]{2,1,0:T(2,128)S(1)}, f32[1,2,1024]{2,1,0:T(2,128)S(1)}, f32[1,2,1024,128]{3,2,1,0:T(8,128)}) %get-tuple-element.982, (s32[]{:T(128)}, ...), branch_computations={%region_25.25_spmd, %region_26.0_spmd} | conditional | flops 1105730560 | bytes 42082436 | solution.py:29
  419.3 2.9 fusion.118
  422.3 3.5 fusion.131
  425.8 2.3 fusion.120
  429.9 1.6 fusion.175
  431.5 1.6 fusion.176
  433.3 14.2 %convolution_bitcast_fusion = f32[2048,4608]{1,0:T(8,128)} fusion(bf16[2048,128,2]{1,0,2:T(8,128)(2,1)S(1)} %bitcast.446, bf16[2,128,4608]{2,1,0:T(8,128)(2,1)S(1)} %copy-done), kind=kOutput, calls=%fused_computation.160 | convolution fusion | flops 4831838208 | bytes 41156608 | tf_op jit(solution)/shard_map/ahgqd,hgde->aqe/dot_general | solution.py:74
  447.5 231.4 %reduce-scatter.2.cloned.1.call-done = f32[128,4608]{1,0:T(8,128)} async-done(((f32[2048,4608]{1,0:T(8,128)}), f32[128,4608]{1,0:T(8,128)}) %reduce-scatter.2.cloned.1.call-update) | async-done | bytes 2359312 | tf_op jit(solution)/shard_map/reduce_scatter | solution.py:75
  678.9 2.8 convert_element_type.115
  (152 shorter events, 39.9 us)
Async XLA Ops:
  6.5 426.7 %copy-start = (bf16[2,128,4608]{2,1,0:T(8,128)(2,1)S(1)}, bf16[2,128,4608]{2,1,0:T(8,128)(2,1)}, u32[]{:S(2)}) copy-start(bf16[2,128,4608]{2,1,0:T(8,128)(2,1)} %param.23) | copy-start | bytes 7077892
  6.5 127.9 %all-gather.2.cloned.1.call-start = ((), (), s32[]{:S(2)}) async-start(), calls=%async_computation.1 | async-start | bytes 20054016 | tf_op jit(solution)/shard_map/all_gather | solution.py:37
  7.3 671.7 %reduce-scatter.2.cloned.1.call-start = ((), (), s32[]{:S(2)}) async-start(), calls=%async_computation.2 | async-start | bytes 40108032 | tf_op jit(solution)/shard_map/reduce_scatter | solution.py:75
  153.4 12.1 %copy-start.24 = (bf16[2048,4608]{1,0:T(8,128)(2,1)S(1)}, bf16[2048,4608]{1,0:T(8,128)(2,1)}, u32[]{:S(2)}) copy-start(bf16[2048,4608]{1,0:T(8,128)(2,1)} %all-gather.2.cloned.1.call-done) | copy-start | bytes 56623108
  153.4 12.3 %copy-start.25 = (bf16[4608,1,128]{2,0,1:T(8,128)(2,1)S(1)}, bf16[4608,1,128]{2,0,1:T(8,128)(2,1)}, u32[]{:S(2)}) copy-start(bf16[4608,1,128]{2,0,1:T(8,128)(2,1)} %param.21) | copy-start | bytes 3538948
  165.8 5.1 copy-start.20
  165.8 6.1 copy-start.8
  170.9 8.9 %copy-start.9 = (bf16[2048,128]{1,0:T(8,128)(2,1)}, bf16[2048,128]{1,0:T(8,128)(2,1)S(1)}, u32[]{:S(2)}) copy-start(bf16[2048,128]{1,0:T(8,128)(2,1)S(1)} %convolution_convert_fusion.2) | copy-start | bytes 1572868
  173.2 6.6 copy-start.1
  181.1 7.2 %copy-start.2 = (f32[1024,1024,2]{1,0,2:T(8,128)S(1)}, f32[1024,1024,2]{1,0,2:T(8,128)}, u32[]{:S(2)}) copy-start(f32[1024,1024,2]{1,0,2:T(8,128)} %copy-done.1) | copy-start | bytes 25165828
  181.1 8.6 %copy-start.3 = (f32[1024,1024,2]{1,0,2:T(8,128)S(1)}, f32[1024,1024,2]{1,0,2:T(8,128)}, u32[]{:S(2)}) copy-start(f32[1024,1024,2]{1,0,2:T(8,128)} %get-tuple-element.771) | copy-start | bytes 25165828
  189.7 4.2 copy-start.21
  213.3 8.1 %collective-permute-start.1 = (bf16[2,1024,1,128]{3,1,2,0:T(8,128)(2,1)}, bf16[2,1024,1,128]{3,1,2,0:T(8,128)(2,1)S(1)}, u32[]{:S(2)}, u32[]{:S(2)}) collective-permute-start(bf16[2,1024,1,128]{3,1,2,0:T(8,128)(2,1)} %get-tuple-element.941), channel_id=1, source_target_pairs={{0,1},{1,2},{2,3},{3,4},{4,5},{5,6},{6,7},{7,0},{8,9},{9,10},{10,1... | collective-permute-start | bytes 1572872 | tf_op jit(solution)/shard_map/while/body/eval_jaxpr/ppermute | solution.py:67
  215.3 11.7 %collective-permute-start = (bf16[2,1024,1,128]{3,1,2,0:T(8,128)(2,1)}, bf16[2,1024,1,128]{3,1,2,0:T(8,128)(2,1)S(1)}, u32[]{:S(2)}, u32[]{:S(2)}) collective-permute-start(bf16[2,1024,1,128]{3,1,2,0:T(8,128)(2,1)} %get-tuple-element.940), channel_id=1, source_target_pairs={{0,1},{1,2},{2,3},{3,4},{4,5},{5,6},{6,7},{7,0},{8,9},{9,10},{10,1... | collective-permute-start | bytes 1572872 | tf_op jit(solution)/shard_map/while/body/eval_jaxpr/ppermute | solution.py:67
  229.0 5.3 copy-start.7
  229.0 5.3 copy-start.16
  237.8 1.0 copy-start.17
  240.4 8.6 %collective-permute-start.1 = (bf16[2,1024,1,128]{3,1,2,0:T(8,128)(2,1)}, bf16[2,1024,1,128]{3,1,2,0:T(8,128)(2,1)S(1)}, u32[]{:S(2)}, u32[]{:S(2)}) collective-permute-start(bf16[2,1024,1,128]{3,1,2,0:T(8,128)(2,1)} %get-tuple-element.941), channel_id=1, source_target_pairs={{0,1},{1,2},{2,3},{3,4},{4,5},{5,6},{6,7},{7,0},{8,9},{9,10},{10,1... | collective-permute-start | bytes 1572872 | tf_op jit(solution)/shard_map/while/body/eval_jaxpr/ppermute | solution.py:67
  242.9 11.7 %collective-permute-start = (bf16[2,1024,1,128]{3,1,2,0:T(8,128)(2,1)}, bf16[2,1024,1,128]{3,1,2,0:T(8,128)(2,1)S(1)}, u32[]{:S(2)}, u32[]{:S(2)}) collective-permute-start(bf16[2,1024,1,128]{3,1,2,0:T(8,128)(2,1)} %get-tuple-element.940), channel_id=1, source_target_pairs={{0,1},{1,2},{2,3},{3,4},{4,5},{5,6},{6,7},{7,0},{8,9},{9,10},{10,1... | collective-permute-start | bytes 1572872 | tf_op jit(solution)/shard_map/while/body/eval_jaxpr/ppermute | solution.py:67
  257.1 20.8 %collective-permute-start.1 = (bf16[2,1024,1,128]{3,1,2,0:T(8,128)(2,1)}, bf16[2,1024,1,128]{3,1,2,0:T(8,128)(2,1)S(1)}, u32[]{:S(2)}, u32[]{:S(2)}) collective-permute-start(bf16[2,1024,1,128]{3,1,2,0:T(8,128)(2,1)} %get-tuple-element.941), channel_id=1, source_target_pairs={{0,1},{1,2},{2,3},{3,4},{4,5},{5,6},{6,7},{7,0},{8,9},{9,10},{10,1... | collective-permute-start | bytes 1572872 | tf_op jit(solution)/shard_map/while/body/eval_jaxpr/ppermute | solution.py:67
  270.6 11.7 %collective-permute-start = (bf16[2,1024,1,128]{3,1,2,0:T(8,128)(2,1)}, bf16[2,1024,1,128]{3,1,2,0:T(8,128)(2,1)S(1)}, u32[]{:S(2)}, u32[]{:S(2)}) collective-permute-start(bf16[2,1024,1,128]{3,1,2,0:T(8,128)(2,1)} %get-tuple-element.940), channel_id=1, source_target_pairs={{0,1},{1,2},{2,3},{3,4},{4,5},{5,6},{6,7},{7,0},{8,9},{9,10},{10,1... | collective-permute-start | bytes 1572872 | tf_op jit(solution)/shard_map/while/body/eval_jaxpr/ppermute | solution.py:67
  284.7 29.3 %collective-permute-start.1 = (bf16[2,1024,1,128]{3,1,2,0:T(8,128)(2,1)}, bf16[2,1024,1,128]{3,1,2,0:T(8,128)(2,1)S(1)}, u32[]{:S(2)}, u32[]{:S(2)}) collective-permute-start(bf16[2,1024,1,128]{3,1,2,0:T(8,128)(2,1)} %get-tuple-element.941), channel_id=1, source_target_pairs={{0,1},{1,2},{2,3},{3,4},{4,5},{5,6},{6,7},{7,0},{8,9},{9,10},{10,1... | collective-permute-start | bytes 1572872 | tf_op jit(solution)/shard_map/while/body/eval_jaxpr/ppermute | solution.py:67
  288.2 28.7 %collective-permute-start = (bf16[2,1024,1,128]{3,1,2,0:T(8,128)(2,1)}, bf16[2,1024,1,128]{3,1,2,0:T(8,128)(2,1)S(1)}, u32[]{:S(2)}, u32[]{:S(2)}) collective-permute-start(bf16[2,1024,1,128]{3,1,2,0:T(8,128)(2,1)} %get-tuple-element.940), channel_id=1, source_target_pairs={{0,1},{1,2},{2,3},{3,4},{4,5},{5,6},{6,7},{7,0},{8,9},{9,10},{10,1... | collective-permute-start | bytes 1572872 | tf_op jit(solution)/shard_map/while/body/eval_jaxpr/ppermute | solution.py:67
  317.7 4.1 copy-start.4
  317.7 4.1 copy-start.12
  325.4 2.3 copy-start.13
  329.4 30.8 %collective-permute-start.1 = (bf16[2,1024,1,128]{3,1,2,0:T(8,128)(2,1)}, bf16[2,1024,1,128]{3,1,2,0:T(8,128)(2,1)S(1)}, u32[]{:S(2)}, u32[]{:S(2)}) collective-permute-start(bf16[2,1024,1,128]{3,1,2,0:T(8,128)(2,1)} %get-tuple-element.941), channel_id=1, source_target_pairs={{0,1},{1,2},{2,3},{3,4},{4,5},{5,6},{6,7},{7,0},{8,9},{9,10},{10,1... | collective-permute-start | bytes 1572872 | tf_op jit(solution)/shard_map/while/body/eval_jaxpr/ppermute | solution.py:67
  331.9 29.1 %collective-permute-start = (bf16[2,1024,1,128]{3,1,2,0:T(8,128)(2,1)}, bf16[2,1024,1,128]{3,1,2,0:T(8,128)(2,1)S(1)}, u32[]{:S(2)}, u32[]{:S(2)}) collective-permute-start(bf16[2,1024,1,128]{3,1,2,0:T(8,128)(2,1)} %get-tuple-element.940), channel_id=1, source_target_pairs={{0,1},{1,2},{2,3},{3,4},{4,5},{5,6},{6,7},{7,0},{8,9},{9,10},{10,1... | collective-permute-start | bytes 1572872 | tf_op jit(solution)/shard_map/while/body/eval_jaxpr/ppermute | solution.py:67
  361.8 4.1 copy-start.4
  361.8 4.1 copy-start.12
  369.4 2.3 copy-start.13
  373.4 14.6 %collective-permute-start.1 = (bf16[2,1024,1,128]{3,1,2,0:T(8,128)(2,1)}, bf16[2,1024,1,128]{3,1,2,0:T(8,128)(2,1)S(1)}, u32[]{:S(2)}, u32[]{:S(2)}) collective-permute-start(bf16[2,1024,1,128]{3,1,2,0:T(8,128)(2,1)} %get-tuple-element.941), channel_id=1, source_target_pairs={{0,1},{1,2},{2,3},{3,4},{4,5},{5,6},{6,7},{7,0},{8,9},{9,10},{10,1... | collective-permute-start | bytes 1572872 | tf_op jit(solution)/shard_map/while/body/eval_jaxpr/ppermute | solution.py:67
  373.4 15.4 %collective-permute-start = (bf16[2,1024,1,128]{3,1,2,0:T(8,128)(2,1)}, bf16[2,1024,1,128]{3,1,2,0:T(8,128)(2,1)S(1)}, u32[]{:S(2)}, u32[]{:S(2)}) collective-permute-start(bf16[2,1024,1,128]{3,1,2,0:T(8,128)(2,1)} %get-tuple-element.940), channel_id=1, source_target_pairs={{0,1},{1,2},{2,3},{3,4},{4,5},{5,6},{6,7},{7,0},{8,9},{9,10},{10,1... | collective-permute-start | bytes 1572872 | tf_op jit(solution)/shard_map/while/body/eval_jaxpr/ppermute | solution.py:67
  389.7 4.1 copy-start.4
  389.7 4.1 copy-start.12
  397.3 2.3 copy-start.13
  401.3 14.6 %collective-permute-start.1 = (bf16[2,1024,1,128]{3,1,2,0:T(8,128)(2,1)}, bf16[2,1024,1,128]{3,1,2,0:T(8,128)(2,1)S(1)}, u32[]{:S(2)}, u32[]{:S(2)}) collective-permute-start(bf16[2,1024,1,128]{3,1,2,0:T(8,128)(2,1)} %get-tuple-element.941), channel_id=1, source_target_pairs={{0,1},{1,2},{2,3},{3,4},{4,5},{5,6},{6,7},{7,0},{8,9},{9,10},{10,1... | collective-permute-start | bytes 1572872 | tf_op jit(solution)/shard_map/while/body/eval_jaxpr/ppermute | solution.py:67
  402.6 14.7 %collective-permute-start = (bf16[2,1024,1,128]{3,1,2,0:T(8,128)(2,1)}, bf16[2,1024,1,128]{3,1,2,0:T(8,128)(2,1)S(1)}, u32[]{:S(2)}, u32[]{:S(2)}) collective-permute-start(bf16[2,1024,1,128]{3,1,2,0:T(8,128)(2,1)} %get-tuple-element.940), channel_id=1, source_target_pairs={{0,1},{1,2},{2,3},{3,4},{4,5},{5,6},{6,7},{7,0},{8,9},{9,10},{10,1... | collective-permute-start | bytes 1572872 | tf_op jit(solution)/shard_map/while/body/eval_jaxpr/ppermute | solution.py:67
  418.1 4.1 copy-start.4
  418.1 4.1 copy-start.12
  425.7 2.3 copy-start.13
Sparse Core Ops, SparseCore 0:
  9.5 124.9 all-gather.1
  447.6 231.2 reduce-scatter.1
where the time goes:
time: 691 us; the launch traced here: 689 us
  waiting for transfers between devices  422 us (61%)
  matrix products  93.3 us (14%)
  starting transfers between devices  63.9 us (9%)
  local copies, waits for them, and re-layouts  52.7 us (8%)
  other arithmetic  27.8 us (4%)
  loops' own time  15.5 us (2%)
  between operations  13.8 us (2%)
    reduce_scatter x1, waiting for transfers between devices, local_attn(): y_rows = lax.psum_scatter(part_sum, 'tp', scatter_dimension=0, tiled=True)  231 us
    all_gather x1, waiting for transfers between devices, local_attn(): x_block = lax.all_gather(x_part, 'tp', axis=0, tiled=True)  127 us
    ppermute x14, starting transfers between devices, ring_free_step(): k_blocks, v_blocks = lax.ppermute((k_blocks, v_blocks), 'sp', next_pairs)  63.9 us
    ppermute x14, waiting for transfers between devices, ring_free_step(): k_blocks, v_blocks = lax.ppermute((k_blocks, v_blocks), 'sp', next_pairs)  62.9 us
    dot_general x7, matrix products, block_update(): jnp.einsum('hgqk,khd->hgqd', prob_blk.astype(jnp.bfloat16), v_blk, prefer...  29.6 us
    dot_general x7, matrix products, block_update(): jnp.einsum('qhgd,khd->hgqk', q_blk, k_blk, preferred_element_type=jnp.flo...  22.6 us
    squeeze x7, local copies, waits for them, and re-layouts, absorb(): q_loc[q_half]  15.8 us
    reduce_sum x6, other arithmetic, block_update(): new_sum = row_sum * rescale + jnp.sum(prob_blk, axis=-1)  15.4 us
  transfers between devices with their start and end apart: 16, of which 14 were waited for; matrix products, arithmetic and copies ran while one was open for 3% of the time, Pallas kernels for 0%

commit v1 on v0

v1 whole, which is shorter than its diff:
```python
import functools

import jax
import jax.numpy as jnp
from jax import lax
from jax.experimental import pallas as pl
from jax.experimental.pallas import tpu as pltpu
from jax.sharding import PartitionSpec as P

WINDOW = 4096
NEG_BIG = -1e30
LOG2E = 1.4426950408889634
MESH = pl.DeviceIdType.MESH
NY = 4
TQ = 256
WIDE = 768
N_WIDE = (WINDOW - TQ) // WIDE


def dot_nt(lhs, rhs):
    return lax.dot_general(lhs, rhs, (((1,), (1,)), ((), ())), preferred_element_type=jnp.float32)


def attn_out_kernel(q_hbm, kv_hbm, wo_hbm, y_hbm, q_v, kv_v, wo_v, s_v, mx_v, mb_v, l_v, acc_v, o_st, og, yst, yv,
                    ld_sem, kv_sem, wo_sem, o_send, o_recv, y_send, y_recv, y_sem):
    sp = lax.axis_index("sp")
    tp = lax.axis_index("tp")
    my_z, my_y = tp // NY, tp % NY
    n_tp = NY * NY
    n_sp = 8
    chunk = kv_v.shape[0] // (2 * n_sp)
    head = kv_v.shape[1] // 2
    cols = yst.shape[2]
    coef = head ** -0.5 * LOG2E
    n_back = WINDOW // chunk

    q_copy = pltpu.make_async_copy(q_hbm, q_v, ld_sem)
    q_copy.start()

    def kv_copy(blk):
        src = kv_hbm.at[blk, 0] if blk < n_sp else kv_hbm.at[2 * n_sp - 1 - blk, 1]
        return pltpu.make_async_copy(src, kv_v.at[pl.ds(blk * chunk, chunk)], kv_sem.at[blk])

    def kv_needed(blk):
        low = (blk <= sp) & (blk >= sp - n_back)
        high = (blk <= 2 * n_sp - 1 - sp) & (blk >= 2 * n_sp - 1 - sp - n_back)
        return low | high

    for blk in range(2 * n_sp):
        @pl.when(kv_needed(blk))
        def _(blk=blk):
            kv_copy(blk).start()

    def wo_copy(idx):
        z_src, y_src = idx // NY, idx % NY
        return pltpu.make_async_copy(wo_hbm.at[:, y_src, (my_z - z_src + NY) % NY], wo_v.at[idx], wo_sem.at[idx])

    for idx in range(n_tp):
        wo_copy(idx).start()

    barrier = pltpu.get_barrier_semaphore()
    for step in range(1, n_tp):
        pl.semaphore_signal(barrier, inc=1, device_id={"tp": (tp + step) % n_tp}, device_id_type=MESH)
    pl.semaphore_wait(barrier, n_tp - 1)

    q_copy.wait()
    for blk in range(2 * n_sp):
        @pl.when(kv_needed(blk))
        def _(blk=blk):
            kv_copy(blk).wait()

    row_i = lax.broadcasted_iota(jnp.int32, (2 * TQ, TQ), 0) % TQ
    col_i = lax.broadcasted_iota(jnp.int32, (2 * TQ, TQ), 1)

    def lane_max(scores):
        best = scores[:, 0:head]
        for idx in range(1, scores.shape[1] // head):
            best = jnp.maximum(best, scores[:, idx * head:(idx + 1) * head])
        return best

    def o_copy(tile, z_dst):
        y_dst, z_row = tile % NY, tile // NY
        rows = chunk // (2 * NY)
        src = o_st.at[pl.ds(pl.multiple_of(tile * rows, rows), rows)]
        dst = og.at[z_row, :, pl.ds(pl.multiple_of(tp * 2 * head, 2 * head), 2 * head)]
        return pltpu.make_async_remote_copy(src_ref=src, dst_ref=dst, send_sem=o_send.at[tile, z_dst], recv_sem=o_recv.at[z_row, tp],
                                            device_id={"tp": NY * z_dst + y_dst}, device_id_type=MESH)

    def attend(q_idx, gidx, wide, start_tile, n_steps, with_first):
        q_blk = q_v[pl.ds(pl.multiple_of(q_idx * TQ, TQ), TQ), :]
        q_two = jnp.concatenate([q_blk[:, :head], q_blk[:, head:]], axis=0)

        def keys(tile, width):
            return kv_v[pl.ds(pl.multiple_of(tile * TQ, TQ), width), 0:head]

        def values(tile, width):
            return kv_v[pl.ds(pl.multiple_of(tile * TQ, TQ), width), head:2 * head]

        per = wide // TQ
        scores = jnp.where(col_i <= row_i, dot_nt(q_two, keys(gidx, TQ)), NEG_BIG)
        s_v[:, 0:TQ] = scores
        best = lane_max(scores)
        if with_first:
            scores = jnp.where(col_i > row_i, dot_nt(q_two, keys(gidx - WINDOW // TQ, TQ)), NEG_BIG)
            s_v[:, TQ:2 * TQ] = scores
            best = jnp.maximum(best, lane_max(scores))
        mx_v[...] = best

        def score_step(idx, carry):
            part = dot_nt(q_two, keys(start_tile + per * idx, wide))
            s_v[:, pl.ds(pl.multiple_of(2 * TQ + idx * wide, TQ), wide)] = part
            mx_v[...] = jnp.maximum(mx_v[...], lane_max(part))
            return carry

        lax.fori_loop(0, n_steps, score_step, 0)
        row_best = jnp.max(mx_v[...], axis=1, keepdims=True) * coef
        mb_v[...] = jnp.broadcast_to(row_best, mb_v.shape)

        def probs(col, width):
            base = mb_v[...]
            total = None
            parts = []
            for idx in range(width // head):
                part = jnp.exp2(s_v[:, pl.ds(pl.multiple_of(col + idx * head, head), head)] * coef - base)
                total = part if total is None else total + part
                parts.append(part.astype(jnp.bfloat16))
            return jnp.concatenate(parts, axis=1), total

        prob, total = probs(0, TQ)
        acc = jnp.dot(prob, values(gidx, TQ), preferred_element_type=jnp.float32)
        if with_first:
            prob, total_b = probs(TQ, TQ)
            total = total + total_b
            acc = acc + jnp.dot(prob, values(gidx - WINDOW // TQ, TQ), preferred_element_type=jnp.float32)
        l_v[...] = total
        acc_v[...] = acc

        def value_step(idx, carry):
            prob, total = probs(2 * TQ + idx * wide, wide)
            l_v[...] += total
            acc_v[...] += jnp.dot(prob, values(start_tile + per * idx, wide), preferred_element_type=jnp.float32)
            return carry

        lax.fori_loop(0, n_steps, value_step, 0)
        denom = jnp.sum(l_v[...], axis=1, keepdims=True)
        out = (acc_v[...] / denom).astype(jnp.bfloat16)
        out = jnp.concatenate([out[:TQ], out[TQ:]], axis=1)
        o_st[pl.ds(pl.multiple_of(q_idx * TQ, TQ), TQ), :] = out

    def q_step(q_idx, carry):
        tiles = chunk // TQ
        blk = jnp.where(q_idx < tiles, sp, 2 * n_sp - 1 - sp)
        gidx = blk * tiles + q_idx % tiles

        @pl.when(gidx >= WINDOW // TQ)
        def _():
            attend(q_idx, gidx, WIDE, gidx - WINDOW // TQ + 1, N_WIDE, True)

        @pl.when(gidx < WINDOW // TQ)
        def _():
            attend(q_idx, gidx, TQ, 0, gidx, False)

        for sub in range(2):
            tile = 2 * q_idx + sub
            for z_dst in range(NY):
                mine = (tile % NY == my_y) & (my_z == z_dst)

                @pl.when(jnp.logical_not(mine))
                def _(tile=tile, z_dst=z_dst):
                    o_copy(tile, z_dst).start()

            @pl.when(tile % NY == my_y)
            def _(tile=tile):
                rows = chunk // (2 * NY)
                og[tile // NY, :, pl.ds(pl.multiple_of(tp * 2 * head, 2 * head), 2 * head)] = \
                    o_st[pl.ds(pl.multiple_of(tile * rows, rows), rows), :]
        return carry

    lax.fori_loop(0, 2 * chunk // TQ, q_step, 0)

    rows = yst.shape[1]

    def o_arrival(z_row, src):
        dst = og.at[z_row, :, pl.ds(src * 2 * head, 2 * head)]
        return pltpu.make_async_remote_copy(src_ref=o_st.at[pl.ds(0, rows)], dst_ref=dst, send_sem=o_send.at[0, 0],
                                            recv_sem=o_recv.at[z_row, src], device_id={"tp": 0}, device_id_type=MESH)

    def y_copy(z_dst, z_src):
        return pltpu.make_async_remote_copy(
            src_ref=yst.at[z_dst], dst_ref=yv.at[:, pl.ds(pl.multiple_of(z_src * cols, 128), cols)],
            send_sem=y_send.at[z_dst], recv_sem=y_recv.at[z_src], device_id={"tp": NY * z_dst + my_y}, device_id_type=MESH)

    for idx in range(n_tp):
        wo_copy(idx).wait()
    for half in range(2):
        for z_row in (2 * half, 2 * half + 1):
            for src in range(n_tp):
                @pl.when(tp != src)
                def _(z_row=z_row, src=src):
                    o_arrival(z_row, src).wait_recv()
        lhs = og[2 * half:2 * half + 2].reshape(2 * rows, n_tp * 2 * head)
        for col in range(0, cols, 384):
            w_cols = wo_v[:, :, :, col:col + 384].reshape(n_tp * 2 * head, 384)
            res = jnp.dot(lhs, w_cols, preferred_element_type=jnp.float32).astype(jnp.bfloat16)
            yst[2 * half:2 * half + 2, :, col:col + 384] = res.reshape(2, rows, 384)
        for z_dst in (2 * half, 2 * half + 1):
            @pl.when(my_z != z_dst)
            def _(z_dst=z_dst):
                y_copy(z_dst, my_z).start()

            @pl.when(my_z == z_dst)
            def _(z_dst=z_dst):
                yv[:, pl.ds(pl.multiple_of(my_z * cols, 128), cols)] = yst[z_dst]

    for z_src in range(NY):
        @pl.when(my_z != z_src)
        def _(z_src=z_src):
            y_copy(z_src, z_src).wait_recv()
    y_out = pltpu.make_async_copy(yv, y_hbm, y_sem)
    y_out.start()
    for tile in range(2 * n_tp // 2):
        for z_dst in range(NY):
            mine = (tile % NY == my_y) & (my_z == z_dst)

            @pl.when(jnp.logical_not(mine))
            def _(tile=tile, z_dst=z_dst):
                o_copy(tile, z_dst).wait_send()
    for z_dst in range(NY):
        @pl.when(my_z != z_dst)
        def _(z_dst=z_dst):
            y_copy(z_dst, my_z).wait_send()
    y_out.wait()


def attn_out(q_loc, kv_all, wo_rel):
    n_e, _, _, w_rows, cols = wo_rel.shape
    rows, two_head = q_loc.shape
    n_tp = NY * NY
    any_spec = pl.BlockSpec(memory_space=pl.ANY)
    n_keys = kv_all.shape[0] * rows
    dma = pltpu.SemaphoreType.DMA
    return pl.pallas_call(
        attn_out_kernel,
        out_shape=jax.ShapeDtypeStruct((rows // n_tp, NY * cols), jnp.bfloat16),
        in_specs=[any_spec] * 3,
        out_specs=any_spec,
        scratch_shapes=[
            pltpu.VMEM((rows, two_head), jnp.bfloat16),
            pltpu.VMEM((n_keys, two_head), jnp.bfloat16),
            pltpu.VMEM((n_tp, n_e, w_rows, cols), jnp.bfloat16),
            pltpu.VMEM((2 * TQ, WINDOW + TQ), jnp.float32),
            pltpu.VMEM((2 * TQ, two_head // 2), jnp.float32),
            pltpu.VMEM((2 * TQ, two_head // 2), jnp.float32),
            pltpu.VMEM((2 * TQ, two_head // 2), jnp.float32),
            pltpu.VMEM((2 * TQ, two_head // 2), jnp.float32),
            pltpu.VMEM((rows, two_head), jnp.bfloat16),
            pltpu.VMEM((NY, rows // n_tp, n_tp * two_head), jnp.bfloat16),
            pltpu.VMEM((NY, rows // n_tp, cols), jnp.bfloat16),
            pltpu.VMEM((rows // n_tp, NY * cols), jnp.bfloat16),
            dma, dma((16,)), dma((n_tp,)), dma((n_tp, NY)), dma((NY, n_tp)), dma((NY,)), dma((NY,)), dma,
        ],
        compiler_params=pltpu.CompilerParams(collective_id=1, has_side_effects=True, vmem_limit_bytes=62 * 1024 * 1024),
        cost_estimate=pl.CostEstimate(flops=20_000_000_000, bytes_accessed=30_000_000, transcendentals=16_000_000),
        name="attn_out",
    )(q_loc, kv_all, wo_rel)


def gather_w_out(w_out):
    heads_loc, head_dim, d_model = w_out.shape
    sp_rank, tp_rank = lax.axis_index("sp"), lax.axis_index("tp")
    n_sp = lax.axis_size("sp")
    rows = heads_loc * head_dim // n_sp
    flat = w_out.reshape(heads_loc * head_dim, d_model)
    mine = lax.dynamic_slice_in_dim(flat, sp_rank * rows, rows, 0)
    my_z = tp_rank // NY
    pieces = []
    for k in range(NY):
        piece = lax.dynamic_slice_in_dim(mine, ((my_z + k) % NY) * (d_model // NY), d_model // NY, 1)
        if k:
            piece = lax.ppermute(piece, "tp", [(t, ((t // NY + k) % NY) * NY + t % NY) for t in range(NY * NY)])
        pieces.append(piece)
    part = jnp.stack(pieces)
    part = lax.all_gather(part, "tp", axis=0, axis_index_groups=[[NY * z + y for y in range(NY)] for z in range(NY)])
    return lax.all_gather(part, "sp", axis=0)


def solution(mesh):
    def local_attn(x_part, w_query, w_key, w_value, w_out):
        d_model = x_part.shape[1]
        wo_rel = gather_w_out(w_out)
        x_block = lax.all_gather(x_part, "tp", axis=0, tiled=True)
        rows = x_block.shape[0]

        def project(weight):
            return jnp.dot(x_block, weight.reshape(d_model, -1), preferred_element_type=jnp.float32).astype(jnp.bfloat16)

        q_loc = project(w_query)
        kv_loc = jnp.concatenate([project(w_key), project(w_value)], axis=1)
        kv_all = lax.all_gather(kv_loc.reshape(2, rows // 2, -1), "sp", axis=0)
        return attn_out(q_loc, kv_all, wo_rel)

    return jax.shard_map(local_attn, mesh=mesh, in_specs=(P(("dp", "sp", "tp"), None), P(None, "tp", None), P(None, "tp", None), P(None, "tp", None), P("tp", None, None)), out_specs=P(("dp", "sp", "tp"), None), check_vma=False)
```

time: 691 us -> 369 us (0.53)
  the two profiles are of different devices: /device:TPU:1 before, /device:TPU:85 now
where the time goes in v1:
time: 369 us
  waiting for transfers between devices  224 us (61%)
  Pallas kernels  86.6 us (23%)
  matrix products  36.1 us (10%)
  between operations  13.2 us (4%)
  local copies, waits for them, and re-layouts  5.19 us (1%)
    all_gather x1, waiting for transfers between devices, local_attn(): x_block = lax.all_gather(x_part, 'tp', axis=0, tiled=True)  125 us
    pallas_call x1, Pallas kernels, attn_out(): pl.pallas_call(attn_out_kernel, out_shape=jax.ShapeDtypeStruct((rows // n...  86.6 us
    all_gather x1, waiting for transfers between devices, local_attn(): kv_all = lax.all_gather(kv_loc.reshape(2, rows // 2, -1), 'sp', axis=0)  51.3 us
    dot_general x3, matrix products, project(): jnp.dot(x_block, weight.reshape(d_model, -1), preferred_element_type=jnp....  36.1 us
    all_gather x1, waiting for transfers between devices, gather_w_out(): lax.all_gather(part, 'tp', axis=0, axis_index_groups=[[NY * z + y for y i...  23.5 us
    all_gather x1, waiting for transfers between devices, gather_w_out(): return lax.all_gather(part, 'sp', axis=0)  18.8 us
  transfers between devices with their start and end apart: 7, of which 7 were waited for; matrix products, arithmetic and copies ran while one was open for 10% of the time, Pallas kernels for 0%

profile of v1, /device:TPU:85, one launch (start us, length us, event | category | flops | bytes accessed | tf_op | source)
XLA Modules:
  0.0 368.9 jit_solution(7679445948730026693)
XLA Ops:
  6.5 0.0 copy-start
  6.5 0.0 all-gather.11.cloned.1.call-start
  6.5 1.3 dynamic-slice_bitcast_fusion
  7.9 0.1 collective-permute-start.2
  7.9 3.1 collective-permute-start.1
  11.1 0.0 collective-permute-start
  11.1 0.1 collective-permute-done.2
  11.1 1.7 collective-permute-done.1
  12.8 2.2 collective-permute-done
  14.9 0.8 pad_maximum_fusion.1
  15.7 0.0 all-gather.11.cloned.1.call-update
  15.7 0.0 all-gather.7.cloned.1.call-start
  15.8 0.7 all-gather.7.cloned.1.call-update
  16.5 0.0 all-gather.13.cloned.1.call-start
  16.5 23.5 %all-gather.11.cloned.1.call-done = bf16[16,32,1152]{2,1,0:T(8,128)(2,1)} async-done(((bf16[4,32,1152]{2,1,0:T(8,128)(2,1)}), bf16[16,32,1152]{2,1,0:T(8,128)(2,1)}) %all-gather.11.cloned.1.call-update) | async-done | bytes 1179664 | tf_op jit(solution)/shard_map/all_gather | solution.py:283
  40.0 0.0 all-gather.13.cloned.1.call-update
  40.0 0.0 all-gather.9.cloned.1.call-start
  40.1 125.3 %all-gather.7.cloned.1.call-done = bf16[2048,4608]{1,0:T(8,128)(2,1)} async-done(((bf16[128,4608]{1,0:T(8,128)(2,1)}), bf16[2048,4608]{1,0:T(8,128)(2,1)}) %all-gather.7.cloned.1.call-update) | async-done | bytes 18874384 | tf_op jit(solution)/shard_map/all_gather | solution.py:291
  165.4 0.0 copy-done
  165.4 12.7 %convolution_convert_fusion.1 = bf16[2048,128]{0,1:T(8,128)(2,1)S(1)} fusion(bf16[2048,4608]{1,0:T(8,128)(2,1)} %all-gather.7.cloned.1.call-done, bf16[4608,1,128]{2,0,1:T(8,128)(2,1)S(1)} %copy-done), kind=kOutput, calls=%fused_computation.1 | convolution fusion | flops 2416181248 | bytes 20578304 | tf_op jit(solution)/shard_map/dot_general | solution.py:295
  178.1 13.0 %convolution_convert_fusion.2 = bf16[2048,128]{0,1:T(8,128)(2,1)S(1)} fusion(bf16[2048,4608]{1,0:T(8,128)(2,1)} %all-gather.7.cloned.1.call-done, bf16[4608,1,128]{2,0,1:T(8,128)(2,1)} %param.7), kind=kOutput, calls=%fused_computation.2 | convolution fusion | flops 2416181248 | bytes 20578304 | tf_op jit(solution)/shard_map/dot_general | solution.py:295
  191.1 0.1 pad_maximum_fusion
  191.2 1.5 copy.8
  192.7 0.0 all-gather.9.cloned.1.call-update
  192.8 10.4 %convolution_convert_fusion.q_hbm = bf16[2048,256]{1,0:T(8,128)(2,1)} fusion(bf16[2048,4608]{1,0:T(8,128)(2,1)} %all-gather.7.cloned.1.call-done, bf16[576,8,2,128]{3,2,1,0:T(2,128)(2,1)} %bitcast.29), kind=kOutput, calls=%fused_computation | convolution fusion | flops 4832362496 | bytes 22282240 | tf_op jit(solution)/shard_map/dot_general | solution.py:295
  203.2 18.8 %all-gather.13.cloned.1.call-done = bf16[32,4,32,1152]{3,2,1,0:T(8,128)(2,1)} async-done(((bf16[4,4,32,1152]{3,2,1,0:T(8,128)(2,1)}), bf16[32,4,32,1152]{3,2,1,0:T(8,128)(2,1)}) %all-gather.13.cloned.1.call-update) | async-done | bytes 9437200 | tf_op jit(solution)/shard_map/all_gather | solution.py:284
  222.0 51.3 %all-gather.9.cloned.1.call-done.kv_hbm = bf16[8,2,1024,256]{3,2,1,0:T(8,128)(2,1)} async-done(((bf16[1,2,1024,256]{3,2,1,0:T(8,128)(2,1)}), bf16[8,2,1024,256]{3,2,1,0:T(8,128)(2,1)}) %all-gather.9.cloned.1.call-update) | async-done | bytes 8388624 | tf_op jit(solution)/shard_map/all_gather | solution.py:299
  273.4 86.6 %attn_out.1 = bf16[128,4608]{1,0:T(8,128)(2,1)} custom-call(bf16[2048,256]{1,0:T(8,128)(2,1)} %convolution_convert_fusion.q_hbm, bf16[8,2,1024,256]{3,2,1,0:T(8,128)(2,1)} %all-gather.9.cloned.1.call-done.kv_hbm, bf16[8,4,4,32,1152]{4,3,2,1,0:T(8,128)(2,1)} %bitcast.28), custom_call_target="tpu_custom_call" | custom-call | flops 20000000000 | bytes 30000000 | tf_op jit(solution)/shard_map/attn_out/pallas_call | solution.py:242
  360.0 2.4 copy.15
Async XLA Ops:
  6.5 158.9 %copy-start = (bf16[4608,1,128]{2,0,1:T(8,128)(2,1)S(1)}, bf16[4608,1,128]{2,0,1:T(8,128)(2,1)}, u32[]{:S(2)}) copy-start(bf16[4608,1,128]{2,0,1:T(8,128)(2,1)} %param.8) | copy-start | bytes 3538948
  6.5 33.5 %all-gather.11.cloned.1.call-start = ((), (), s32[]{:S(2)}) async-start(), calls=%async_computation.2 | async-start | bytes 1474560 | tf_op jit(solution)/shard_map/all_gather | solution.py:283
  7.9 3.3 collective-permute-start.2
  7.9 4.9 %collective-permute-start.1 = (bf16[32,1152]{1,0:T(8,128)(2,1)S(1)}, bf16[32,1152]{1,0:T(8,128)(2,1)S(1)}, u32[]{:S(2)}, u32[]{:S(2)}) collective-permute-start(bf16[32,1152]{1,0:T(8,128)(2,1)S(1)} %get-tuple-element.7), channel_id=1, source_target_pairs={{0,64},{8,72},{16,80},{24,88},{32,96},{40,104},{48,112},{56,120},{... | collective-permute-start | bytes 221192 | tf_op jit(solution)/shard_map/ppermute | solution.py:280
  11.1 3.9 %collective-permute-start = (bf16[32,1152]{1,0:T(8,128)(2,1)S(1)}, bf16[32,1152]{1,0:T(8,128)(2,1)S(1)}, u32[]{:S(2)}, u32[]{:S(2)}) collective-permute-start(bf16[32,1152]{1,0:T(8,128)(2,1)S(1)} %get-tuple-element.8), channel_id=1, source_target_pairs={{0,32},{8,40},{16,48},{24,56},{32,64},{40,72},{48,80},{56,88},{64,... | collective-permute-start | bytes 221192 | tf_op jit(solution)/shard_map/ppermute | solution.py:280
  15.7 149.7 %all-gather.7.cloned.1.call-start = ((), (), s32[]{:S(2)}) async-start(), calls=%async_computation | async-start | bytes 20054016 | tf_op jit(solution)/shard_map/all_gather | solution.py:291
  16.5 205.6 %all-gather.13.cloned.1.call-start = ((), (), s32[]{:S(2)}) async-start(), calls=%async_computation.3 | async-start | bytes 10616832 | tf_op jit(solution)/shard_map/all_gather | solution.py:284
  40.0 233.3 %all-gather.9.cloned.1.call-start = ((), (), s32[]{:S(2)}) async-start(), calls=%async_computation.1 | async-start | bytes 9437184 | tf_op jit(solution)/shard_map/all_gather | solution.py:299
Sparse Core Ops, SparseCore 0:
  15.8 24.1 all-gather.10
  42.1 123.2 all-gather.6
  167.1 54.8 all-gather.12
  223.6 49.7 all-gather.8

commit v2 on v1

--- a/solution.py
+++ b/solution.py
@@ -21,53 +21,210 @@
     return lax.dot_general(lhs, rhs, (((1,), (1,)), ((), ())), preferred_element_type=jnp.float32)
 
 
-def attn_out_kernel(q_hbm, kv_hbm, wo_hbm, y_hbm, q_v, kv_v, wo_v, s_v, mx_v, mb_v, l_v, acc_v, o_st, og, yst, yv,
-                    ld_sem, kv_sem, wo_sem, o_send, o_recv, y_send, y_recv, y_sem):
+def layer_kernel(x_hbm, wq_hbm, wk_hbm, wv_hbm, wo_hbm, y_hbm, xg, w_v, q_v, kv_v, wo_v, s_v, mx_v, mb_v, l_v, acc_v, o_st, og, yst, yv,
+                 x_sem, w_sem, x_send, x_recv, kv_send, kv_recv, wo_sem, wo_send, wo_recv, sl_send, sl_recv, o_send, o_recv, y_send, y_recv, y_sem):
     sp = lax.axis_index("sp")
     tp = lax.axis_index("tp")
     my_z, my_y = tp // NY, tp % NY
+    my_x, my_c = sp // 2, sp % 2
     n_tp = NY * NY
     n_sp = 8
     chunk = kv_v.shape[0] // (2 * n_sp)
     head = kv_v.shape[1] // 2
     cols = yst.shape[2]
+    rows = yst.shape[1]
     coef = head ** -0.5 * LOG2E
     n_back = WINDOW // chunk
-
-    q_copy = pltpu.make_async_copy(q_hbm, q_v, ld_sem)
-    q_copy.start()
-
-    def kv_copy(blk):
-        src = kv_hbm.at[blk, 0] if blk < n_sp else kv_hbm.at[2 * n_sp - 1 - blk, 1]
-        return pltpu.make_async_copy(src, kv_v.at[pl.ds(blk * chunk, chunk)], kv_sem.at[blk])
-
-    def kv_needed(blk):
-        low = (blk <= sp) & (blk >= sp - n_back)
-        high = (blk <= 2 * n_sp - 1 - sp) & (blk >= 2 * n_sp - 1 - sp - n_back)
-        return low | high
-
-    for blk in range(2 * n_sp):
-        @pl.when(kv_needed(blk))
-        def _(blk=blk):
-            kv_copy(blk).start()
-
-    def wo_copy(idx):
-        z_src, y_src = idx // NY, idx % NY
-        return pltpu.make_async_copy(wo_hbm.at[:, y_src, (my_z - z_src + NY) % NY], wo_v.at[idx], wo_sem.at[idx])
-
-    for idx in range(n_tp):
-        wo_copy(idx).start()
+    part = rows // 4
+
+    x_load = pltpu.make_async_copy(x_hbm, xg.at[tp], x_sem)
+    x_load.start()
+    w_loads = (pltpu.make_async_copy(wq_hbm, w_v.at[:, 0:2 * head], w_sem.at[0]),
+               pltpu.make_async_copy(wk_hbm, w_v.at[:, 2 * head:3 * head], w_sem.at[1]),
+               pltpu.make_async_copy(wv_hbm, w_v.at[:, 3 * head:4 * head], w_sem.at[2]))
+    for load in w_loads:
+        load.start()
 
     barrier = pltpu.get_barrier_semaphore()
     for step in range(1, n_tp):
         pl.semaphore_signal(barrier, inc=1, device_id={"tp": (tp + step) % n_tp}, device_id_type=MESH)
-    pl.semaphore_wait(barrier, n_tp - 1)
-
-    q_copy.wait()
-    for blk in range(2 * n_sp):
-        @pl.when(kv_needed(blk))
-        def _(blk=blk):
-            kv_copy(blk).wait()
+    for step in range(1, n_sp):
+        pl.semaphore_signal(barrier, inc=1, device_id={"sp": (sp + step) % n_sp}, device_id_type=MESH)
+    pl.semaphore_wait(barrier, n_tp + n_sp - 2)
+
+    zm, zp, zo = (my_z + 3) % NY, (my_z + 1) % NY, (my_z + 2) % NY
+    ym, yp, yo = (my_y + 3) % NY, (my_y + 1) % NY, (my_y + 2) % NY
+    sends = []
+
+    def x_copy(src_tp, first, count, dst_tp, slot):
+        ref = xg.at[src_tp, pl.ds(first * part, count * part)]
+        return pltpu.make_async_remote_copy(src_ref=ref, dst_ref=ref, send_sem=x_send.at[slot], recv_sem=x_recv.at[src_tp, first],
+                                            device_id={"tp": dst_tp}, device_id_type=MESH)
+
+    def x_put(z_src, y_src, first, count, z_dst, y_dst):
+        copy = x_copy(NY * z_src + y_src, first, count, NY * z_dst + y_dst, len(sends))
+        sends.append(copy)
+        copy.start()
+
+    def x_wait(z_src, y_src, first, count):
+        x_copy(NY * z_src + y_src, first, count, 0, 0).wait_recv()
+
+    def kv_copy(src_blk, first, count, half, back, dst_sp):
+        ref = kv_v.at[pl.ds(pl.multiple_of(src_blk * chunk + first, rows), count)]
+        return pltpu.make_async_remote_copy(src_ref=ref, dst_ref=ref, send_sem=kv_send.at[half, back - 1], recv_sem=kv_recv.at[src_blk],
+                                            device_id={"sp": dst_sp}, device_id_type=MESH)
+
+    def kv_target(blk, back):
+        tgt = blk + back
+        low = tgt < n_sp
+        dst = jnp.where(low, tgt, 2 * n_sp - 1 - tgt)
+        return dst, (tgt < 2 * n_sp) & (low | (blk >= n_sp) | (dst < sp))
+
+    def project(tiles):
+        def body(idx, carry):
+            tile = tiles[0]
+            for other in range(1, len(tiles)):
+                tile = jnp.where(idx == other, tiles[other], tile)
+            prod = jnp.dot(xg[tile], w_v[...], preferred_element_type=jnp.float32).astype(jnp.bfloat16)
+            half = tile // (n_tp // 2)
+            blk = jnp.where(half == 0, sp, 2 * n_sp - 1 - sp)
+            first = (tile % (n_tp // 2)) * rows
+            q_v[pl.ds(pl.multiple_of(tile * rows, rows), rows), :] = prod[:, :2 * head]
+            kv_v[pl.ds(pl.multiple_of(blk * chunk + first, rows), rows), :] = prod[:, 2 * head:]
+            for back in range(1, n_back + 1):
+                dst, wanted = kv_target(blk, back)
+
+                @pl.when(wanted)
+                def _(back=back, dst=dst):
+                    kv_copy(blk, first, rows, half, back, dst).start()
+            return carry
+
+        lax.fori_loop(0, len(tiles), body, 0)
+
+    def tile_of(z_idx, y_idx):
+        return NY * z_idx + y_idx
+
+    x_load.wait()
+    for z_dst, y_dst, first in ((zp, my_y, 0), (zm, my_y, 0), (my_z, yp, 2), (my_z, ym, 2), (my_z, yp, 0), (my_z, ym, 0), (zp, my_y, 2), (zm, my_y, 2)):
+        x_put(my_z, my_y, first, 2, z_dst, y_dst)
+    for load in w_loads:
+        load.wait()
+    project([tp])
+
+    def take_items(z_item, y_item):
+        for y_src, first, y_dst in ((ym, 0, yp), (yp, 1, ym)):
+            x_wait(z_item, y_src, 0, 2)
+            x_put(z_item, y_src, first, 1, my_z, y_dst)
+        for z_src, first, z_dst in ((zm, 2, zp), (zp, 3, zm)):
+            x_wait(z_src, y_item, 2, 2)
+            x_put(z_src, y_item, first, 1, z_dst, my_y)
+
+    def send_items(z_item, y_item):
+        for y_dst in (yp, ym):
+            x_put(z_item, my_y, 0, 2, my_z, y_dst)
+        for z_dst in (zp, zm):
+            x_put(my_z, y_item, 2, 2, z_dst, my_y)
+
+    def take_far(z_item, y_item):
+        for first in range(2):
+            x_wait(z_item, yo, first, 1)
+            x_wait(zo, y_item, 2 + first, 1)
+
+    for z_src, first, z_dst in ((zm, 0, zp), (zp, 1, zm)):
+        x_wait(z_src, my_y, 0, 2)
+        x_put(z_src, my_y, first, 1, z_dst, my_y)
+    for y_src, first, y_dst in ((ym, 2, yp), (yp, 3, ym)):
+        x_wait(my_z, y_src, 2, 2)
+        x_put(my_z, y_src, first, 1, my_z, y_dst)
+    send_items(zm, ym)
+    send_items(zp, yp)
+    take_items(my_z, my_y)
+    project([tile_of(zm, my_y), tile_of(zp, my_y), tile_of(my_z, ym), tile_of(my_z, yp)])
+    for first in range(2):
+        x_wait(zo, my_y, first, 1)
+        x_wait(my_z, yo, 2 + first, 1)
+    send_items(zo, yo)
+    take_items(zm, ym)
+    project([tile_of(zm, ym)])
+    take_items(zp, yp)
+    project([tile_of(zm, yp), tile_of(zp, ym), tile_of(zp, yp)])
+    take_far(my_z, my_y)
+    project([tile_of(my_z, yo), tile_of(zo, my_y)])
+    take_items(zo, yo)
+
+    def wo_copy(step):
+        dst = (tp + step) % n_tp
+        src_ref = wo_hbm.at[sp, :, pl.ds(pl.multiple_of((dst // NY) * cols, 128), cols)]
+        return pltpu.make_async_remote_copy(src_ref=src_ref, dst_ref=wo_v.at[tp, sp], send_sem=wo_send.at[step], recv_sem=wo_recv.at[tp],
+                                            device_id={"tp": dst}, device_id_type=MESH)
+
+    wo_own = pltpu.make_async_copy(wo_hbm.at[sp, :, pl.ds(pl.multiple_of(my_z * cols, 128), cols)], wo_v.at[tp, sp], wo_sem)
+    wo_own.start()
+    for step in range(1, n_tp):
+        wo_copy(step).start()
+
+    take_far(zm, ym)
+    project([tile_of(zm, yo), tile_of(zo, ym)])
+    take_far(zp, yp)
+    project([tile_of(zp, yo), tile_of(zo, yp)])
+    take_far(zo, yo)
+    project([tile_of(zo, yo)])
+
+    x_left, x_right, x_far = (my_x + 3) % NY, (my_x + 1) % NY, (my_x + 2) % NY
+    slabs = []
+
+    def slab_copy(x_src, c_src, first, count, x_dst, c_dst, slot):
+        ref = wo_v.at[pl.ds(first * (n_tp // 2), count * (n_tp // 2)), 2 * x_src + c_src]
+        return pltpu.make_async_remote_copy(src_ref=ref, dst_ref=ref, send_sem=sl_send.at[slot], recv_sem=sl_recv.at[2 * x_src + c_src, first],
+                                            device_id={"sp": 2 * x_dst + c_dst}, device_id_type=MESH)
+
+    def slab_put(x_src, first, count, x_dst, c_dst):
+        copy = slab_copy(x_src, my_c, first, count, x_dst, c_dst, len(slabs))
+        slabs.append(copy)
+        copy.start()
+
+    def slab_wait(x_src, c_src, first, count):
+        slab_copy(x_src, c_src, first, count, 0, 0, 0).wait_recv()
+
+    def wo_first():
+        wo_own.wait()
+        for step in range(1, n_tp):
+            src = (tp + step) % n_tp
+            pltpu.make_async_remote_copy(src_ref=wo_v.at[src, sp], dst_ref=wo_v.at[src, sp], send_sem=wo_send.at[step], recv_sem=wo_recv.at[src],
+                                         device_id={"tp": src}, device_id_type=MESH).wait_recv()
+        for x_dst in (x_right, x_left):
+            slab_put(my_x, 0, 2, x_dst, my_c)
+        slab_put(my_x, 0, 2, my_x, 1 - my_c)
+
+    def wo_second():
+        for x_src, first, x_dst in ((x_left, 0, x_right), (x_right, 1, x_left)):
+            slab_wait(x_src, my_c, 0, 2)
+            slab_put(x_src, first, 1, x_dst, my_c)
+        for x_src in (x_left, x_right):
+            slab_put(x_src, 0, 2, my_x, 1 - my_c)
+
+    def wo_third():
+        for first in range(2):
+            slab_wait(x_far, my_c, first, 1)
+            slab_put(x_far, first, 1, my_x, 1 - my_c)
+
+    def wo_last():
+        for x_src in (my_x, x_left, x_right):
+            slab_wait(x_src, 1 - my_c, 0, 2)
+        for first in range(2):
+            slab_wait(x_far, 1 - my_c, first, 1)
+
+    def low_needs(blk):
+        return (blk < sp) & (blk >= sp - n_back)
+
+    def high_needs(blk):
+        return (blk < 2 * n_sp - 1 - sp) & (blk >= 2 * n_sp - 1 - sp - n_back) & (blk != sp) & jnp.logical_not(low_needs(blk))
+
+    def kv_wait(needs):
+        for blk in range(2 * n_sp - 1):
+            @pl.when(needs(blk))
+            def _(blk=blk):
+                kv_copy(blk, 0, chunk, 0, 1, 0).wait_recv()
 
     row_i = lax.broadcasted_iota(jnp.int32, (2 * TQ, TQ), 0) % TQ
     col_i = lax.broadcasted_iota(jnp.int32, (2 * TQ, TQ), 1)
@@ -80,7 +237,6 @@
 
     def o_copy(tile, z_dst):
         y_dst, z_row = tile % NY, tile // NY
-        rows = chunk // (2 * NY)
         src = o_st.at[pl.ds(pl.multiple_of(tile * rows, rows), rows)]
         dst = og.at[z_row, :, pl.ds(pl.multiple_of(tp * 2 * head, 2 * head), 2 * head)]
         return pltpu.make_async_remote_copy(src_ref=src, dst_ref=dst, send_sem=o_send.at[tile, z_dst], recv_sem=o_recv.at[z_row, tp],
@@ -171,14 +327,19 @@
 
             @pl.when(tile % NY == my_y)
             def _(tile=tile):
-                rows = chunk // (2 * NY)
                 og[tile // NY, :, pl.ds(pl.multiple_of(tp * 2 * head, 2 * head), 2 * head)] = \
                     o_st[pl.ds(pl.multiple_of(tile * rows, rows), rows), :]
         return carry
 
-    lax.fori_loop(0, 2 * chunk // TQ, q_step, 0)
-
-    rows = yst.shape[1]
+    kv_wait(low_needs)
+    lax.fori_loop(0, 3, q_step, 0)
+    wo_first()
+    lax.fori_loop(3, 4, q_step, 0)
+    kv_wait(high_needs)
+    lax.fori_loop(4, 7, q_step, 0)
+    wo_second()
+    lax.fori_loop(7, 8, q_step, 0)
+    wo_third()
 
     def o_arrival(z_row, src):
         dst = og.at[z_row, :, pl.ds(src * 2 * head, 2 * head)]
@@ -190,8 +351,7 @@
             src_ref=yst.at[z_dst], dst_ref=yv.at[:, pl.ds(pl.multiple_of(z_src * cols, 128), cols)],
             send_sem=y_send.at[z_dst], recv_sem=y_recv.at[z_src], device_id={"tp": NY * z_dst + my_y}, device_id_type=MESH)
 
-    for idx in range(n_tp):
-        wo_copy(idx).wait()
+    wo_last()
     for half in range(2):
         for z_row in (2 * half, 2 * half + 1):
             for src in range(n_tp):
@@ -229,74 +389,60 @@
         @pl.when(my_z != z_dst)
         def _(z_dst=z_dst):
             y_copy(z_dst, my_z).wait_send()
+    for copy in sends + slabs:
+        copy.wait_send()
+    for step in range(1, n_tp):
+        wo_copy(step).wait_send()
+    for half in range(2):
+        blk = (sp, 2 * n_sp - 1 - sp)[half]
+        for back in range(1, n_back + 1):
+            dst, wanted = kv_target(blk, back)
+
+            @pl.when(wanted)
+            def _(half=half, blk=blk, back=back, dst=dst):
+                kv_copy(blk, 0, chunk, half, back, dst).wait_send()
     y_out.wait()
 
 
-def attn_out(q_loc, kv_all, wo_rel):
-    n_e, _, _, w_rows, cols = wo_rel.shape
-    rows, two_head = q_loc.shape
-    n_tp = NY * NY
-    any_spec = pl.BlockSpec(memory_space=pl.ANY)
-    n_keys = kv_all.shape[0] * rows
-    dma = pltpu.SemaphoreType.DMA
-    return pl.pallas_call(
-        attn_out_kernel,
-        out_shape=jax.ShapeDtypeStruct((rows // n_tp, NY * cols), jnp.bfloat16),
-        in_specs=[any_spec] * 3,
-        out_specs=any_spec,
-        scratch_shapes=[
-            pltpu.VMEM((rows, two_head), jnp.bfloat16),
-            pltpu.VMEM((n_keys, two_head), jnp.bfloat16),
-            pltpu.VMEM((n_tp, n_e, w_rows, cols), jnp.bfloat16),
-            pltpu.VMEM((2 * TQ, WINDOW + TQ), jnp.float32),
-            pltpu.VMEM((2 * TQ, two_head // 2), jnp.float32),
-            pltpu.VMEM((2 * TQ, two_head // 2), jnp.float32),
-            pltpu.VMEM((2 * TQ, two_head // 2), jnp.float32),
-            pltpu.VMEM((2 * TQ, two_head // 2), jnp.float32),
-            pltpu.VMEM((rows, two_head), jnp.bfloat16),
-            pltpu.VMEM((NY, rows // n_tp, n_tp * two_head), jnp.bfloat16),
-            pltpu.VMEM((NY, rows // n_tp, cols), jnp.bfloat16),
-            pltpu.VMEM((rows // n_tp, NY * cols), jnp.bfloat16),
-            dma, dma((16,)), dma((n_tp,)), dma((n_tp, NY)), dma((NY, n_tp)), dma((NY,)), dma((NY,)), dma,
-        ],
-        compiler_params=pltpu.CompilerParams(collective_id=1, has_side_effects=True, vmem_limit_bytes=62 * 1024 * 1024),
-        cost_estimate=pl.CostEstimate(flops=20_000_000_000, bytes_accessed=30_000_000, transcendentals=16_000_000),
-        name="attn_out",
-    )(q_loc, kv_all, wo_rel)
-
-
-def gather_w_out(w_out):
-    heads_loc, head_dim, d_model = w_out.shape
-    sp_rank, tp_rank = lax.axis_index("sp"), lax.axis_index("tp")
-    n_sp = lax.axis_size("sp")
-    rows = heads_loc * head_dim // n_sp
-    flat = w_out.reshape(heads_loc * head_dim, d_model)
-    mine = lax.dynamic_slice_in_dim(flat, sp_rank * rows, rows, 0)
-    my_z = tp_rank // NY
-    pieces = []
-    for k in range(NY):
-        piece = lax.dynamic_slice_in_dim(mine, ((my_z + k) % NY) * (d_model // NY), d_model // NY, 1)
-        if k:
-            piece = lax.ppermute(piece, "tp", [(t, ((t // NY + k) % NY) * NY + t % NY) for t in range(NY * NY)])
-        pieces.append(piece)
-    part = jnp.stack(pieces)
-    part = lax.all_gather(part, "tp", axis=0, axis_index_groups=[[NY * z + y for y in range(NY)] for z in range(NY)])
-    return lax.all_gather(part, "sp", axis=0)
-
-
 def solution(mesh):
+    n_sp, n_tp = mesh.shape["sp"], mesh.shape["tp"]
+
     def local_attn(x_part, w_query, w_key, w_value, w_out):
-        d_model = x_part.shape[1]
-        wo_rel = gather_w_out(w_out)
-        x_block = lax.all_gather(x_part, "tp", axis=0, tiled=True)
-        rows = x_block.shape[0]
-
-        def project(weight):
-            return jnp.dot(x_block, weight.reshape(d_model, -1), preferred_element_type=jnp.float32).astype(jnp.bfloat16)
-
-        q_loc = project(w_query)
-        kv_loc = jnp.concatenate([project(w_key), project(w_value)], axis=1)
-        kv_all = lax.all_gather(kv_loc.reshape(2, rows // 2, -1), "sp", axis=0)
-        return attn_out(q_loc, kv_all, wo_rel)
+        rows, d_model = x_part.shape
+        heads_loc, head = w_query.shape[1], w_query.shape[2]
+        two_head = heads_loc * head
+        seq_loc = rows * n_tp
+        cols = d_model // NY
+        any_spec = pl.BlockSpec(memory_space=pl.ANY)
+        dma = pltpu.SemaphoreType.DMA
+        bf16, f32 = jnp.bfloat16, jnp.float32
+        wo_rows = w_out.shape[0] * w_out.shape[1] // n_sp
+        return pl.pallas_call(
+            layer_kernel,
+            out_shape=jax.ShapeDtypeStruct((rows, d_model), bf16),
+            in_specs=[any_spec] * 5,
+            out_specs=any_spec,
+            scratch_shapes=[
+                pltpu.VMEM((n_tp, rows, d_model), bf16),
+                pltpu.VMEM((d_model, 2 * two_head), bf16),
+                pltpu.VMEM((seq_loc, two_head), bf16),
+                pltpu.VMEM((n_sp * seq_loc, two_head), bf16),
+                pltpu.VMEM((n_tp, n_sp, wo_rows, cols), bf16),
+                pltpu.VMEM((2 * TQ, WINDOW + TQ), f32),
+                pltpu.VMEM((2 * TQ, head), f32),
+                pltpu.VMEM((2 * TQ, head), f32),
+                pltpu.VMEM((2 * TQ, head), f32),
+                pltpu.VMEM((2 * TQ, head), f32),
+                pltpu.VMEM((seq_loc, two_head), bf16),
+                pltpu.VMEM((NY, rows, n_tp * two_head), bf16),
+                pltpu.VMEM((NY, rows, cols), bf16),
+                pltpu.VMEM((rows, d_model), bf16),
+                dma, dma((3,)), dma((48,)), dma((n_tp, 4)), dma((2, 4)), dma((2 * n_sp,)), dma, dma((n_tp,)), dma((n_tp,)),
+                dma((16,)), dma((n_sp, 2)), dma((n_tp, NY)), dma((NY, n_tp)), dma((NY,)), dma((NY,)), dma,
+            ],
+            compiler_params=pltpu.CompilerParams(collective_id=1, has_side_effects=True, vmem_limit_bytes=67043328),
+            name="layer",
+        )(x_part, w_query.reshape(d_model, two_head), w_key.reshape(d_model, head), w_value.reshape(d_model, head),
+          w_out.reshape(n_sp, wo_rows, d_model))
 
     return jax.shard_map(local_attn, mesh=mesh, in_specs=(P(("dp", "sp", "tp"), None), P(None, "tp", None), P(None, "tp", None), P(None, "tp", None), P("tp", None, None)), out_specs=P(("dp", "sp", "tp"), None), check_vma=False)

time: 369 us -> 207 us (0.56)
  the two profiles are of different devices: /device:TPU:85 before, /device:TPU:1 now
where the time goes in v2:
time: 207 us; the launch traced here: 206 us
  Pallas kernels  201 us (97%)
  local copies, waits for them, and re-layouts  5.74 us (3%)
    pallas_call x1, Pallas kernels, local_attn(): pl.pallas_call(layer_kernel, out_shape=jax.ShapeDtypeStruct((rows, d_mode...  201 us
    unnamed x2, local copies, waits for them, and re-layouts  5.74 us

profile of v2, /device:TPU:1, one launch (start us, length us, event | category | flops | bytes accessed | tf_op | source)
XLA Modules:
  0.0 206.3 jit_solution(16549524301746764736)
XLA Ops:
  0.0 3.4 %copy.8 = bf16[576,8,2,128]{3,1,2,0:T(8,128)(2,1)} copy(bf16[576,8,2,128]{3,2,1,0:T(2,128)(2,1)} %bitcast.8) | data formatting | bytes 4718592
  3.4 200.6 %layer.1 = bf16[128,4608]{1,0:T(8,128)(2,1)} custom-call(bf16[128,4608]{1,0:T(8,128)(2,1)} %x_hbm.1, bf16[4608,256]{1,0:T(8,128)(2,1)} %bitcast.7, bf16[4608,128]{1,0:T(8,128)(2,1)} %bitcast.10, bf16[4608,128]{1,0:T(8,128)(2,1)} %bitcast.11, bf16[8,32,4608]{2,1,0:T(8,128)(2,1)} %bitcast.9), custom_call_target="tpu_custom_call" | custom-call | tf_op jit(solution)/shard_map/layer/pallas_call | solution.py:420
  204.0 2.4 %copy.10 = bf16[128,4608]{1,0:T(8,128)(2,1)} copy(bf16[128,4608]{1,0:T(8,128)(2,1)} %layer.1) | data formatting | bytes 2359296

commit v3 on v2

--- a/solution.py
+++ b/solution.py
@@ -21,8 +21,9 @@
     return lax.dot_general(lhs, rhs, (((1,), (1,)), ((), ())), preferred_element_type=jnp.float32)
 
 
-def layer_kernel(x_hbm, wq_hbm, wk_hbm, wv_hbm, wo_hbm, y_hbm, xg, w_v, q_v, kv_v, wo_v, s_v, mx_v, mb_v, l_v, acc_v, o_st, og, yst, yv,
-                 x_sem, w_sem, x_send, x_recv, kv_send, kv_recv, wo_sem, wo_send, wo_recv, sl_send, sl_recv, o_send, o_recv, y_send, y_recv, y_sem):
+def layer_kernel(x_hbm, wq_hbm, wk_hbm, wv_hbm, wo_hbm, y_hbm, xg, w_v, q_v, kv_v, q_st, kv_st, wo_v, s_v, mx_v, mb_v, l_v, acc_v, o_st, og,
+                 yst, yv, x_sem, wl_sem, x_send, x_recv, w_send, w_recv, share_send, share_recv, a_send, a_recv, kv_send, kv_recv, wo_sem,
+                 wo_send, wo_recv, sl_send, sl_recv, o_send, o_recv, y_send, y_recv, y_sem):
     sp = lax.axis_index("sp")
     tp = lax.axis_index("tp")
     my_z, my_y = tp // NY, tp % NY
@@ -33,15 +34,17 @@
     head = kv_v.shape[1] // 2
     cols = yst.shape[2]
     rows = yst.shape[1]
+    part = NY * rows
     coef = head ** -0.5 * LOG2E
-    n_back = WINDOW // chunk
-    part = rows // 4
-
-    x_load = pltpu.make_async_copy(x_hbm, xg.at[tp], x_sem)
+    d_half = w_v.shape[1] // 2
+    s_rows = d_half // 6
+    d_rows = 2 * s_rows
+
+    x_load = pltpu.make_async_copy(x_hbm, xg.at[my_y], x_sem)
     x_load.start()
-    w_loads = (pltpu.make_async_copy(wq_hbm, w_v.at[:, 0:2 * head], w_sem.at[0]),
-               pltpu.make_async_copy(wk_hbm, w_v.at[:, 2 * head:3 * head], w_sem.at[1]),
-               pltpu.make_async_copy(wv_hbm, w_v.at[:, 3 * head:4 * head], w_sem.at[2]))
+    w_loads = (pltpu.make_async_copy(wq_hbm, w_v.at[my_z, :, 0:2 * head], wl_sem.at[0]),
+               pltpu.make_async_copy(wk_hbm, w_v.at[my_z, :, 2 * head:3 * head], wl_sem.at[1]),
+               pltpu.make_async_copy(wv_hbm, w_v.at[my_z, :, 3 * head:4 * head], wl_sem.at[2]))
     for load in w_loads:
         load.start()
 
@@ -54,103 +57,167 @@
 
     zm, zp, zo = (my_z + 3) % NY, (my_z + 1) % NY, (my_z + 2) % NY
     ym, yp, yo = (my_y + 3) % NY, (my_y + 1) % NY, (my_y + 2) % NY
+    x_left, x_right, x_far = (my_x + 3) % NY, (my_x + 1) % NY, (my_x + 2) % NY
     sends = []
-
-    def x_copy(src_tp, first, count, dst_tp, slot):
-        ref = xg.at[src_tp, pl.ds(first * part, count * part)]
-        return pltpu.make_async_remote_copy(src_ref=ref, dst_ref=ref, send_sem=x_send.at[slot], recv_sem=x_recv.at[src_tp, first],
-                                            device_id={"tp": dst_tp}, device_id_type=MESH)
-
-    def x_put(z_src, y_src, first, count, z_dst, y_dst):
-        copy = x_copy(NY * z_src + y_src, first, count, NY * z_dst + y_dst, len(sends))
+    n_sends = [0, 0]
+
+    def x_copy(y_src, first, count, y_dst, slot):
+        ref = xg.at[y_src, pl.ds(first * (rows // 2), count * (rows // 2))]
+        return pltpu.make_async_remote_copy(src_ref=ref, dst_ref=ref, send_sem=x_send.at[slot], recv_sem=x_recv.at[y_src, first],
+                                            device_id={"tp": NY * my_z + y_dst}, device_id_type=MESH)
+
+    def x_put(y_src, first, count, y_dst):
+        copy = x_copy(y_src, first, count, y_dst, n_sends[0])
+        n_sends[0] += 1
         sends.append(copy)
         copy.start()
 
-    def x_wait(z_src, y_src, first, count):
-        x_copy(NY * z_src + y_src, first, count, 0, 0).wait_recv()
-
-    def kv_copy(src_blk, first, count, half, back, dst_sp):
-        ref = kv_v.at[pl.ds(pl.multiple_of(src_blk * chunk + first, rows), count)]
-        return pltpu.make_async_remote_copy(src_ref=ref, dst_ref=ref, send_sem=kv_send.at[half, back - 1], recv_sem=kv_recv.at[src_blk],
-                                            device_id={"sp": dst_sp}, device_id_type=MESH)
-
-    def kv_target(blk, back):
-        tgt = blk + back
-        low = tgt < n_sp
-        dst = jnp.where(low, tgt, 2 * n_sp - 1 - tgt)
-        return dst, (tgt < 2 * n_sp) & (low | (blk >= n_sp) | (dst < sp))
-
-    def project(tiles):
+    def x_wait(y_src, first, count):
+        x_copy(y_src, first, count, 0, 0).wait_recv()
+
+    def w_copy(z_src, x_src, first, count, dst, slot):
+        size = d_rows if x_src is None else s_rows
+        base = my_c * d_half + (0 if x_src is None else d_rows + x_src * s_rows)
+        ref = w_v.at[z_src, pl.ds(pl.multiple_of(base + first * (size // 2), 64), count * (size // 2))]
+        return pltpu.make_async_remote_copy(src_ref=ref, dst_ref=ref, send_sem=w_send.at[slot],
+                                            recv_sem=w_recv.at[z_src, NY if x_src is None else x_src, first], device_id=dst, device_id_type=MESH)
+
+    def w_put(z_src, x_src, first, count, dst):
+        copy = w_copy(z_src, x_src, first, count, dst, n_sends[1])
+        n_sends[1] += 1
+        sends.append(copy)
+        copy.start()
+
+    def w_wait(z_src, x_src, first, count):
+        w_copy(z_src, x_src, first, count, {"tp": 0}, 0).wait_recv()
+
+    def to_z(z_dst):
+        return {"tp": NY * z_dst + my_y}
+
+    def to_x(x_dst):
+        return {"sp": 2 * x_dst + my_c}
+
+    def share_copy(z_src, core, slot):
+        ref = w_v.at[z_src, pl.ds(pl.multiple_of(core * d_half, 64), d_half)]
+        return pltpu.make_async_remote_copy(src_ref=ref, dst_ref=ref, send_sem=share_send.at[slot], recv_sem=share_recv.at[z_src],
+                                            device_id={"sp": 2 * my_x + 1 - my_c}, device_id_type=MESH)
+
+    def blk_of(z_idx):
+        return jnp.where(z_idx < NY // 2, sp, 2 * n_sp - 1 - sp)
+
+    def kv_rows(z_idx):
+        return pl.multiple_of(blk_of(z_idx) * chunk + (z_idx % 2) * part, part)
+
+    def own_products(y_list):
         def body(idx, carry):
-            tile = tiles[0]
-            for other in range(1, len(tiles)):
-                tile = jnp.where(idx == other, tiles[other], tile)
-            prod = jnp.dot(xg[tile], w_v[...], preferred_element_type=jnp.float32).astype(jnp.bfloat16)
-            half = tile // (n_tp // 2)
-            blk = jnp.where(half == 0, sp, 2 * n_sp - 1 - sp)
-            first = (tile % (n_tp // 2)) * rows
-            q_v[pl.ds(pl.multiple_of(tile * rows, rows), rows), :] = prod[:, :2 * head]
-            kv_v[pl.ds(pl.multiple_of(blk * chunk + first, rows), rows), :] = prod[:, 2 * head:]
-            for back in range(1, n_back + 1):
-                dst, wanted = kv_target(blk, back)
-
-                @pl.when(wanted)
-                def _(back=back, dst=dst):
-                    kv_copy(blk, first, rows, half, back, dst).start()
+            y_idx = y_list[0]
+            for other in range(1, len(y_list)):
+                y_idx = jnp.where(idx == other, y_list[other], y_idx)
+            prod = jnp.dot(xg[y_idx], w_v[my_z], preferred_element_type=jnp.float32).astype(jnp.bfloat16)
+            q_v[pl.ds(pl.multiple_of(my_z * part + y_idx * rows, rows), rows), :] = prod[:, :2 * head]
+            kv_v[pl.ds(pl.multiple_of(kv_rows(my_z) + y_idx * rows, rows), rows), :] = prod[:, 2 * head:]
             return carry
 
-        lax.fori_loop(0, len(tiles), body, 0)
-
-    def tile_of(z_idx, y_idx):
-        return NY * z_idx + y_idx
-
-    x_load.wait()
-    for z_dst, y_dst, first in ((zp, my_y, 0), (zm, my_y, 0), (my_z, yp, 2), (my_z, ym, 2), (my_z, yp, 0), (my_z, ym, 0), (zp, my_y, 2), (zm, my_y, 2)):
-        x_put(my_z, my_y, first, 2, z_dst, y_dst)
-    for load in w_loads:
-        load.wait()
-    project([tp])
-
-    def take_items(z_item, y_item):
-        for y_src, first, y_dst in ((ym, 0, yp), (yp, 1, ym)):
-            x_wait(z_item, y_src, 0, 2)
-            x_put(z_item, y_src, first, 1, my_z, y_dst)
-        for z_src, first, z_dst in ((zm, 2, zp), (zp, 3, zm)):
-            x_wait(z_src, y_item, 2, 2)
-            x_put(z_src, y_item, first, 1, z_dst, my_y)
-
-    def send_items(z_item, y_item):
-        for y_dst in (yp, ym):
-            x_put(z_item, my_y, 0, 2, my_z, y_dst)
-        for z_dst in (zp, zm):
-            x_put(my_z, y_item, 2, 2, z_dst, my_y)
-
-    def take_far(z_item, y_item):
-        for first in range(2):
-            x_wait(z_item, yo, first, 1)
-            x_wait(zo, y_item, 2 + first, 1)
-
-    for z_src, first, z_dst in ((zm, 0, zp), (zp, 1, zm)):
-        x_wait(z_src, my_y, 0, 2)
-        x_put(z_src, my_y, first, 1, z_dst, my_y)
-    for y_src, first, y_dst in ((ym, 2, yp), (yp, 3, ym)):
-        x_wait(my_z, y_src, 2, 2)
-        x_put(my_z, y_src, first, 1, my_z, y_dst)
-    send_items(zm, ym)
-    send_items(zp, yp)
-    take_items(my_z, my_y)
-    project([tile_of(zm, my_y), tile_of(zp, my_y), tile_of(my_z, ym), tile_of(my_z, yp)])
-    for first in range(2):
-        x_wait(zo, my_y, first, 1)
-        x_wait(my_z, yo, 2 + first, 1)
-    send_items(zo, yo)
-    take_items(zm, ym)
-    project([tile_of(zm, ym)])
-    take_items(zp, yp)
-    project([tile_of(zm, yp), tile_of(zp, ym), tile_of(zp, yp)])
-    take_far(my_z, my_y)
-    project([tile_of(my_z, yo), tile_of(zo, my_y)])
-    take_items(zo, yo)
+        lax.fori_loop(0, len(y_list), body, 0)
+
+    def a_copy(kind, z_src, z_dst, slot):
+        if kind:
+            src, dst = q_st.at[slot], q_v.at[pl.ds(pl.multiple_of(z_src * part, part), part)]
+        else:
+            src, dst = kv_st.at[slot], kv_v.at[pl.ds(kv_rows(z_src), part)]
+        return pltpu.make_async_remote_copy(src_ref=src, dst_ref=dst, send_sem=a_send.at[kind, slot], recv_sem=a_recv.at[kind, z_src],
+                                            device_id=to_z(z_dst), device_id_type=MESH)
+
+    def products(z_dst, slot):
+        def body(idx, carry):
+            lhs = xg[pl.ds(2 * idx, 2)].reshape(2 * rows, xg.shape[2])
+            prod = jnp.dot(lhs, w_v[z_dst], preferred_element_type=jnp.float32).astype(jnp.bfloat16)
+            at = pl.ds(pl.multiple_of(idx * 2 * rows, 2 * rows), 2 * rows)
+            q_st[slot, at, :] = prod[:, :2 * head]
+            kv_st[slot, at, :] = prod[:, 2 * head:]
+            return carry
+
+        lax.fori_loop(0, 2, body, 0)
+        for kind in range(2):
+            a_copy(kind, my_z, z_dst, slot).start()
+
+    def a_wait(kind, z_src):
+        a_copy(kind, z_src, 0, 0).wait_recv()
+
+    def kv_part(pair, core, z_idx, kind, dst):
+        blk = jnp.where(pair < NY, 2 * pair + core, 2 * pair + 1 - core)
+        ref = kv_v.at[pl.ds(pl.multiple_of(blk * chunk + (z_idx % 2) * part, part), part)]
+        return pltpu.make_async_remote_copy(src_ref=ref, dst_ref=ref, send_sem=kv_send.at[z_idx, kind], recv_sem=kv_recv.at[blk, z_idx % 2],
+                                            device_id=dst, device_id_type=MESH)
+
+    partner = {"sp": 2 * my_x + 1 - my_c}
+
+    def own_pair(z_idx):
+        return jnp.where(z_idx < NY // 2, my_x, 2 * NY - 1 - my_x)
+
+    def own_next(z_idx):
+        low = z_idx < NY // 2
+        return jnp.where(low, jnp.where(my_x < NY - 1, my_x + 1, NY - 2), my_x - 1), low | (my_x >= 1)
+
+    def direct_in(z_idx):
+        low = z_idx < NY // 2
+        return jnp.where(low, my_x - 1, 2 * NY - 2 - my_x), (low & (my_x >= 1)) | (jnp.logical_not(low) & (my_x < NY - 1))
+
+    def direct_next(z_idx):
+        return jnp.where(z_idx < NY // 2, my_x + 1, my_x - 1), (my_x >= 1) & (my_x < NY - 1)
+
+    def relay_in(z_idx):
+        low = z_idx < NY // 2
+        return jnp.where(low, my_x - 2, 2 * NY - 3 - my_x), (low & (my_x >= 2)) | (jnp.logical_not(low) & (my_x < NY - 2))
+
+    def turn_in(z_idx):
+        return NY - 1, (z_idx < NY // 2) & (my_x == NY - 2)
+
+    def kv_own(z_idx, act):
+        dst, wanted = own_next(z_idx)
+
+        @pl.when(wanted)
+        def _():
+            act(kv_part(own_pair(z_idx), my_c, z_idx, 1, to_x(dst)))
+
+        act(kv_part(own_pair(z_idx), my_c, z_idx, 0, partner))
+
+    def kv_direct(z_idx, act, arrive):
+        pair, wanted = direct_in(z_idx)
+
+        @pl.when(wanted)
+        def _():
+            if arrive:
+                kv_part(pair, my_c, z_idx, 2, partner).wait_recv()
+            dst, more = direct_next(z_idx)
+
+            @pl.when(more)
+            def _():
+                act(kv_part(pair, my_c, z_idx, 3, to_x(dst)))
+
+            act(kv_part(pair, my_c, z_idx, 2, partner))
+
+    def kv_relay(z_idx, act, arrive):
+        for kind, (pair, wanted) in ((4, relay_in(z_idx)), (5, turn_in(z_idx))):
+            @pl.when(wanted)
+            def _(kind=kind, pair=pair):
+                copy = kv_part(pair, my_c, z_idx, kind, partner)
+                if arrive:
+                    copy.wait_recv()
+                act(copy)
+
+    def kv_from_partner(z_idx):
+        kv_part(own_pair(z_idx), 1 - my_c, z_idx, 0, partner).wait_recv()
+        for pair, wanted in (direct_in(z_idx), relay_in(z_idx), turn_in(z_idx)):
+            @pl.when(wanted)
+            def _(pair=pair):
+                kv_part(pair, 1 - my_c, z_idx, 0, partner).wait_recv()
+
+    def start(copy):
+        copy.start()
+
+    def done(copy):
+        copy.wait_send()
 
     def wo_copy(step):
         dst = (tp + step) % n_tp
@@ -158,19 +225,6 @@
         return pltpu.make_async_remote_copy(src_ref=src_ref, dst_ref=wo_v.at[tp, sp], send_sem=wo_send.at[step], recv_sem=wo_recv.at[tp],
                                             device_id={"tp": dst}, device_id_type=MESH)
 
-    wo_own = pltpu.make_async_copy(wo_hbm.at[sp, :, pl.ds(pl.multiple_of(my_z * cols, 128), cols)], wo_v.at[tp, sp], wo_sem)
-    wo_own.start()
-    for step in range(1, n_tp):
-        wo_copy(step).start()
-
-    take_far(zm, ym)
-    project([tile_of(zm, yo), tile_of(zo, ym)])
-    take_far(zp, yp)
-    project([tile_of(zp, yo), tile_of(zo, yp)])
-    take_far(zo, yo)
-    project([tile_of(zo, yo)])
-
-    x_left, x_right, x_far = (my_x + 3) % NY, (my_x + 1) % NY, (my_x + 2) % NY
     slabs = []
 
     def slab_copy(x_src, c_src, first, count, x_dst, c_dst, slot):
@@ -214,17 +268,79 @@
         for first in range(2):
             slab_wait(x_far, 1 - my_c, first, 1)
 
-    def low_needs(blk):
-        return (blk < sp) & (blk >= sp - n_back)
-
-    def high_needs(blk):
-        return (blk < 2 * n_sp - 1 - sp) & (blk >= 2 * n_sp - 1 - sp - n_back) & (blk != sp) & jnp.logical_not(low_needs(blk))
-
-    def kv_wait(needs):
-        for blk in range(2 * n_sp - 1):
-            @pl.when(needs(blk))
-            def _(blk=blk):
-                kv_copy(blk, 0, chunk, 0, 1, 0).wait_recv()
+    x_load.wait()
+    x_put(my_y, 0, 2, yp)
+    x_put(my_y, 0, 2, ym)
+    for load in w_loads:
+        load.wait()
+    for z_dst in (zp, zm):
+        w_put(my_z, my_x, 0, 2, to_z(z_dst))
+    for z_src, first, z_dst in ((zm, 0, zp), (zp, 1, zm)):
+        w_wait(z_src, my_x, 0, 2)
+        w_put(z_src, my_x, first, 1, to_z(z_dst))
+        for x_dst in (x_right, x_left):
+            w_put(z_src, my_x, 0, 2, to_x(x_dst))
+    for z_dst in (zp, zm):
+        w_put(my_z, None, 0, 2, to_z(z_dst))
+    own_products([my_y])
+    for z_src in (zm, zp):
+        for x_src, first, x_dst in ((x_left, 0, x_right), (x_right, 1, x_left)):
+            w_wait(z_src, x_src, 0, 2)
+            w_put(z_src, x_src, first, 1, to_x(x_dst))
+    for first in range(2):
+        w_wait(zo, my_x, first, 1)
+    for x_dst in (x_right, x_left):
+        w_put(zo, my_x, 0, 2, to_x(x_dst))
+    for y_src, first, y_dst in ((ym, 0, yp), (yp, 1, ym)):
+        x_wait(y_src, 0, 2)
+        x_put(y_src, first, 1, y_dst)
+    for z_src, first, z_dst in ((zm, 0, zp), (zp, 1, zm)):
+        w_wait(z_src, None, 0, 2)
+        w_put(z_src, None, first, 1, to_z(z_dst))
+    own_products([ym, yp])
+    for slot, z_src in enumerate((zm, zp)):
+        for first in range(2):
+            w_wait(z_src, x_far, first, 1)
+        share_copy(z_src, my_c, slot).start()
+    for x_src, first, x_dst in ((x_left, 0, x_right), (x_right, 1, x_left)):
+        w_wait(zo, x_src, 0, 2)
+        w_put(zo, x_src, first, 1, to_x(x_dst))
+    for first in range(2):
+        x_wait(yo, first, 1)
+    own_products([yo])
+    kv_own(my_z, start)
+    for slot, z_dst in enumerate((zm, zp)):
+        share_copy(z_dst, 1 - my_c, slot).wait_recv()
+        products(z_dst, slot)
+    for first in range(2):
+        w_wait(zo, None, first, 1)
+        w_wait(zo, x_far, first, 1)
+    share_copy(zo, my_c, 2).start()
+    share_copy(zo, 1 - my_c, 2).wait_recv()
+    products(zo, 2)
+    kv_direct(my_z, start, True)
+    for z_src in (zm, zp):
+        a_wait(0, z_src)
+        kv_own(z_src, start)
+    kv_relay(my_z, start, True)
+    wo_own = pltpu.make_async_copy(wo_hbm.at[sp, :, pl.ds(pl.multiple_of(my_z * cols, 128), cols)], wo_v.at[tp, sp], wo_sem)
+    wo_own.start()
+    for step in range(1, n_tp):
+        wo_copy(step).start()
+
+    for z_src in (zm, zp):
+        kv_direct(z_src, start, True)
+    a_wait(0, zo)
+    kv_own(zo, start)
+    for z_src in (zm, zp):
+        kv_relay(z_src, start, True)
+    kv_direct(zo, start, True)
+    kv_relay(zo, start, True)
+    wo_first()
+    for z_src in (zm, zp, zo):
+        a_wait(1, z_src)
+    for z_idx in range(NY):
+        kv_from_partner(z_idx)
 
     row_i = lax.broadcasted_iota(jnp.int32, (2 * TQ, TQ), 0) % TQ
     col_i = lax.broadcasted_iota(jnp.int32, (2 * TQ, TQ), 1)
@@ -331,14 +447,9 @@
                     o_st[pl.ds(pl.multiple_of(tile * rows, rows), rows), :]
         return carry
 
-    kv_wait(low_needs)
-    lax.fori_loop(0, 3, q_step, 0)
-    wo_first()
-    lax.fori_loop(3, 4, q_step, 0)
-    kv_wait(high_needs)
-    lax.fori_loop(4, 7, q_step, 0)
+    lax.fori_loop(0, 5, q_step, 0)
     wo_second()
-    lax.fori_loop(7, 8, q_step, 0)
+    lax.fori_loop(5, 2 * chunk // TQ, q_step, 0)
     wo_third()
 
     def o_arrival(z_row, src):
@@ -393,14 +504,14 @@
         copy.wait_send()
     for step in range(1, n_tp):
         wo_copy(step).wait_send()
-    for half in range(2):
-        blk = (sp, 2 * n_sp - 1 - sp)[half]
-        for back in range(1, n_back + 1):
-            dst, wanted = kv_target(blk, back)
-
-            @pl.when(wanted)
-            def _(half=half, blk=blk, back=back, dst=dst):
-                kv_copy(blk, 0, chunk, half, back, dst).wait_send()
+    for slot in range(3):
+        share_copy(my_z, my_c, slot).wait_send()
+        for kind in range(2):
+            a_copy(kind, my_z, 0, slot).wait_send()
+    for z_idx in range(NY):
+        kv_own(z_idx, done)
+        kv_direct(z_idx, done, False)
+        kv_relay(z_idx, done, False)
     y_out.wait()
 
 
@@ -423,10 +534,12 @@
             in_specs=[any_spec] * 5,
             out_specs=any_spec,
             scratch_shapes=[
-                pltpu.VMEM((n_tp, rows, d_model), bf16),
-                pltpu.VMEM((d_model, 2 * two_head), bf16),
+                pltpu.VMEM((NY, rows, d_model), bf16),
+                pltpu.VMEM((NY, d_model, 2 * two_head), bf16),
                 pltpu.VMEM((seq_loc, two_head), bf16),
                 pltpu.VMEM((n_sp * seq_loc, two_head), bf16),
+                pltpu.VMEM((NY - 1, seq_loc // NY, two_head), bf16),
+                pltpu.VMEM((NY - 1, seq_loc // NY, two_head), bf16),
                 pltpu.VMEM((n_tp, n_sp, wo_rows, cols), bf16),
                 pltpu.VMEM((2 * TQ, WINDOW + TQ), f32),
                 pltpu.VMEM((2 * TQ, head), f32),
@@ -437,7 +550,8 @@
                 pltpu.VMEM((NY, rows, n_tp * two_head), bf16),
                 pltpu.VMEM((NY, rows, cols), bf16),
                 pltpu.VMEM((rows, d_model), bf16),
-                dma, dma((3,)), dma((48,)), dma((n_tp, 4)), dma((2, 4)), dma((2 * n_sp,)), dma, dma((n_tp,)), dma((n_tp,)),
+                dma, dma((3,)), dma((4,)), dma((NY, 2)), dma((24,)), dma((NY, NY + 1, 2)), dma((3,)), dma((NY,)), dma((2, 3)), dma((2, NY)),
+                dma((NY, 6)), dma((2 * n_sp, 2)), dma, dma((n_tp,)), dma((n_tp,)),
                 dma((16,)), dma((n_sp, 2)), dma((n_tp, NY)), dma((NY, n_tp)), dma((NY,)), dma((NY,)), dma,
             ],
             compiler_params=pltpu.CompilerParams(collective_id=1, has_side_effects=True, vmem_limit_bytes=67043328),

time: 207 us -> 184 us (0.89)
  the two profiles are of different devices: /device:TPU:1 before, /device:TPU:83 now
where the time goes in v3:
time: 184 us
  Pallas kernels  178 us (97%)
  local copies, waits for them, and re-layouts  5.74 us (3%)
    pallas_call x1, Pallas kernels, local_attn(): pl.pallas_call(layer_kernel, out_shape=jax.ShapeDtypeStruct((rows, d_mode...  178 us
    unnamed x2, local copies, waits for them, and re-layouts  5.74 us

profile of v3, /device:TPU:83, one launch (start us, length us, event | category | flops | bytes accessed | tf_op | source)
XLA Modules:
  0.0 183.8 jit_solution(5543222642883289866)
XLA Ops:
  0.0 3.4 %copy.8 = bf16[576,8,2,128]{3,1,2,0:T(8,128)(2,1)} copy(bf16[576,8,2,128]{3,2,1,0:T(2,128)(2,1)} %bitcast.8) | data formatting | bytes 4718592
  3.4 178.1 %layer.1 = bf16[128,4608]{1,0:T(8,128)(2,1)} custom-call(bf16[128,4608]{1,0:T(8,128)(2,1)} %x_hbm.1, bf16[4608,256]{1,0:T(8,128)(2,1)} %bitcast.7, bf16[4608,128]{1,0:T(8,128)(2,1)} %bitcast.10, bf16[4608,128]{1,0:T(8,128)(2,1)} %bitcast.11, bf16[8,32,4608]{2,1,0:T(8,128)(2,1)} %bitcast.9), custom_call_target="tpu_custom_call" | custom-call | tf_op jit(solution)/shard_map/layer/pallas_call | solution.py:531
  181.5 2.4 %copy.10 = bf16[128,4608]{1,0:T(8,128)(2,1)} copy(bf16[128,4608]{1,0:T(8,128)(2,1)} %layer.1) | data formatting | bytes 2359296

commit v4 on v3

--- a/solution.py
+++ b/solution.py
@@ -21,9 +21,10 @@
     return lax.dot_general(lhs, rhs, (((1,), (1,)), ((), ())), preferred_element_type=jnp.float32)
 
 
-def layer_kernel(x_hbm, wq_hbm, wk_hbm, wv_hbm, wo_hbm, y_hbm, xg, w_v, q_v, kv_v, q_st, kv_st, wo_v, s_v, mx_v, mb_v, l_v, acc_v, o_st, og,
-                 yst, yv, x_sem, wl_sem, x_send, x_recv, w_send, w_recv, share_send, share_recv, a_send, a_recv, kv_send, kv_recv, wo_sem,
-                 wo_send, wo_recv, sl_send, sl_recv, o_send, o_recv, y_send, y_recv, y_sem):
+def layer_kernel(x_hbm, wq_hbm, wk_hbm, wv_hbm, wo_hbm, y_hbm, xg, w_v, q_v, kv_v, kv_st, far_st, wo_v, s_v, mx_v, mb_v, l_v, acc_v, o_st,
+                 og, yst, yv, x_sem, wl_sem, x_send, x_recv, w_send, w_recv, share_send, share_recv, a_send, a_recv, far_send, far_recv,
+                 pass_send, pass_recv, kv_send, kv_recv, wo_sem, wo_send, wo_recv, wy_send, wy_recv, sl_send, sl_recv, oy_send, oy_recv,
+                 oz_send, oz_recv, of_send, of_recv, y_send, y_recv, y_sem):
     sp = lax.axis_index("sp")
     tp = lax.axis_index("tp")
     my_z, my_y = tp // NY, tp % NY
@@ -122,7 +123,7 @@
 
     def a_copy(kind, z_src, z_dst, slot):
         if kind:
-            src, dst = q_st.at[slot], q_v.at[pl.ds(pl.multiple_of(z_src * part, part), part)]
+            src, dst = o_st.at[pl.ds(slot * part, part)], q_v.at[pl.ds(pl.multiple_of(z_src * part, part), part)]
         else:
             src, dst = kv_st.at[slot], kv_v.at[pl.ds(kv_rows(z_src), part)]
         return pltpu.make_async_remote_copy(src_ref=src, dst_ref=dst, send_sem=a_send.at[kind, slot], recv_sem=a_recv.at[kind, z_src],
@@ -132,17 +133,40 @@
         def body(idx, carry):
             lhs = xg[pl.ds(2 * idx, 2)].reshape(2 * rows, xg.shape[2])
             prod = jnp.dot(lhs, w_v[z_dst], preferred_element_type=jnp.float32).astype(jnp.bfloat16)
-            at = pl.ds(pl.multiple_of(idx * 2 * rows, 2 * rows), 2 * rows)
-            q_st[slot, at, :] = prod[:, :2 * head]
-            kv_st[slot, at, :] = prod[:, 2 * head:]
+            o_st[pl.ds(pl.multiple_of(slot * part + idx * 2 * rows, 2 * rows), 2 * rows), :] = prod[:, :2 * head]
+            kv_st[slot, pl.ds(pl.multiple_of(idx * 2 * rows, 2 * rows), 2 * rows), :] = prod[:, 2 * head:]
             return carry
 
         lax.fori_loop(0, 2, body, 0)
+
+    def a_start(z_dst, slot):
         for kind in range(2):
             a_copy(kind, my_z, z_dst, slot).start()
 
     def a_wait(kind, z_src):
         a_copy(kind, z_src, 0, 0).wait_recv()
+
+    half_rows = part // 2
+
+    def far_copy(kind, half):
+        src = o_st.at[pl.ds(2 * part + half * half_rows, half_rows)] if kind else kv_st.at[2, pl.ds(half * half_rows, half_rows)]
+        return pltpu.make_async_remote_copy(src_ref=src, dst_ref=far_st.at[kind, half], send_sem=far_send.at[kind, half],
+                                            recv_sem=far_recv.at[kind, half], device_id=to_z(zm if half else zp), device_id_type=MESH)
+
+    def pass_copy(kind, half, z_src):
+        at = (z_src * part if kind else kv_rows(z_src)) + half * half_rows
+        dst = (q_v if kind else kv_v).at[pl.ds(pl.multiple_of(at, half_rows), half_rows)]
+        return pltpu.make_async_remote_copy(src_ref=far_st.at[kind, half], dst_ref=dst, send_sem=pass_send.at[kind, half],
+                                            recv_sem=pass_recv.at[kind, half], device_id=to_z(zm if half else zp), device_id_type=MESH)
+
+    def far_pass(kind):
+        for half in range(2):
+            far_copy(kind, half).wait_recv()
+            pass_copy(kind, half, zp if half else zm).start()
+
+    def far_wait(kind):
+        for half in range(2):
+            pass_copy(kind, half, zo).wait_recv()
 
     def kv_part(pair, core, z_idx, kind, dst):
         blk = jnp.where(pair < NY, 2 * pair + core, 2 * pair + 1 - core)
@@ -220,12 +244,41 @@
         copy.wait_send()
 
     def wo_copy(step):
-        dst = (tp + step) % n_tp
-        src_ref = wo_hbm.at[sp, :, pl.ds(pl.multiple_of((dst // NY) * cols, 128), cols)]
-        return pltpu.make_async_remote_copy(src_ref=src_ref, dst_ref=wo_v.at[tp, sp], send_sem=wo_send.at[step], recv_sem=wo_recv.at[tp],
-                                            device_id={"tp": dst}, device_id_type=MESH)
+        dst = (my_z + step) % NY
+        src_ref = wo_hbm.at[sp, :, pl.ds(pl.multiple_of(dst * cols, 128), cols)]
+        return pltpu.make_async_remote_copy(src_ref=src_ref, dst_ref=wo_v.at[NY * my_y + my_z, sp], send_sem=wo_send.at[step],
+                                            recv_sem=wo_recv.at[my_z], device_id=to_z(dst), device_id_type=MESH)
+
+    wo_own = pltpu.make_async_copy(wo_hbm.at[sp, :, pl.ds(pl.multiple_of(my_z * cols, 128), cols)], wo_v.at[NY * my_y + my_z, sp], wo_sem)
+
+    def wo_z_start():
+        wo_own.start()
+        for step in range(1, NY):
+            wo_copy(step).start()
+
+    def wy_copy(y_src, first, count, y_dst, slot):
+        ref = wo_v.at[pl.ds(NY * y_src + 2 * first, 2 * count), sp]
+        return pltpu.make_async_remote_copy(src_ref=ref, dst_ref=ref, send_sem=wy_send.at[slot], recv_sem=wy_recv.at[y_src, first],
+                                            device_id={"tp": NY * my_z + y_dst}, device_id_type=MESH)
+
+    wy_sends = (wy_copy(my_y, 0, 2, yp, 0), wy_copy(my_y, 0, 2, ym, 1), wy_copy(ym, 0, 1, yp, 2), wy_copy(yp, 1, 1, ym, 3))
+
+    def wo_y_start():
+        wo_own.wait()
+        for z_src in (zm, zp, zo):
+            ref = wo_v.at[NY * my_y + z_src, sp]
+            pltpu.make_async_remote_copy(src_ref=ref, dst_ref=ref, send_sem=wo_send.at[1], recv_sem=wo_recv.at[z_src],
+                                         device_id=to_z(z_src), device_id_type=MESH).wait_recv()
+        for copy in wy_sends[:2]:
+            copy.start()
+
+    def wo_y_pass():
+        for y_src, copy in ((ym, wy_sends[2]), (yp, wy_sends[3])):
+            wy_copy(y_src, 0, 2, 0, 0).wait_recv()
+            copy.start()
 
     slabs = []
+    other_c = 1 - my_c
 
     def slab_copy(x_src, c_src, first, count, x_dst, c_dst, slot):
         ref = wo_v.at[pl.ds(first * (n_tp // 2), count * (n_tp // 2)), 2 * x_src + c_src]
@@ -233,40 +286,36 @@
                                             device_id={"sp": 2 * x_dst + c_dst}, device_id_type=MESH)
 
     def slab_put(x_src, first, count, x_dst, c_dst):
-        copy = slab_copy(x_src, my_c, first, count, x_dst, c_dst, len(slabs))
-        slabs.append(copy)
-        copy.start()
+        slabs.append((x_src, my_c, first, count, x_dst, c_dst, len(slabs)))
+        slab_copy(*slabs[-1]).start()
 
     def slab_wait(x_src, c_src, first, count):
         slab_copy(x_src, c_src, first, count, 0, 0, 0).wait_recv()
 
     def wo_first():
-        wo_own.wait()
-        for step in range(1, n_tp):
-            src = (tp + step) % n_tp
-            pltpu.make_async_remote_copy(src_ref=wo_v.at[src, sp], dst_ref=wo_v.at[src, sp], send_sem=wo_send.at[step], recv_sem=wo_recv.at[src],
-                                         device_id={"tp": src}, device_id_type=MESH).wait_recv()
+        for first in range(2):
+            wy_copy(yo, first, 1, 0, 0).wait_recv()
         for x_dst in (x_right, x_left):
             slab_put(my_x, 0, 2, x_dst, my_c)
-        slab_put(my_x, 0, 2, my_x, 1 - my_c)
+        slab_put(my_x, 0, 2, my_x, other_c)
 
     def wo_second():
         for x_src, first, x_dst in ((x_left, 0, x_right), (x_right, 1, x_left)):
             slab_wait(x_src, my_c, 0, 2)
             slab_put(x_src, first, 1, x_dst, my_c)
         for x_src in (x_left, x_right):
-            slab_put(x_src, 0, 2, my_x, 1 - my_c)
+            slab_put(x_src, 0, 2, my_x, other_c)
 
     def wo_third():
         for first in range(2):
             slab_wait(x_far, my_c, first, 1)
-            slab_put(x_far, first, 1, my_x, 1 - my_c)
+            slab_put(x_far, first, 1, my_x, other_c)
 
     def wo_last():
         for x_src in (my_x, x_left, x_right):
-            slab_wait(x_src, 1 - my_c, 0, 2)
+            slab_wait(x_src, other_c, 0, 2)
         for first in range(2):
-            slab_wait(x_far, 1 - my_c, first, 1)
+            slab_wait(x_far, other_c, first, 1)
 
     x_load.wait()
     x_put(my_y, 0, 2, yp)
@@ -282,6 +331,7 @@
             w_put(z_src, my_x, 0, 2, to_x(x_dst))
     for z_dst in (zp, zm):
         w_put(my_z, None, 0, 2, to_z(z_dst))
+    wo_z_start()
     own_products([my_y])
     for z_src in (zm, zp):
         for x_src, first, x_dst in ((x_left, 0, x_right), (x_right, 1, x_left)):
@@ -307,38 +357,45 @@
         w_put(zo, x_src, first, 1, to_x(x_dst))
     for first in range(2):
         x_wait(yo, first, 1)
+    wo_y_start()
     own_products([yo])
     kv_own(my_z, start)
     for slot, z_dst in enumerate((zm, zp)):
         share_copy(z_dst, 1 - my_c, slot).wait_recv()
         products(z_dst, slot)
+        a_start(z_dst, slot)
     for first in range(2):
         w_wait(zo, None, first, 1)
         w_wait(zo, x_far, first, 1)
     share_copy(zo, my_c, 2).start()
     share_copy(zo, 1 - my_c, 2).wait_recv()
     products(zo, 2)
+    for kind in range(2):
+        for half in range(2):
+            far_copy(kind, half).start()
     kv_direct(my_z, start, True)
     for z_src in (zm, zp):
         a_wait(0, z_src)
         kv_own(z_src, start)
+    far_pass(0)
     kv_relay(my_z, start, True)
-    wo_own = pltpu.make_async_copy(wo_hbm.at[sp, :, pl.ds(pl.multiple_of(my_z * cols, 128), cols)], wo_v.at[tp, sp], wo_sem)
-    wo_own.start()
-    for step in range(1, n_tp):
-        wo_copy(step).start()
-
+    wo_y_pass()
     for z_src in (zm, zp):
         kv_direct(z_src, start, True)
-    a_wait(0, zo)
+    far_wait(0)
     kv_own(zo, start)
+    far_pass(1)
     for z_src in (zm, zp):
         kv_relay(z_src, start, True)
     kv_direct(zo, start, True)
     kv_relay(zo, start, True)
     wo_first()
-    for z_src in (zm, zp, zo):
+    for z_src in (zm, zp):
         a_wait(1, z_src)
+    far_wait(1)
+    for slot in range(2):
+        a_copy(1, my_z, 0, slot).wait_send()
+        far_copy(1, slot).wait_send()
     for z_idx in range(NY):
         kv_from_partner(z_idx)
 
@@ -351,12 +408,38 @@
             best = jnp.maximum(best, scores[:, idx * head:(idx + 1) * head])
         return best
 
-    def o_copy(tile, z_dst):
-        y_dst, z_row = tile % NY, tile // NY
-        src = o_st.at[pl.ds(pl.multiple_of(tile * rows, rows), rows)]
-        dst = og.at[z_row, :, pl.ds(pl.multiple_of(tp * 2 * head, 2 * head), 2 * head)]
-        return pltpu.make_async_remote_copy(src_ref=src, dst_ref=dst, send_sem=o_send.at[tile, z_dst], recv_sem=o_recv.at[z_row, tp],
-                                            device_id={"tp": NY * z_dst + y_dst}, device_id_type=MESH)
+    wide_o = NY * 2 * head
+
+    def oy_copy(tile, src_tp):
+        return pltpu.make_async_remote_copy(
+            src_ref=o_st.at[pl.ds(pl.multiple_of(tile * rows, rows), rows)],
+            dst_ref=og.at[tile // NY, :, pl.ds(pl.multiple_of(src_tp * 2 * head, 2 * head), 2 * head)],
+            send_sem=oy_send.at[tile], recv_sem=oy_recv.at[tile // NY, src_tp % NY], device_id={"tp": NY * my_z + tile % NY}, device_id_type=MESH)
+
+    def oz_copy(row, z_src, side):
+        ref = og.at[row, :, pl.ds(pl.multiple_of(z_src * wide_o, wide_o), wide_o)]
+        return pltpu.make_async_remote_copy(src_ref=ref, dst_ref=ref, send_sem=oz_send.at[row, side], recv_sem=oz_recv.at[row, z_src],
+                                            device_id=to_z(zm if side else zp), device_id_type=MESH)
+
+    def of_copy(row, z_src, side):
+        ref = og.at[row, pl.ds(side * (rows // 2), rows // 2), pl.ds(pl.multiple_of(z_src * wide_o, wide_o), wide_o)]
+        return pltpu.make_async_remote_copy(src_ref=ref, dst_ref=ref, send_sem=of_send.at[row, side], recv_sem=of_recv.at[row, side],
+                                            device_id=to_z(zm if side else zp), device_id_type=MESH)
+
+    def o_round(row):
+        for y_src in (ym, yp, yo):
+            oy_copy(NY * row + my_y, NY * my_z + y_src).wait_recv()
+        for side in range(2):
+            oz_copy(row, my_z, side).start()
+
+    def o_pass(row):
+        for side, z_src in ((0, zm), (1, zp)):
+            oz_copy(row, z_src, side).wait_recv()
+            of_copy(row, z_src, side).start()
+
+    def o_far(row):
+        for side in range(2):
+            of_copy(row, zo, side).wait_recv()
 
     def attend(q_idx, gidx, wide, start_tile, n_steps, with_first):
         q_blk = q_v[pl.ds(pl.multiple_of(q_idx * TQ, TQ), TQ), :]
@@ -434,47 +517,47 @@
 
         for sub in range(2):
             tile = 2 * q_idx + sub
-            for z_dst in range(NY):
-                mine = (tile % NY == my_y) & (my_z == z_dst)
-
-                @pl.when(jnp.logical_not(mine))
-                def _(tile=tile, z_dst=z_dst):
-                    o_copy(tile, z_dst).start()
+
+            @pl.when(tile % NY != my_y)
+            def _(tile=tile):
+                oy_copy(tile, tp).start()
 
             @pl.when(tile % NY == my_y)
             def _(tile=tile):
                 og[tile // NY, :, pl.ds(pl.multiple_of(tp * 2 * head, 2 * head), 2 * head)] = \
                     o_st[pl.ds(pl.multiple_of(tile * rows, rows), rows), :]
+
+        @pl.when((q_idx >= 2) & (q_idx % 2 == 0))
+        def _():
+            o_round(q_idx // 2 - 1)
+
+        @pl.when((q_idx >= 3) & (q_idx % 2 == 1))
+        def _():
+            o_pass((q_idx - 3) // 2)
+
+        @pl.when(q_idx == 5)
+        def _():
+            wo_second()
+
         return carry
 
-    lax.fori_loop(0, 5, q_step, 0)
-    wo_second()
-    lax.fori_loop(5, 2 * chunk // TQ, q_step, 0)
-    wo_third()
-
-    def o_arrival(z_row, src):
-        dst = og.at[z_row, :, pl.ds(src * 2 * head, 2 * head)]
-        return pltpu.make_async_remote_copy(src_ref=o_st.at[pl.ds(0, rows)], dst_ref=dst, send_sem=o_send.at[0, 0],
-                                            recv_sem=o_recv.at[z_row, src], device_id={"tp": 0}, device_id_type=MESH)
+    lax.fori_loop(0, 2 * chunk // TQ, q_step, 0)
 
     def y_copy(z_dst, z_src):
         return pltpu.make_async_remote_copy(
             src_ref=yst.at[z_dst], dst_ref=yv.at[:, pl.ds(pl.multiple_of(z_src * cols, 128), cols)],
             send_sem=y_send.at[z_dst], recv_sem=y_recv.at[z_src], device_id={"tp": NY * z_dst + my_y}, device_id_type=MESH)
 
-    wo_last()
-    for half in range(2):
-        for z_row in (2 * half, 2 * half + 1):
-            for src in range(n_tp):
-                @pl.when(tp != src)
-                def _(z_row=z_row, src=src):
-                    o_arrival(z_row, src).wait_recv()
-        lhs = og[2 * half:2 * half + 2].reshape(2 * rows, n_tp * 2 * head)
+    def out_product(first, count):
+        for row in range(first, first + count):
+            o_far(row)
+        lhs = og[first:first + count].reshape(count * rows, n_tp * 2 * head)
         for col in range(0, cols, 384):
-            w_cols = wo_v[:, :, :, col:col + 384].reshape(n_tp * 2 * head, 384)
+            w_cols = jnp.concatenate([wo_v[NY * y_idx + z_idx, :, :, col:col + 384].reshape(2 * head, 384)
+                                      for z_idx in range(NY) for y_idx in range(NY)], axis=0)
             res = jnp.dot(lhs, w_cols, preferred_element_type=jnp.float32).astype(jnp.bfloat16)
-            yst[2 * half:2 * half + 2, :, col:col + 384] = res.reshape(2, rows, 384)
-        for z_dst in (2 * half, 2 * half + 1):
+            yst[first:first + count, :, col:col + 384] = res.reshape(count, rows, 384)
+        for z_dst in range(first, first + count):
             @pl.when(my_z != z_dst)
             def _(z_dst=z_dst):
                 y_copy(z_dst, my_z).start()
@@ -483,31 +566,44 @@
             def _(z_dst=z_dst):
                 yv[:, pl.ds(pl.multiple_of(my_z * cols, 128), cols)] = yst[z_dst]
 
+    o_round(NY - 1)
+    wo_third()
+    o_pass(NY - 1)
+    wo_last()
+    out_product(0, 2)
+    out_product(2, 1)
+    out_product(3, 1)
     for z_src in range(NY):
         @pl.when(my_z != z_src)
         def _(z_src=z_src):
             y_copy(z_src, z_src).wait_recv()
     y_out = pltpu.make_async_copy(yv, y_hbm, y_sem)
     y_out.start()
-    for tile in range(2 * n_tp // 2):
-        for z_dst in range(NY):
-            mine = (tile % NY == my_y) & (my_z == z_dst)
-
-            @pl.when(jnp.logical_not(mine))
-            def _(tile=tile, z_dst=z_dst):
-                o_copy(tile, z_dst).wait_send()
+    for tile in range(n_tp):
+        @pl.when(tile % NY != my_y)
+        def _(tile=tile):
+            oy_copy(tile, tp).wait_send()
+    for row in range(NY):
+        for side, z_src in ((0, zm), (1, zp)):
+            oz_copy(row, my_z, side).wait_send()
+            of_copy(row, z_src, side).wait_send()
     for z_dst in range(NY):
         @pl.when(my_z != z_dst)
         def _(z_dst=z_dst):
             y_copy(z_dst, my_z).wait_send()
-    for copy in sends + slabs:
+    for copy in sends + [slab_copy(*slab) for slab in slabs]:
         copy.wait_send()
-    for step in range(1, n_tp):
+    for step in range(1, NY):
         wo_copy(step).wait_send()
+    for copy in wy_sends:
+        copy.wait_send()
     for slot in range(3):
         share_copy(my_z, my_c, slot).wait_send()
+    for slot in range(2):
+        a_copy(0, my_z, 0, slot).wait_send()
+        far_copy(0, slot).wait_send()
         for kind in range(2):
-            a_copy(kind, my_z, 0, slot).wait_send()
+            pass_copy(kind, slot, my_z).wait_send()
     for z_idx in range(NY):
         kv_own(z_idx, done)
         kv_direct(z_idx, done, False)
@@ -539,7 +635,7 @@
                 pltpu.VMEM((seq_loc, two_head), bf16),
                 pltpu.VMEM((n_sp * seq_loc, two_head), bf16),
                 pltpu.VMEM((NY - 1, seq_loc // NY, two_head), bf16),
-                pltpu.VMEM((NY - 1, seq_loc // NY, two_head), bf16),
+                pltpu.VMEM((2, 2, seq_loc // (2 * NY), two_head), bf16),
                 pltpu.VMEM((n_tp, n_sp, wo_rows, cols), bf16),
                 pltpu.VMEM((2 * TQ, WINDOW + TQ), f32),
                 pltpu.VMEM((2 * TQ, head), f32),
@@ -550,9 +646,10 @@
                 pltpu.VMEM((NY, rows, n_tp * two_head), bf16),
                 pltpu.VMEM((NY, rows, cols), bf16),
                 pltpu.VMEM((rows, d_model), bf16),
-                dma, dma((3,)), dma((4,)), dma((NY, 2)), dma((24,)), dma((NY, NY + 1, 2)), dma((3,)), dma((NY,)), dma((2, 3)), dma((2, NY)),
-                dma((NY, 6)), dma((2 * n_sp, 2)), dma, dma((n_tp,)), dma((n_tp,)),
-                dma((16,)), dma((n_sp, 2)), dma((n_tp, NY)), dma((NY, n_tp)), dma((NY,)), dma((NY,)), dma,
+                dma, dma((3,)), dma((4,)), dma((NY, 2)), dma((24,)), dma((NY, NY + 1, 2)), dma((3,)), dma((NY,)), dma((2, 2)), dma((2, NY)),
+                dma((2, 2)), dma((2, 2)), dma((2, 2)), dma((2, 2)), dma((NY, 6)), dma((2 * n_sp, 2)), dma, dma((NY,)), dma((NY,)), dma((4,)),
+                dma((NY, 2)), dma((16,)), dma((n_sp, 2)), dma((n_tp,)), dma((NY, NY)), dma((NY, 2)), dma((NY, NY)), dma((NY, 2)), dma((NY, 2)),
+                dma((NY,)), dma((NY,)), dma,
             ],
             compiler_params=pltpu.CompilerParams(collective_id=1, has_side_effects=True, vmem_limit_bytes=67043328),
             name="layer",

time: 184 us -> 185 us (level)
  the two profiles are of different devices: /device:TPU:83 before, /device:TPU:99 now
where the time goes in v4:
time: 185 us
  Pallas kernels  179 us (97%)
  local copies, waits for them, and re-layouts  5.74 us (3%)
    pallas_call x1, Pallas kernels, local_attn(): pl.pallas_call(layer_kernel, out_shape=jax.ShapeDtypeStruct((rows, d_mode...  179 us
    unnamed x2, local copies, waits for them, and re-layouts  5.74 us

profile of v4, /device:TPU:99, one launch (start us, length us, event | category | flops | bytes accessed | tf_op | source)
XLA Modules:
  0.0 185.1 jit_solution(17537171363579806852)
XLA Ops:
  0.0 3.4 %copy.8 = bf16[576,8,2,128]{3,1,2,0:T(8,128)(2,1)} copy(bf16[576,8,2,128]{3,2,1,0:T(2,128)(2,1)} %bitcast.8) | data formatting | bytes 4718592
  3.4 179.4 %layer.1 = bf16[128,4608]{1,0:T(8,128)(2,1)} custom-call(bf16[128,4608]{1,0:T(8,128)(2,1)} %x_hbm.1, bf16[4608,256]{1,0:T(8,128)(2,1)} %bitcast.7, bf16[4608,128]{1,0:T(8,128)(2,1)} %bitcast.10, bf16[4608,128]{1,0:T(8,128)(2,1)} %bitcast.11, bf16[8,32,4608]{2,1,0:T(8,128)(2,1)} %bitcast.9), custom_call_target="tpu_custom_call" | custom-call | tf_op jit(solution)/shard_map/layer/pallas_call | solution.py:627
  182.8 2.4 %copy.10 = bf16[128,4608]{1,0:T(8,128)(2,1)} copy(bf16[128,4608]{1,0:T(8,128)(2,1)} %layer.1) | data formatting | bytes 2359296

commit v5 on v4

--- a/solution.py
+++ b/solution.py
@@ -38,8 +38,8 @@
     part = NY * rows
     coef = head ** -0.5 * LOG2E
     d_half = w_v.shape[1] // 2
-    s_rows = d_half // 6
-    d_rows = 2 * s_rows
+    s_rows = d_half // (6 * 32) * 32 - 32
+    d_rows = d_half - NY * s_rows
 
     x_load = pltpu.make_async_copy(x_hbm, xg.at[my_y], x_sem)
     x_load.start()
@@ -59,6 +59,7 @@
     zm, zp, zo = (my_z + 3) % NY, (my_z + 1) % NY, (my_z + 2) % NY
     ym, yp, yo = (my_y + 3) % NY, (my_y + 1) % NY, (my_y + 2) % NY
     x_left, x_right, x_far = (my_x + 3) % NY, (my_x + 1) % NY, (my_x + 2) % NY
+    partner = {"sp": 2 * my_x + 1 - my_c}
     sends = []
     n_sends = [0, 0]
 
@@ -79,7 +80,7 @@
     def w_copy(z_src, x_src, first, count, dst, slot):
         size = d_rows if x_src is None else s_rows
         base = my_c * d_half + (0 if x_src is None else d_rows + x_src * s_rows)
-        ref = w_v.at[z_src, pl.ds(pl.multiple_of(base + first * (size // 2), 64), count * (size // 2))]
+        ref = w_v.at[z_src, pl.ds(pl.multiple_of(base + first * (size // 2), 16), count * (size // 2))]
         return pltpu.make_async_remote_copy(src_ref=ref, dst_ref=ref, send_sem=w_send.at[slot],
                                             recv_sem=w_recv.at[z_src, NY if x_src is None else x_src, first], device_id=dst, device_id_type=MESH)
 
@@ -101,7 +102,7 @@
     def share_copy(z_src, core, slot):
         ref = w_v.at[z_src, pl.ds(pl.multiple_of(core * d_half, 64), d_half)]
         return pltpu.make_async_remote_copy(src_ref=ref, dst_ref=ref, send_sem=share_send.at[slot], recv_sem=share_recv.at[z_src],
-                                            device_id={"sp": 2 * my_x + 1 - my_c}, device_id_type=MESH)
+                                            device_id=partner, device_id_type=MESH)
 
     def blk_of(z_idx):
         return jnp.where(z_idx < NY // 2, sp, 2 * n_sp - 1 - sp)
@@ -139,9 +140,8 @@
 
         lax.fori_loop(0, 2, body, 0)
 
-    def a_start(z_dst, slot):
-        for kind in range(2):
-            a_copy(kind, my_z, z_dst, slot).start()
+    def a_start(kind, z_dst, slot):
+        a_copy(kind, my_z, z_dst, slot).start()
 
     def a_wait(kind, z_src):
         a_copy(kind, z_src, 0, 0).wait_recv()
@@ -173,8 +173,6 @@
         ref = kv_v.at[pl.ds(pl.multiple_of(blk * chunk + (z_idx % 2) * part, part), part)]
         return pltpu.make_async_remote_copy(src_ref=ref, dst_ref=ref, send_sem=kv_send.at[z_idx, kind], recv_sem=kv_recv.at[blk, z_idx % 2],
                                             device_id=dst, device_id_type=MESH)
-
-    partner = {"sp": 2 * my_x + 1 - my_c}
 
     def own_pair(z_idx):
         return jnp.where(z_idx < NY // 2, my_x, 2 * NY - 1 - my_x)
@@ -243,13 +241,16 @@
     def done(copy):
         copy.wait_send()
 
+    group = 2 * (my_x % 2) + my_c
+    x_group = 2 - 2 * (my_x % 2) + my_c
+
     def wo_copy(step):
         dst = (my_z + step) % NY
-        src_ref = wo_hbm.at[sp, :, pl.ds(pl.multiple_of(dst * cols, 128), cols)]
-        return pltpu.make_async_remote_copy(src_ref=src_ref, dst_ref=wo_v.at[NY * my_y + my_z, sp], send_sem=wo_send.at[step],
+        src_ref = wo_hbm.at[group, :, pl.ds(pl.multiple_of(dst * cols, 128), cols)]
+        return pltpu.make_async_remote_copy(src_ref=src_ref, dst_ref=wo_v.at[NY * my_y + my_z, group], send_sem=wo_send.at[step],
                                             recv_sem=wo_recv.at[my_z], device_id=to_z(dst), device_id_type=MESH)
 
-    wo_own = pltpu.make_async_copy(wo_hbm.at[sp, :, pl.ds(pl.multiple_of(my_z * cols, 128), cols)], wo_v.at[NY * my_y + my_z, sp], wo_sem)
+    wo_own = pltpu.make_async_copy(wo_hbm.at[group, :, pl.ds(pl.multiple_of(my_z * cols, 128), cols)], wo_v.at[NY * my_y + my_z, group], wo_sem)
 
     def wo_z_start():
         wo_own.start()
@@ -257,7 +258,7 @@
             wo_copy(step).start()
 
     def wy_copy(y_src, first, count, y_dst, slot):
-        ref = wo_v.at[pl.ds(NY * y_src + 2 * first, 2 * count), sp]
+        ref = wo_v.at[pl.ds(NY * y_src + 2 * first, 2 * count), group]
         return pltpu.make_async_remote_copy(src_ref=ref, dst_ref=ref, send_sem=wy_send.at[slot], recv_sem=wy_recv.at[y_src, first],
                                             device_id={"tp": NY * my_z + y_dst}, device_id_type=MESH)
 
@@ -266,7 +267,7 @@
     def wo_y_start():
         wo_own.wait()
         for z_src in (zm, zp, zo):
-            ref = wo_v.at[NY * my_y + z_src, sp]
+            ref = wo_v.at[NY * my_y + z_src, group]
             pltpu.make_async_remote_copy(src_ref=ref, dst_ref=ref, send_sem=wo_send.at[1], recv_sem=wo_recv.at[z_src],
                                          device_id=to_z(z_src), device_id_type=MESH).wait_recv()
         for copy in wy_sends[:2]:
@@ -277,45 +278,28 @@
             wy_copy(y_src, 0, 2, 0, 0).wait_recv()
             copy.start()
 
-    slabs = []
-    other_c = 1 - my_c
-
-    def slab_copy(x_src, c_src, first, count, x_dst, c_dst, slot):
-        ref = wo_v.at[pl.ds(first * (n_tp // 2), count * (n_tp // 2)), 2 * x_src + c_src]
-        return pltpu.make_async_remote_copy(src_ref=ref, dst_ref=ref, send_sem=sl_send.at[slot], recv_sem=sl_recv.at[2 * x_src + c_src, first],
-                                            device_id={"sp": 2 * x_dst + c_dst}, device_id_type=MESH)
-
-    def slab_put(x_src, first, count, x_dst, c_dst):
-        slabs.append((x_src, my_c, first, count, x_dst, c_dst, len(slabs)))
-        slab_copy(*slabs[-1]).start()
-
-    def slab_wait(x_src, c_src, first, count):
-        slab_copy(x_src, c_src, first, count, 0, 0, 0).wait_recv()
+    def slab_copy(grp, first, count, dst, slot):
+        ref = wo_v.at[pl.ds(first * (n_tp // 2), count * (n_tp // 2)), grp]
+        return pltpu.make_async_remote_copy(src_ref=ref, dst_ref=ref, send_sem=sl_send.at[slot], recv_sem=sl_recv.at[grp, first],
+                                            device_id=dst, device_id_type=MESH)
+
+    slabs = (slab_copy(group, 0, 1, to_x(x_right), 0), slab_copy(group, 1, 1, to_x(x_left), 1), slab_copy(group, 0, 2, partner, 2),
+             slab_copy(x_group, 0, 2, partner, 3))
 
     def wo_first():
         for first in range(2):
             wy_copy(yo, first, 1, 0, 0).wait_recv()
-        for x_dst in (x_right, x_left):
-            slab_put(my_x, 0, 2, x_dst, my_c)
-        slab_put(my_x, 0, 2, my_x, other_c)
+        for copy in slabs[:3]:
+            copy.start()
 
     def wo_second():
-        for x_src, first, x_dst in ((x_left, 0, x_right), (x_right, 1, x_left)):
-            slab_wait(x_src, my_c, 0, 2)
-            slab_put(x_src, first, 1, x_dst, my_c)
-        for x_src in (x_left, x_right):
-            slab_put(x_src, 0, 2, my_x, other_c)
-
-    def wo_third():
         for first in range(2):
-            slab_wait(x_far, my_c, first, 1)
-            slab_put(x_far, first, 1, my_x, other_c)
+            slab_copy(x_group, first, 1, partner, 3).wait_recv()
+        slabs[3].start()
 
     def wo_last():
-        for x_src in (my_x, x_left, x_right):
-            slab_wait(x_src, other_c, 0, 2)
-        for first in range(2):
-            slab_wait(x_far, other_c, first, 1)
+        for grp in (2 * (my_x % 2), 2 - 2 * (my_x % 2)):
+            slab_copy(grp + 1 - my_c, 0, 2, partner, 3).wait_recv()
 
     x_load.wait()
     x_put(my_y, 0, 2, yp)
@@ -363,21 +347,24 @@
     for slot, z_dst in enumerate((zm, zp)):
         share_copy(z_dst, 1 - my_c, slot).wait_recv()
         products(z_dst, slot)
-        a_start(z_dst, slot)
+        a_start(0, z_dst, slot)
     for first in range(2):
         w_wait(zo, None, first, 1)
         w_wait(zo, x_far, first, 1)
     share_copy(zo, my_c, 2).start()
     share_copy(zo, 1 - my_c, 2).wait_recv()
     products(zo, 2)
-    for kind in range(2):
-        for half in range(2):
-            far_copy(kind, half).start()
+    for half in range(2):
+        far_copy(0, half).start()
+    for slot, z_dst in enumerate((zm, zp)):
+        a_start(1, z_dst, slot)
     kv_direct(my_z, start, True)
     for z_src in (zm, zp):
         a_wait(0, z_src)
         kv_own(z_src, start)
     far_pass(0)
+    for half in range(2):
+        far_copy(1, half).start()
     kv_relay(my_z, start, True)
     wo_y_pass()
     for z_src in (zm, zp):
@@ -452,23 +439,23 @@
             return kv_v[pl.ds(pl.multiple_of(tile * TQ, TQ), width), head:2 * head]
 
         per = wide // TQ
-        scores = jnp.where(col_i <= row_i, dot_nt(q_two, keys(gidx, TQ)), NEG_BIG)
+        scores = jnp.where(col_i <= row_i, dot_nt(q_two, keys(gidx, TQ)) * coef, NEG_BIG)
         s_v[:, 0:TQ] = scores
         best = lane_max(scores)
         if with_first:
-            scores = jnp.where(col_i > row_i, dot_nt(q_two, keys(gidx - WINDOW // TQ, TQ)), NEG_BIG)
+            scores = jnp.where(col_i > row_i, dot_nt(q_two, keys(gidx - WINDOW // TQ, TQ)) * coef, NEG_BIG)
             s_v[:, TQ:2 * TQ] = scores
             best = jnp.maximum(best, lane_max(scores))
         mx_v[...] = best
 
         def score_step(idx, carry):
-            part = dot_nt(q_two, keys(start_tile + per * idx, wide))
+            part = dot_nt(q_two, keys(start_tile + per * idx, wide)) * coef
             s_v[:, pl.ds(pl.multiple_of(2 * TQ + idx * wide, TQ), wide)] = part
             mx_v[...] = jnp.maximum(mx_v[...], lane_max(part))
             return carry
 
         lax.fori_loop(0, n_steps, score_step, 0)
-        row_best = jnp.max(mx_v[...], axis=1, keepdims=True) * coef
+        row_best = jnp.max(mx_v[...], axis=1, keepdims=True)
         mb_v[...] = jnp.broadcast_to(row_best, mb_v.shape)
 
         def probs(col, width):
@@ -476,7 +463,7 @@
             total = None
             parts = []
             for idx in range(width // head):
-                part = jnp.exp2(s_v[:, pl.ds(pl.multiple_of(col + idx * head, head), head)] * coef - base)
+                part = jnp.exp2(s_v[:, pl.ds(pl.multiple_of(col + idx * head, head), head)] - base)
                 total = part if total is None else total + part
                 parts.append(part.astype(jnp.bfloat16))
             return jnp.concatenate(parts, axis=1), total
@@ -535,7 +522,7 @@
         def _():
             o_pass((q_idx - 3) // 2)
 
-        @pl.when(q_idx == 5)
+        @pl.when(q_idx == 4)
         def _():
             wo_second()
 
@@ -567,10 +554,9 @@
                 yv[:, pl.ds(pl.multiple_of(my_z * cols, 128), cols)] = yst[z_dst]
 
     o_round(NY - 1)
-    wo_third()
-    o_pass(NY - 1)
     wo_last()
     out_product(0, 2)
+    o_pass(NY - 1)
     out_product(2, 1)
     out_product(3, 1)
     for z_src in range(NY):
@@ -591,7 +577,7 @@
         @pl.when(my_z != z_dst)
         def _(z_dst=z_dst):
             y_copy(z_dst, my_z).wait_send()
-    for copy in sends + [slab_copy(*slab) for slab in slabs]:
+    for copy in sends + list(slabs):
         copy.wait_send()
     for step in range(1, NY):
         wo_copy(step).wait_send()
@@ -623,7 +609,7 @@
         any_spec = pl.BlockSpec(memory_space=pl.ANY)
         dma = pltpu.SemaphoreType.DMA
         bf16, f32 = jnp.bfloat16, jnp.float32
-        wo_rows = w_out.shape[0] * w_out.shape[1] // n_sp
+        wo_rows = w_out.shape[0] * w_out.shape[1] // NY
         return pl.pallas_call(
             layer_kernel,
             out_shape=jax.ShapeDtypeStruct((rows, d_model), bf16),
@@ -636,7 +622,7 @@
                 pltpu.VMEM((n_sp * seq_loc, two_head), bf16),
                 pltpu.VMEM((NY - 1, seq_loc // NY, two_head), bf16),
                 pltpu.VMEM((2, 2, seq_loc // (2 * NY), two_head), bf16),
-                pltpu.VMEM((n_tp, n_sp, wo_rows, cols), bf16),
+                pltpu.VMEM((n_tp, NY, wo_rows, cols), bf16),
                 pltpu.VMEM((2 * TQ, WINDOW + TQ), f32),
                 pltpu.VMEM((2 * TQ, head), f32),
                 pltpu.VMEM((2 * TQ, head), f32),
@@ -654,6 +640,6 @@
             compiler_params=pltpu.CompilerParams(collective_id=1, has_side_effects=True, vmem_limit_bytes=67043328),
             name="layer",
         )(x_part, w_query.reshape(d_model, two_head), w_key.reshape(d_model, head), w_value.reshape(d_model, head),
-          w_out.reshape(n_sp, wo_rows, d_model))
+          w_out.reshape(NY, wo_rows, d_model))
 
     return jax.shard_map(local_attn, mesh=mesh, in_specs=(P(("dp", "sp", "tp"), None), P(None, "tp", None), P(None, "tp", None), P(None, "tp", None), P("tp", None, None)), out_specs=P(("dp", "sp", "tp"), None), check_vma=False)

time: 185 us -> 193 us (1.043)
  the two profiles are of different devices: /device:TPU:99 before, /device:TPU:113 now
where the time goes in v5:
time: 193 us
  Pallas kernels  187 us (97%)
  local copies, waits for them, and re-layouts  5.74 us (3%)
    pallas_call x1, Pallas kernels, local_attn(): pl.pallas_call(layer_kernel, out_shape=jax.ShapeDtypeStruct((rows, d_mode...  187 us
    unnamed x2, local copies, waits for them, and re-layouts  5.74 us

profile of v5, /device:TPU:113, one launch (start us, length us, event | category | flops | bytes accessed | tf_op | source)
XLA Modules:
  0.0 193.1 jit_solution(6043562558493236415)
XLA Ops:
  0.0 3.4 %copy.8 = bf16[576,8,2,128]{3,1,2,0:T(8,128)(2,1)} copy(bf16[576,8,2,128]{3,2,1,0:T(2,128)(2,1)} %bitcast.8) | data formatting | bytes 4718592
  3.4 187.3 %layer.1 = bf16[128,4608]{1,0:T(8,128)(2,1)} custom-call(bf16[128,4608]{1,0:T(8,128)(2,1)} %x_hbm.1, bf16[4608,256]{1,0:T(8,128)(2,1)} %bitcast.7, bf16[4608,128]{1,0:T(8,128)(2,1)} %bitcast.10, bf16[4608,128]{1,0:T(8,128)(2,1)} %bitcast.11, bf16[4,64,4608]{2,1,0:T(8,128)(2,1)} %bitcast.9), custom_call_target="tpu_custom_call" | custom-call | tf_op jit(solution)/shard_map/layer/pallas_call | solution.py:613
  190.7 2.4 %copy.10 = bf16[128,4608]{1,0:T(8,128)(2,1)} copy(bf16[128,4608]{1,0:T(8,128)(2,1)} %layer.1) | data formatting | bytes 2359296

commit v6 on v5

--- a/solution.py
+++ b/solution.py
@@ -21,7 +21,7 @@
     return lax.dot_general(lhs, rhs, (((1,), (1,)), ((), ())), preferred_element_type=jnp.float32)
 
 
-def layer_kernel(x_hbm, wq_hbm, wk_hbm, wv_hbm, wo_hbm, y_hbm, xg, w_v, q_v, kv_v, kv_st, far_st, wo_v, s_v, mx_v, mb_v, l_v, acc_v, o_st,
+def layer_kernel(x_hbm, wq_hbm, wk_hbm, wv_hbm, wo_hbm, y_hbm, xg, wq_v, wkv_v, q_v, kv_v, kv_st, far_st, wo_v, s_v, mx_v, mb_v, l_v, acc_v, o_st,
                  og, yst, yv, x_sem, wl_sem, x_send, x_recv, w_send, w_recv, share_send, share_recv, a_send, a_recv, far_send, far_recv,
                  pass_send, pass_recv, kv_send, kv_recv, wo_sem, wo_send, wo_recv, wy_send, wy_recv, sl_send, sl_recv, oy_send, oy_recv,
                  oz_send, oz_recv, of_send, of_recv, y_send, y_recv, y_sem):
@@ -37,15 +37,15 @@
     rows = yst.shape[1]
     part = NY * rows
     coef = head ** -0.5 * LOG2E
-    d_half = w_v.shape[1] // 2
+    d_half = wq_v.shape[1] // 2
     s_rows = d_half // (6 * 32) * 32 - 32
     d_rows = d_half - NY * s_rows
 
     x_load = pltpu.make_async_copy(x_hbm, xg.at[my_y], x_sem)
     x_load.start()
-    w_loads = (pltpu.make_async_copy(wq_hbm, w_v.at[my_z, :, 0:2 * head], wl_sem.at[0]),
-               pltpu.make_async_copy(wk_hbm, w_v.at[my_z, :, 2 * head:3 * head], wl_sem.at[1]),
-               pltpu.make_async_copy(wv_hbm, w_v.at[my_z, :, 3 * head:4 * head], wl_sem.at[2]))
+    w_loads = (pltpu.make_async_copy(wk_hbm, wkv_v.at[my_z, :, 0:head], wl_sem.at[0]),
+               pltpu.make_async_copy(wv_hbm, wkv_v.at[my_z, :, head:2 * head], wl_sem.at[1]),
+               pltpu.make_async_copy(wq_hbm, wq_v.at[my_z], wl_sem.at[2]))
     for load in w_loads:
         load.start()
 
@@ -77,21 +77,21 @@
     def x_wait(y_src, first, count):
         x_copy(y_src, first, count, 0, 0).wait_recv()
 
-    def w_copy(z_src, x_src, first, count, dst, slot):
+    def w_copy(kind, z_src, x_src, first, count, dst, slot):
         size = d_rows if x_src is None else s_rows
         base = my_c * d_half + (0 if x_src is None else d_rows + x_src * s_rows)
-        ref = w_v.at[z_src, pl.ds(pl.multiple_of(base + first * (size // 2), 16), count * (size // 2))]
+        ref = (wq_v if kind else wkv_v).at[z_src, pl.ds(pl.multiple_of(base + first * (size // 2), 16), count * (size // 2))]
         return pltpu.make_async_remote_copy(src_ref=ref, dst_ref=ref, send_sem=w_send.at[slot],
-                                            recv_sem=w_recv.at[z_src, NY if x_src is None else x_src, first], device_id=dst, device_id_type=MESH)
-
-    def w_put(z_src, x_src, first, count, dst):
-        copy = w_copy(z_src, x_src, first, count, dst, n_sends[1])
+                                            recv_sem=w_recv.at[kind, z_src, NY if x_src is None else x_src, first], device_id=dst, device_id_type=MESH)
+
+    def w_put(kind, z_src, x_src, first, count, dst):
+        copy = w_copy(kind, z_src, x_src, first, count, dst, n_sends[1])
         n_sends[1] += 1
         sends.append(copy)
         copy.start()
 
-    def w_wait(z_src, x_src, first, count):
-        w_copy(z_src, x_src, first, count, {"tp": 0}, 0).wait_recv()
+    def w_wait(kind, z_src, x_src, first, count):
+        w_copy(kind, z_src, x_src, first, count, {"tp": 0}, 0).wait_recv()
 
     def to_z(z_dst):
         return {"tp": NY * z_dst + my_y}
@@ -99,9 +99,9 @@
     def to_x(x_dst):
         return {"sp": 2 * x_dst + my_c}
 
-    def share_copy(z_src, core, slot):
-        ref = w_v.at[z_src, pl.ds(pl.multiple_of(core * d_half, 64), d_half)]
-        return pltpu.make_async_remote_copy(src_ref=ref, dst_ref=ref, send_sem=share_send.at[slot], recv_sem=share_recv.at[z_src],
+    def share_copy(kind, z_src, core, slot):
+        ref = (wq_v if kind else wkv_v).at[z_src, pl.ds(pl.multiple_of(core * d_half, 64), d_half)]
+        return pltpu.make_async_remote_copy(src_ref=ref, dst_ref=ref, send_sem=share_send.at[kind, slot], recv_sem=share_recv.at[kind, z_src],
                                             device_id=partner, device_id_type=MESH)
 
     def blk_of(z_idx):
@@ -115,9 +115,10 @@
             y_idx = y_list[0]
             for other in range(1, len(y_list)):
                 y_idx = jnp.where(idx == other, y_list[other], y_idx)
-            prod = jnp.dot(xg[y_idx], w_v[my_z], preferred_element_type=jnp.float32).astype(jnp.bfloat16)
-            q_v[pl.ds(pl.multiple_of(my_z * part + y_idx * rows, rows), rows), :] = prod[:, :2 * head]
-            kv_v[pl.ds(pl.multiple_of(kv_rows(my_z) + y_idx * rows, rows), rows), :] = prod[:, 2 * head:]
+            prod = jnp.dot(xg[y_idx], wkv_v[my_z], preferred_element_type=jnp.float32).astype(jnp.bfloat16)
+            kv_v[pl.ds(pl.multiple_of(kv_rows(my_z) + y_idx * rows, rows), rows), :] = prod
+            prod = jnp.dot(xg[y_idx], wq_v[my_z], preferred_element_type=jnp.float32).astype(jnp.bfloat16)
+            q_v[pl.ds(pl.multiple_of(my_z * part + y_idx * rows, rows), rows), :] = prod
             return carry
 
         lax.fori_loop(0, len(y_list), body, 0)
@@ -130,12 +131,14 @@
         return pltpu.make_async_remote_copy(src_ref=src, dst_ref=dst, send_sem=a_send.at[kind, slot], recv_sem=a_recv.at[kind, z_src],
                                             device_id=to_z(z_dst), device_id_type=MESH)
 
-    def products(z_dst, slot):
+    def products(kind, z_dst, slot):
         def body(idx, carry):
             lhs = xg[pl.ds(2 * idx, 2)].reshape(2 * rows, xg.shape[2])
-            prod = jnp.dot(lhs, w_v[z_dst], preferred_element_type=jnp.float32).astype(jnp.bfloat16)
-            o_st[pl.ds(pl.multiple_of(slot * part + idx * 2 * rows, 2 * rows), 2 * rows), :] = prod[:, :2 * head]
-            kv_st[slot, pl.ds(pl.multiple_of(idx * 2 * rows, 2 * rows), 2 * rows), :] = prod[:, 2 * head:]
+            prod = jnp.dot(lhs, (wq_v if kind else wkv_v)[z_dst], preferred_element_type=jnp.float32).astype(jnp.bfloat16)
+            if kind:
+                o_st[pl.ds(pl.multiple_of(slot * part + idx * 2 * rows, 2 * rows), 2 * rows), :] = prod
+            else:
+                kv_st[slot, pl.ds(pl.multiple_of(idx * 2 * rows, 2 * rows), 2 * rows), :] = prod
             return carry
 
         lax.fori_loop(0, 2, body, 0)
@@ -301,79 +304,118 @@
         for grp in (2 * (my_x % 2), 2 - 2 * (my_x % 2)):
             slab_copy(grp + 1 - my_c, 0, 2, partner, 3).wait_recv()
 
+    def w_own_slice(kind):
+        for z_dst in (zp, zm):
+            w_put(kind, my_z, my_x, 0, 2, to_z(z_dst))
+
+    def w_slices(kind):
+        for z_src, first, z_dst in ((zm, 0, zp), (zp, 1, zm)):
+            w_wait(kind, z_src, my_x, 0, 2)
+            w_put(kind, z_src, my_x, first, 1, to_z(z_dst))
+            for x_dst in (x_right, x_left):
+                w_put(kind, z_src, my_x, 0, 2, to_x(x_dst))
+
+    def w_own_rest(kind):
+        for z_dst in (zp, zm):
+            w_put(kind, my_z, None, 0, 2, to_z(z_dst))
+
+    def w_far_slice(kind):
+        for first in range(2):
+            w_wait(kind, zo, my_x, first, 1)
+        for x_dst in (x_right, x_left):
+            w_put(kind, zo, my_x, 0, 2, to_x(x_dst))
+
+    def w_ring(kind, z_src):
+        for x_src, first, x_dst in ((x_left, 0, x_right), (x_right, 1, x_left)):
+            w_wait(kind, z_src, x_src, 0, 2)
+            w_put(kind, z_src, x_src, first, 1, to_x(x_dst))
+
+    def w_rest(kind):
+        for z_src, first, z_dst in ((zm, 0, zp), (zp, 1, zm)):
+            w_wait(kind, z_src, None, 0, 2)
+            w_put(kind, z_src, None, first, 1, to_z(z_dst))
+
+    def w_share(kind, z_src, slot):
+        for first in range(2):
+            w_wait(kind, z_src, x_far, first, 1)
+            if slot == 2:
+                w_wait(kind, z_src, None, first, 1)
+        share_copy(kind, z_src, my_c, slot).start()
+
+    def w_full(kind, z_src, slot):
+        share_copy(kind, z_src, 1 - my_c, slot).wait_recv()
+
     x_load.wait()
     x_put(my_y, 0, 2, yp)
     x_put(my_y, 0, 2, ym)
-    for load in w_loads:
+    for load in w_loads[:2]:
         load.wait()
-    for z_dst in (zp, zm):
-        w_put(my_z, my_x, 0, 2, to_z(z_dst))
-    for z_src, first, z_dst in ((zm, 0, zp), (zp, 1, zm)):
-        w_wait(z_src, my_x, 0, 2)
-        w_put(z_src, my_x, first, 1, to_z(z_dst))
-        for x_dst in (x_right, x_left):
-            w_put(z_src, my_x, 0, 2, to_x(x_dst))
-    for z_dst in (zp, zm):
-        w_put(my_z, None, 0, 2, to_z(z_dst))
-    wo_z_start()
+    w_own_slice(0)
+    w_slices(0)
+    w_own_rest(0)
+    w_loads[2].wait()
+    w_own_slice(1)
+    w_far_slice(0)
     own_products([my_y])
-    for z_src in (zm, zp):
-        for x_src, first, x_dst in ((x_left, 0, x_right), (x_right, 1, x_left)):
-            w_wait(z_src, x_src, 0, 2)
-            w_put(z_src, x_src, first, 1, to_x(x_dst))
-    for first in range(2):
-        w_wait(zo, my_x, first, 1)
-    for x_dst in (x_right, x_left):
-        w_put(zo, my_x, 0, 2, to_x(x_dst))
+    w_ring(0, zm)
+    w_ring(0, zp)
+    w_rest(0)
+    w_ring(0, zo)
+    w_slices(1)
+    w_own_rest(1)
+    w_share(0, zm, 0)
+    w_share(0, zp, 1)
     for y_src, first, y_dst in ((ym, 0, yp), (yp, 1, ym)):
         x_wait(y_src, 0, 2)
         x_put(y_src, first, 1, y_dst)
-    for z_src, first, z_dst in ((zm, 0, zp), (zp, 1, zm)):
-        w_wait(z_src, None, 0, 2)
-        w_put(z_src, None, first, 1, to_z(z_dst))
+    w_share(0, zo, 2)
+    w_far_slice(1)
     own_products([ym, yp])
-    for slot, z_src in enumerate((zm, zp)):
-        for first in range(2):
-            w_wait(z_src, x_far, first, 1)
-        share_copy(z_src, my_c, slot).start()
-    for x_src, first, x_dst in ((x_left, 0, x_right), (x_right, 1, x_left)):
-        w_wait(zo, x_src, 0, 2)
-        w_put(zo, x_src, first, 1, to_x(x_dst))
+    w_ring(1, zm)
+    w_ring(1, zp)
+    w_rest(1)
+    wo_z_start()
+    w_ring(1, zo)
     for first in range(2):
         x_wait(yo, first, 1)
-    wo_y_start()
     own_products([yo])
     kv_own(my_z, start)
     for slot, z_dst in enumerate((zm, zp)):
-        share_copy(z_dst, 1 - my_c, slot).wait_recv()
-        products(z_dst, slot)
+        w_full(0, z_dst, slot)
+        products(0, z_dst, slot)
         a_start(0, z_dst, slot)
-    for first in range(2):
-        w_wait(zo, None, first, 1)
-        w_wait(zo, x_far, first, 1)
-    share_copy(zo, my_c, 2).start()
-    share_copy(zo, 1 - my_c, 2).wait_recv()
-    products(zo, 2)
+    w_full(0, zo, 2)
+    products(0, zo, 2)
     for half in range(2):
         far_copy(0, half).start()
-    for slot, z_dst in enumerate((zm, zp)):
-        a_start(1, z_dst, slot)
+    w_share(1, zm, 0)
+    w_share(1, zp, 1)
+    w_share(1, zo, 2)
+    wo_y_start()
     kv_direct(my_z, start, True)
     for z_src in (zm, zp):
         a_wait(0, z_src)
         kv_own(z_src, start)
+    w_full(1, zm, 0)
+    products(1, zm, 0)
     far_pass(0)
+    a_start(1, zm, 0)
+    kv_relay(my_z, start, True)
+    w_full(1, zp, 1)
+    products(1, zp, 1)
+    a_start(1, zp, 1)
+    for z_src in (zm, zp):
+        kv_direct(z_src, start, True)
+    w_full(1, zo, 2)
+    products(1, zo, 2)
     for half in range(2):
         far_copy(1, half).start()
-    kv_relay(my_z, start, True)
+    far_wait(0)
+    kv_own(zo, start)
     wo_y_pass()
     for z_src in (zm, zp):
-        kv_direct(z_src, start, True)
-    far_wait(0)
-    kv_own(zo, start)
+        kv_relay(z_src, start, True)
     far_pass(1)
-    for z_src in (zm, zp):
-        kv_relay(z_src, start, True)
     kv_direct(zo, start, True)
     kv_relay(zo, start, True)
     wo_first()
@@ -489,47 +531,6 @@
         out = jnp.concatenate([out[:TQ], out[TQ:]], axis=1)
         o_st[pl.ds(pl.multiple_of(q_idx * TQ, TQ), TQ), :] = out
 
-    def q_step(q_idx, carry):
-        tiles = chunk // TQ
-        blk = jnp.where(q_idx < tiles, sp, 2 * n_sp - 1 - sp)
-        gidx = blk * tiles + q_idx % tiles
-
-        @pl.when(gidx >= WINDOW // TQ)
-        def _():
-            attend(q_idx, gidx, WIDE, gidx - WINDOW // TQ + 1, N_WIDE, True)
-
-        @pl.when(gidx < WINDOW // TQ)
-        def _():
-            attend(q_idx, gidx, TQ, 0, gidx, False)
-
-        for sub in range(2):
-            tile = 2 * q_idx + sub
-
-            @pl.when(tile % NY != my_y)
-            def _(tile=tile):
-                oy_copy(tile, tp).start()
-
-            @pl.when(tile % NY == my_y)
-            def _(tile=tile):
-                og[tile // NY, :, pl.ds(pl.multiple_of(tp * 2 * head, 2 * head), 2 * head)] = \
-                    o_st[pl.ds(pl.multiple_of(tile * rows, rows), rows), :]
-
-        @pl.when((q_idx >= 2) & (q_idx % 2 == 0))
-        def _():
-            o_round(q_idx // 2 - 1)
-
-        @pl.when((q_idx >= 3) & (q_idx % 2 == 1))
-        def _():
-            o_pass((q_idx - 3) // 2)
-
-        @pl.when(q_idx == 4)
-        def _():
-            wo_second()
-
-        return carry
-
-    lax.fori_loop(0, 2 * chunk // TQ, q_step, 0)
-
     def y_copy(z_dst, z_src):
         return pltpu.make_async_remote_copy(
             src_ref=yst.at[z_dst], dst_ref=yv.at[:, pl.ds(pl.multiple_of(z_src * cols, 128), cols)],
@@ -544,6 +545,8 @@
                                       for z_idx in range(NY) for y_idx in range(NY)], axis=0)
             res = jnp.dot(lhs, w_cols, preferred_element_type=jnp.float32).astype(jnp.bfloat16)
             yst[first:first + count, :, col:col + 384] = res.reshape(count, rows, 384)
+
+    def y_put(first, count):
         for z_dst in range(first, first + count):
             @pl.when(my_z != z_dst)
             def _(z_dst=z_dst):
@@ -553,12 +556,59 @@
             def _(z_dst=z_dst):
                 yv[:, pl.ds(pl.multiple_of(my_z * cols, 128), cols)] = yst[z_dst]
 
+    def q_step(q_idx, carry):
+        tiles = chunk // TQ
+        blk = jnp.where(q_idx < tiles, sp, 2 * n_sp - 1 - sp)
+        gidx = blk * tiles + q_idx % tiles
+
+        @pl.when(gidx >= WINDOW // TQ)
+        def _():
+            attend(q_idx, gidx, WIDE, gidx - WINDOW // TQ + 1, N_WIDE, True)
+
+        @pl.when(gidx < WINDOW // TQ)
+        def _():
+            attend(q_idx, gidx, TQ, 0, gidx, False)
+
+        for sub in range(2):
+            tile = 2 * q_idx + sub
+
+            @pl.when(tile % NY != my_y)
+            def _(tile=tile):
+                oy_copy(tile, tp).start()
+
+            @pl.when(tile % NY == my_y)
+            def _(tile=tile):
+                og[tile // NY, :, pl.ds(pl.multiple_of(tp * 2 * head, 2 * head), 2 * head)] = \
+                    o_st[pl.ds(pl.multiple_of(tile * rows, rows), rows), :]
+
+        @pl.when((q_idx >= 2) & (q_idx % 2 == 0))
+        def _():
+            o_round(q_idx // 2 - 1)
+
+        @pl.when((q_idx >= 3) & (q_idx % 2 == 1))
+        def _():
+            o_pass((q_idx - 3) // 2)
+
+        @pl.when(q_idx == 4)
+        def _():
+            wo_second()
+
+        @pl.when(q_idx == 6)
+        def _():
+            wo_last()
+            out_product(0, 2)
+            y_put(0, 2)
+
+        return carry
+
+    lax.fori_loop(0, 2 * chunk // TQ, q_step, 0)
+
     o_round(NY - 1)
-    wo_last()
-    out_product(0, 2)
+    out_product(2, 1)
     o_pass(NY - 1)
-    out_product(2, 1)
+    y_put(2, 1)
     out_product(3, 1)
+    y_put(3, 1)
     for z_src in range(NY):
         @pl.when(my_z != z_src)
         def _(z_src=z_src):
@@ -584,7 +634,8 @@
     for copy in wy_sends:
         copy.wait_send()
     for slot in range(3):
-        share_copy(my_z, my_c, slot).wait_send()
+        for kind in range(2):
+            share_copy(kind, my_z, my_c, slot).wait_send()
     for slot in range(2):
         a_copy(0, my_z, 0, slot).wait_send()
         far_copy(0, slot).wait_send()
@@ -617,7 +668,8 @@
             out_specs=any_spec,
             scratch_shapes=[
                 pltpu.VMEM((NY, rows, d_model), bf16),
-                pltpu.VMEM((NY, d_model, 2 * two_head), bf16),
+                pltpu.VMEM((NY, d_model, two_head), bf16),
+                pltpu.VMEM((NY, d_model, two_head), bf16),
                 pltpu.VMEM((seq_loc, two_head), bf16),
                 pltpu.VMEM((n_sp * seq_loc, two_head), bf16),
                 pltpu.VMEM((NY - 1, seq_loc // NY, two_head), bf16),
@@ -632,7 +684,7 @@
                 pltpu.VMEM((NY, rows, n_tp * two_head), bf16),
                 pltpu.VMEM((NY, rows, cols), bf16),
                 pltpu.VMEM((rows, d_model), bf16),
-                dma, dma((3,)), dma((4,)), dma((NY, 2)), dma((24,)), dma((NY, NY + 1, 2)), dma((3,)), dma((NY,)), dma((2, 2)), dma((2, NY)),
+                dma, dma((3,)), dma((4,)), dma((NY, 2)), dma((40,)), dma((2, NY, NY + 1, 2)), dma((2, 3)), dma((2, NY)), dma((2, 2)), dma((2, NY)),
                 dma((2, 2)), dma((2, 2)), dma((2, 2)), dma((2, 2)), dma((NY, 6)), dma((2 * n_sp, 2)), dma, dma((NY,)), dma((NY,)), dma((4,)),
                 dma((NY, 2)), dma((16,)), dma((n_sp, 2)), dma((n_tp,)), dma((NY, NY)), dma((NY, 2)), dma((NY, NY)), dma((NY, 2)), dma((NY, 2)),
                 dma((NY,)), dma((NY,)), dma,

time: 193 us -> 191 us (0.990)
  the two profiles are of different devices: /device:TPU:113 before, /device:TPU:102 now
where the time goes in v6:
time: 191 us
  Pallas kernels  185 us (97%)
  local copies, waits for them, and re-layouts  5.74 us (3%)
    pallas_call x1, Pallas kernels, local_attn(): pl.pallas_call(layer_kernel, out_shape=jax.ShapeDtypeStruct((rows, d_mode...  185 us
    unnamed x2, local copies, waits for them, and re-layouts  5.74 us

profile of v6, /device:TPU:102, one launch (start us, length us, event | category | flops | bytes accessed | tf_op | source)
XLA Modules:
  0.0 190.6 jit_solution(7842730832992280382)
XLA Ops:
  0.0 3.4 %copy.8 = bf16[576,8,2,128]{3,1,2,0:T(8,128)(2,1)} copy(bf16[576,8,2,128]{3,2,1,0:T(2,128)(2,1)} %bitcast.8) | data formatting | bytes 4718592
  3.4 184.8 %layer.1 = bf16[128,4608]{1,0:T(8,128)(2,1)} custom-call(bf16[128,4608]{1,0:T(8,128)(2,1)} %x_hbm.1, bf16[4608,256]{1,0:T(8,128)(2,1)} %bitcast.7, bf16[4608,128]{1,0:T(8,128)(2,1)} %bitcast.10, bf16[4608,128]{1,0:T(8,128)(2,1)} %bitcast.11, bf16[4,64,4608]{2,1,0:T(8,128)(2,1)} %bitcast.9), custom_call_target="tpu_custom_call" | custom-call | tf_op jit(solution)/shard_map/layer/pallas_call | solution.py:664
  188.2 2.4 %copy.10 = bf16[128,4608]{1,0:T(8,128)(2,1)} copy(bf16[128,4608]{1,0:T(8,128)(2,1)} %layer.1) | data formatting | bytes 2359296

commit v7 on v6

--- a/solution.py
+++ b/solution.py
@@ -21,10 +21,10 @@
     return lax.dot_general(lhs, rhs, (((1,), (1,)), ((), ())), preferred_element_type=jnp.float32)
 
 
-def layer_kernel(x_hbm, wq_hbm, wk_hbm, wv_hbm, wo_hbm, y_hbm, xg, wq_v, wkv_v, q_v, kv_v, kv_st, far_st, wo_v, s_v, mx_v, mb_v, l_v, acc_v, o_st,
-                 og, yst, yv, x_sem, wl_sem, x_send, x_recv, w_send, w_recv, share_send, share_recv, a_send, a_recv, far_send, far_recv,
-                 pass_send, pass_recv, kv_send, kv_recv, wo_sem, wo_send, wo_recv, wy_send, wy_recv, sl_send, sl_recv, oy_send, oy_recv,
-                 oz_send, oz_recv, of_send, of_recv, y_send, y_recv, y_sem):
+def layer_kernel(x_hbm, wq_hbm, wk_hbm, wv_hbm, wo_hbm, y_hbm, xg, wq_v, wkv_v, q_v, kv_v, kv_st, wo_v, s_v, mx_v, mb_v, l_v, acc_v, o_st,
+                 og, yst, yv, x_sem, wl_sem, x_send, x_recv, w_send, w_recv, share_send, share_recv, a_send, a_recv,
+                 kv_send, kv_recv, wo_sem, wo_send, wo_recv, wy_send, wy_recv, sl_send, sl_recv, o_send, o_recv,
+                 y_send, y_recv, y_sem):
     sp = lax.axis_index("sp")
     tp = lax.axis_index("tp")
     my_z, my_y = tp // NY, tp % NY
@@ -149,28 +149,6 @@
     def a_wait(kind, z_src):
         a_copy(kind, z_src, 0, 0).wait_recv()
 
-    half_rows = part // 2
-
-    def far_copy(kind, half):
-        src = o_st.at[pl.ds(2 * part + half * half_rows, half_rows)] if kind else kv_st.at[2, pl.ds(half * half_rows, half_rows)]
-        return pltpu.make_async_remote_copy(src_ref=src, dst_ref=far_st.at[kind, half], send_sem=far_send.at[kind, half],
-                                            recv_sem=far_recv.at[kind, half], device_id=to_z(zm if half else zp), device_id_type=MESH)
-
-    def pass_copy(kind, half, z_src):
-        at = (z_src * part if kind else kv_rows(z_src)) + half * half_rows
-        dst = (q_v if kind else kv_v).at[pl.ds(pl.multiple_of(at, half_rows), half_rows)]
-        return pltpu.make_async_remote_copy(src_ref=far_st.at[kind, half], dst_ref=dst, send_sem=pass_send.at[kind, half],
-                                            recv_sem=pass_recv.at[kind, half], device_id=to_z(zm if half else zp), device_id_type=MESH)
-
-    def far_pass(kind):
-        for half in range(2):
-            far_copy(kind, half).wait_recv()
-            pass_copy(kind, half, zp if half else zm).start()
-
-    def far_wait(kind):
-        for half in range(2):
-            pass_copy(kind, half, zo).wait_recv()
-
     def kv_part(pair, core, z_idx, kind, dst):
         blk = jnp.where(pair < NY, 2 * pair + core, 2 * pair + 1 - core)
         ref = kv_v.at[pl.ds(pl.multiple_of(blk * chunk + (z_idx % 2) * part, part), part)]
@@ -353,6 +331,7 @@
     w_own_slice(0)
     w_slices(0)
     w_own_rest(0)
+    wo_z_start()
     w_loads[2].wait()
     w_own_slice(1)
     w_far_slice(0)
@@ -363,68 +342,48 @@
     w_ring(0, zo)
     w_slices(1)
     w_own_rest(1)
-    w_share(0, zm, 0)
-    w_share(0, zp, 1)
     for y_src, first, y_dst in ((ym, 0, yp), (yp, 1, ym)):
         x_wait(y_src, 0, 2)
         x_put(y_src, first, 1, y_dst)
-    w_share(0, zo, 2)
+    w_share(0, zm, 0)
+    w_share(0, zp, 1)
     w_far_slice(1)
     own_products([ym, yp])
+    w_share(0, zo, 2)
     w_ring(1, zm)
     w_ring(1, zp)
-    w_rest(1)
-    wo_z_start()
-    w_ring(1, zo)
     for first in range(2):
         x_wait(yo, first, 1)
     own_products([yo])
     kv_own(my_z, start)
-    for slot, z_dst in enumerate((zm, zp)):
+    for slot, z_dst in enumerate((zo, zm, zp)):
         w_full(0, z_dst, slot)
         products(0, z_dst, slot)
         a_start(0, z_dst, slot)
-    w_full(0, zo, 2)
-    products(0, zo, 2)
-    for half in range(2):
-        far_copy(0, half).start()
-    w_share(1, zm, 0)
-    w_share(1, zp, 1)
-    w_share(1, zo, 2)
+    w_rest(1)
+    w_ring(1, zo)
     wo_y_start()
     kv_direct(my_z, start, True)
-    for z_src in (zm, zp):
+    for z_src in (zo, zm, zp):
         a_wait(0, z_src)
         kv_own(z_src, start)
-    w_full(1, zm, 0)
-    products(1, zm, 0)
-    far_pass(0)
-    a_start(1, zm, 0)
+    for slot, z_src in enumerate((zm, zp, zo)):
+        w_share(1, z_src, slot)
     kv_relay(my_z, start, True)
-    w_full(1, zp, 1)
-    products(1, zp, 1)
-    a_start(1, zp, 1)
-    for z_src in (zm, zp):
-        kv_direct(z_src, start, True)
-    w_full(1, zo, 2)
-    products(1, zo, 2)
-    for half in range(2):
-        far_copy(1, half).start()
-    far_wait(0)
-    kv_own(zo, start)
-    wo_y_pass()
-    for z_src in (zm, zp):
+    for slot, z_dst in enumerate((zo, zm, zp)):
+        w_full(1, z_dst, slot)
+        products(1, z_dst, slot)
+        a_start(1, z_dst, slot)
+        kv_direct(z_dst, start, True)
+        if slot == 0:
+            wo_y_pass()
+    for z_src in (zo, zm, zp):
         kv_relay(z_src, start, True)
-    far_pass(1)
-    kv_direct(zo, start, True)
-    kv_relay(zo, start, True)
     wo_first()
-    for z_src in (zm, zp):
+    for z_src in (zm, zp, zo):
         a_wait(1, z_src)
-    far_wait(1)
-    for slot in range(2):
+    for slot in range(3):
         a_copy(1, my_z, 0, slot).wait_send()
-        far_copy(1, slot).wait_send()
     for z_idx in range(NY):
         kv_from_partner(z_idx)
 
@@ -437,38 +396,17 @@
             best = jnp.maximum(best, scores[:, idx * head:(idx + 1) * head])
         return best
 
-    wide_o = NY * 2 * head
-
-    def oy_copy(tile, src_tp):
-        return pltpu.make_async_remote_copy(
-            src_ref=o_st.at[pl.ds(pl.multiple_of(tile * rows, rows), rows)],
-            dst_ref=og.at[tile // NY, :, pl.ds(pl.multiple_of(src_tp * 2 * head, 2 * head), 2 * head)],
-            send_sem=oy_send.at[tile], recv_sem=oy_recv.at[tile // NY, src_tp % NY], device_id={"tp": NY * my_z + tile % NY}, device_id_type=MESH)
-
-    def oz_copy(row, z_src, side):
-        ref = og.at[row, :, pl.ds(pl.multiple_of(z_src * wide_o, wide_o), wide_o)]
-        return pltpu.make_async_remote_copy(src_ref=ref, dst_ref=ref, send_sem=oz_send.at[row, side], recv_sem=oz_recv.at[row, z_src],
-                                            device_id=to_z(zm if side else zp), device_id_type=MESH)
-
-    def of_copy(row, z_src, side):
-        ref = og.at[row, pl.ds(side * (rows // 2), rows // 2), pl.ds(pl.multiple_of(z_src * wide_o, wide_o), wide_o)]
-        return pltpu.make_async_remote_copy(src_ref=ref, dst_ref=ref, send_sem=of_send.at[row, side], recv_sem=of_recv.at[row, side],
-                                            device_id=to_z(zm if side else zp), device_id_type=MESH)
-
-    def o_round(row):
-        for y_src in (ym, yp, yo):
-            oy_copy(NY * row + my_y, NY * my_z + y_src).wait_recv()
-        for side in range(2):
-            oz_copy(row, my_z, side).start()
-
-    def o_pass(row):
-        for side, z_src in ((0, zm), (1, zp)):
-            oz_copy(row, z_src, side).wait_recv()
-            of_copy(row, z_src, side).start()
-
-    def o_far(row):
-        for side in range(2):
-            of_copy(row, zo, side).wait_recv()
+    def o_copy(tile, z_dst):
+        y_dst, z_row = tile % NY, tile // NY
+        src = o_st.at[pl.ds(pl.multiple_of(tile * rows, rows), rows)]
+        dst = og.at[z_row, :, pl.ds(pl.multiple_of(tp * 2 * head, 2 * head), 2 * head)]
+        return pltpu.make_async_remote_copy(src_ref=src, dst_ref=dst, send_sem=o_send.at[tile, z_dst], recv_sem=o_recv.at[z_row, tp],
+                                            device_id={"tp": NY * z_dst + y_dst}, device_id_type=MESH)
+
+    def o_arrival(z_row, src):
+        dst = og.at[z_row, :, pl.ds(src * 2 * head, 2 * head)]
+        return pltpu.make_async_remote_copy(src_ref=o_st.at[pl.ds(0, rows)], dst_ref=dst, send_sem=o_send.at[0, 0],
+                                            recv_sem=o_recv.at[z_row, src], device_id={"tp": 0}, device_id_type=MESH)
 
     def attend(q_idx, gidx, wide, start_tile, n_steps, with_first):
         q_blk = q_v[pl.ds(pl.multiple_of(q_idx * TQ, TQ), TQ), :]
@@ -538,7 +476,10 @@
 
     def out_product(first, count):
         for row in range(first, first + count):
-            o_far(row)
+            for src in range(n_tp):
+                @pl.when(tp != src)
+                def _(row=row, src=src):
+                    o_arrival(row, src).wait_recv()
         lhs = og[first:first + count].reshape(count * rows, n_tp * 2 * head)
         for col in range(0, cols, 384):
             w_cols = jnp.concatenate([wo_v[NY * y_idx + z_idx, :, :, col:col + 384].reshape(2 * head, 384)
@@ -572,40 +513,38 @@
         for sub in range(2):
             tile = 2 * q_idx + sub
 
-            @pl.when(tile % NY != my_y)
-            def _(tile=tile):
-                oy_copy(tile, tp).start()
+            for z_dst in range(NY):
+                mine = (tile % NY == my_y) & (my_z == z_dst)
+
+                @pl.when(jnp.logical_not(mine))
+                def _(tile=tile, z_dst=z_dst):
+                    o_copy(tile, z_dst).start()
 
             @pl.when(tile % NY == my_y)
             def _(tile=tile):
                 og[tile // NY, :, pl.ds(pl.multiple_of(tp * 2 * head, 2 * head), 2 * head)] = \
                     o_st[pl.ds(pl.multiple_of(tile * rows, rows), rows), :]
 
-        @pl.when((q_idx >= 2) & (q_idx % 2 == 0))
-        def _():
-            o_round(q_idx // 2 - 1)
-
-        @pl.when((q_idx >= 3) & (q_idx % 2 == 1))
-        def _():
-            o_pass((q_idx - 3) // 2)
-
-        @pl.when(q_idx == 4)
+        @pl.when(q_idx == 5)
         def _():
             wo_second()
 
         @pl.when(q_idx == 6)
         def _():
             wo_last()
-            out_product(0, 2)
-            y_put(0, 2)
+            out_product(0, 1)
+            y_put(0, 1)
+
+        @pl.when(q_idx == 7)
+        def _():
+            out_product(1, 1)
+            y_put(1, 1)
 
         return carry
 
     lax.fori_loop(0, 2 * chunk // TQ, q_step, 0)
 
-    o_round(NY - 1)
     out_product(2, 1)
-    o_pass(NY - 1)
     y_put(2, 1)
     out_product(3, 1)
     y_put(3, 1)
@@ -616,13 +555,12 @@
     y_out = pltpu.make_async_copy(yv, y_hbm, y_sem)
     y_out.start()
     for tile in range(n_tp):
-        @pl.when(tile % NY != my_y)
-        def _(tile=tile):
-            oy_copy(tile, tp).wait_send()
-    for row in range(NY):
-        for side, z_src in ((0, zm), (1, zp)):
-            oz_copy(row, my_z, side).wait_send()
-            of_copy(row, z_src, side).wait_send()
+        for z_dst in range(NY):
+            mine = (tile % NY == my_y) & (my_z == z_dst)
+
+            @pl.when(jnp.logical_not(mine))
+            def _(tile=tile, z_dst=z_dst):
+                o_copy(tile, z_dst).wait_send()
     for z_dst in range(NY):
         @pl.when(my_z != z_dst)
         def _(z_dst=z_dst):
@@ -636,11 +574,8 @@
     for slot in range(3):
         for kind in range(2):
             share_copy(kind, my_z, my_c, slot).wait_send()
-    for slot in range(2):
+    for slot in range(3):
         a_copy(0, my_z, 0, slot).wait_send()
-        far_copy(0, slot).wait_send()
-        for kind in range(2):
-            pass_copy(kind, slot, my_z).wait_send()
     for z_idx in range(NY):
         kv_own(z_idx, done)
         kv_direct(z_idx, done, False)
@@ -673,7 +608,6 @@
                 pltpu.VMEM((seq_loc, two_head), bf16),
                 pltpu.VMEM((n_sp * seq_loc, two_head), bf16),
                 pltpu.VMEM((NY - 1, seq_loc // NY, two_head), bf16),
-                pltpu.VMEM((2, 2, seq_loc // (2 * NY), two_head), bf16),
                 pltpu.VMEM((n_tp, NY, wo_rows, cols), bf16),
                 pltpu.VMEM((2 * TQ, WINDOW + TQ), f32),
                 pltpu.VMEM((2 * TQ, head), f32),
@@ -684,10 +618,9 @@
                 pltpu.VMEM((NY, rows, n_tp * two_head), bf16),
                 pltpu.VMEM((NY, rows, cols), bf16),
                 pltpu.VMEM((rows, d_model), bf16),
-                dma, dma((3,)), dma((4,)), dma((NY, 2)), dma((40,)), dma((2, NY, NY + 1, 2)), dma((2, 3)), dma((2, NY)), dma((2, 2)), dma((2, NY)),
-                dma((2, 2)), dma((2, 2)), dma((2, 2)), dma((2, 2)), dma((NY, 6)), dma((2 * n_sp, 2)), dma, dma((NY,)), dma((NY,)), dma((4,)),
-                dma((NY, 2)), dma((16,)), dma((n_sp, 2)), dma((n_tp,)), dma((NY, NY)), dma((NY, 2)), dma((NY, NY)), dma((NY, 2)), dma((NY, 2)),
-                dma((NY,)), dma((NY,)), dma,
+                dma, dma((3,)), dma((4,)), dma((NY, 2)), dma((40,)), dma((2, NY, NY + 1, 2)), dma((2, 3)), dma((2, NY)), dma((2, 3)), dma((2, NY)),
+                dma((NY, 6)), dma((2 * n_sp, 2)), dma, dma((NY,)), dma((NY,)), dma((4,)), dma((NY, 2)), dma((4,)), dma((NY, 2)),
+                dma((n_tp, NY)), dma((NY, n_tp)), dma((NY,)), dma((NY,)), dma,
             ],
             compiler_params=pltpu.CompilerParams(collective_id=1, has_side_effects=True, vmem_limit_bytes=67043328),
             name="layer",

time: 191 us -> 179 us (0.937)
  the two profiles are of different devices: /device:TPU:102 before, /device:TPU:123 now
where the time goes in v7:
time: 179 us
  Pallas kernels  173 us (97%)
  local copies, waits for them, and re-layouts  5.74 us (3%)
    pallas_call x1, Pallas kernels, local_attn(): pl.pallas_call(layer_kernel, out_shape=jax.ShapeDtypeStruct((rows, d_mode...  173 us
    unnamed x2, local copies, waits for them, and re-layouts  5.74 us

profile of v7, /device:TPU:123, one launch (start us, length us, event | category | flops | bytes accessed | tf_op | source)
XLA Modules:
  0.0 179.2 jit_solution(5956720187154174028)
XLA Ops:
  0.0 3.4 %copy.8 = bf16[576,8,2,128]{3,1,2,0:T(8,128)(2,1)} copy(bf16[576,8,2,128]{3,2,1,0:T(2,128)(2,1)} %bitcast.8) | data formatting | bytes 4718592
  3.4 173.4 %layer.1 = bf16[128,4608]{1,0:T(8,128)(2,1)} custom-call(bf16[128,4608]{1,0:T(8,128)(2,1)} %x_hbm.1, bf16[4608,256]{1,0:T(8,128)(2,1)} %bitcast.7, bf16[4608,128]{1,0:T(8,128)(2,1)} %bitcast.10, bf16[4608,128]{1,0:T(8,128)(2,1)} %bitcast.11, bf16[4,64,4608]{2,1,0:T(8,128)(2,1)} %bitcast.9), custom_call_target="tpu_custom_call" | custom-call | tf_op jit(solution)/shard_map/layer/pallas_call | solution.py:599
  176.8 2.4 %copy.10 = bf16[128,4608]{1,0:T(8,128)(2,1)} copy(bf16[128,4608]{1,0:T(8,128)(2,1)} %layer.1) | data formatting | bytes 2359296

commit v8 on v7

--- a/solution.py
+++ b/solution.py
@@ -399,16 +399,16 @@
     def o_copy(tile, z_dst):
         y_dst, z_row = tile % NY, tile // NY
         src = o_st.at[pl.ds(pl.multiple_of(tile * rows, rows), rows)]
-        dst = og.at[z_row, :, pl.ds(pl.multiple_of(tp * 2 * head, 2 * head), 2 * head)]
+        dst = og.at[z_row, tp]
         return pltpu.make_async_remote_copy(src_ref=src, dst_ref=dst, send_sem=o_send.at[tile, z_dst], recv_sem=o_recv.at[z_row, tp],
                                             device_id={"tp": NY * z_dst + y_dst}, device_id_type=MESH)
 
     def o_arrival(z_row, src):
-        dst = og.at[z_row, :, pl.ds(src * 2 * head, 2 * head)]
+        dst = og.at[z_row, src]
         return pltpu.make_async_remote_copy(src_ref=o_st.at[pl.ds(0, rows)], dst_ref=dst, send_sem=o_send.at[0, 0],
                                             recv_sem=o_recv.at[z_row, src], device_id={"tp": 0}, device_id_type=MESH)
 
-    def attend(q_idx, gidx, wide, start_tile, n_steps, with_first):
+    def attend(q_idx, gidx, start_tile, n_wide, n_narrow, with_first):
         q_blk = q_v[pl.ds(pl.multiple_of(q_idx * TQ, TQ), TQ), :]
         q_two = jnp.concatenate([q_blk[:, :head], q_blk[:, head:]], axis=0)
 
@@ -418,7 +418,7 @@
         def values(tile, width):
             return kv_v[pl.ds(pl.multiple_of(tile * TQ, TQ), width), head:2 * head]
 
-        per = wide // TQ
+        per = WIDE // TQ
         scores = jnp.where(col_i <= row_i, dot_nt(q_two, keys(gidx, TQ)) * coef, NEG_BIG)
         s_v[:, 0:TQ] = scores
         best = lane_max(scores)
@@ -428,13 +428,25 @@
             best = jnp.maximum(best, lane_max(scores))
         mx_v[...] = best
 
-        def score_step(idx, carry):
-            part = dot_nt(q_two, keys(start_tile + per * idx, wide)) * coef
-            s_v[:, pl.ds(pl.multiple_of(2 * TQ + idx * wide, TQ), wide)] = part
+        def score_step(tile, width):
+            part = dot_nt(q_two, keys(start_tile + tile, width)) * coef
+            s_v[:, pl.ds(pl.multiple_of((2 + tile) * TQ, TQ), width)] = part
             mx_v[...] = jnp.maximum(mx_v[...], lane_max(part))
-            return carry
-
-        lax.fori_loop(0, n_steps, score_step, 0)
+
+        def each_step(step):
+            def wide_step(idx, carry):
+                step(per * idx, WIDE)
+                return carry
+
+            def narrow_step(idx, carry):
+                step(per * n_wide + idx, TQ)
+                return carry
+
+            lax.fori_loop(0, n_wide, wide_step, 0)
+            if n_narrow is not None:
+                lax.fori_loop(0, n_narrow, narrow_step, 0)
+
+        each_step(score_step)
         row_best = jnp.max(mx_v[...], axis=1, keepdims=True)
         mb_v[...] = jnp.broadcast_to(row_best, mb_v.shape)
 
@@ -457,13 +469,12 @@
         l_v[...] = total
         acc_v[...] = acc
 
-        def value_step(idx, carry):
-            prob, total = probs(2 * TQ + idx * wide, wide)
+        def value_step(tile, width):
+            prob, total = probs((2 + tile) * TQ, width)
             l_v[...] += total
-            acc_v[...] += jnp.dot(prob, values(start_tile + per * idx, wide), preferred_element_type=jnp.float32)
-            return carry
-
-        lax.fori_loop(0, n_steps, value_step, 0)
+            acc_v[...] += jnp.dot(prob, values(start_tile + tile, width), preferred_element_type=jnp.float32)
+
+        each_step(value_step)
         denom = jnp.sum(l_v[...], axis=1, keepdims=True)
         out = (acc_v[...] / denom).astype(jnp.bfloat16)
         out = jnp.concatenate([out[:TQ], out[TQ:]], axis=1)
@@ -480,7 +491,7 @@
                 @pl.when(tp != src)
                 def _(row=row, src=src):
                     o_arrival(row, src).wait_recv()
-        lhs = og[first:first + count].reshape(count * rows, n_tp * 2 * head)
+        lhs = jnp.concatenate([og[first:first + count, src].reshape(count * rows, 2 * head) for src in range(n_tp)], axis=1)
         for col in range(0, cols, 384):
             w_cols = jnp.concatenate([wo_v[NY * y_idx + z_idx, :, :, col:col + 384].reshape(2 * head, 384)
                                       for z_idx in range(NY) for y_idx in range(NY)], axis=0)
@@ -504,11 +515,11 @@
 
         @pl.when(gidx >= WINDOW // TQ)
         def _():
-            attend(q_idx, gidx, WIDE, gidx - WINDOW // TQ + 1, N_WIDE, True)
+            attend(q_idx, gidx, gidx - WINDOW // TQ + 1, N_WIDE, None, True)
 
         @pl.when(gidx < WINDOW // TQ)
         def _():
-            attend(q_idx, gidx, TQ, 0, gidx, False)
+            attend(q_idx, gidx, 0, gidx // (WIDE // TQ), gidx % (WIDE // TQ), False)
 
         for sub in range(2):
             tile = 2 * q_idx + sub
@@ -522,28 +533,19 @@
 
             @pl.when(tile % NY == my_y)
             def _(tile=tile):
-                og[tile // NY, :, pl.ds(pl.multiple_of(tp * 2 * head, 2 * head), 2 * head)] = \
-                    o_st[pl.ds(pl.multiple_of(tile * rows, rows), rows), :]
+                og[tile // NY, tp] = o_st[pl.ds(pl.multiple_of(tile * rows, rows), rows), :]
 
         @pl.when(q_idx == 5)
         def _():
             wo_second()
 
-        @pl.when(q_idx == 6)
-        def _():
-            wo_last()
-            out_product(0, 1)
-            y_put(0, 1)
-
-        @pl.when(q_idx == 7)
-        def _():
-            out_product(1, 1)
-            y_put(1, 1)
-
         return carry
 
     lax.fori_loop(0, 2 * chunk // TQ, q_step, 0)
 
+    wo_last()
+    out_product(0, 2)
+    y_put(0, 2)
     out_product(2, 1)
     y_put(2, 1)
     out_product(3, 1)
@@ -615,7 +617,7 @@
                 pltpu.VMEM((2 * TQ, head), f32),
                 pltpu.VMEM((2 * TQ, head), f32),
                 pltpu.VMEM((seq_loc, two_head), bf16),
-                pltpu.VMEM((NY, rows, n_tp * two_head), bf16),
+                pltpu.VMEM((NY, n_tp, rows, two_head), bf16),
                 pltpu.VMEM((NY, rows, cols), bf16),
                 pltpu.VMEM((rows, d_model), bf16),
                 dma, dma((3,)), dma((4,)), dma((NY, 2)), dma((40,)), dma((2, NY, NY + 1, 2)), dma((2, 3)), dma((2, NY)), dma((2, 3)), dma((2, NY)),

time: 179 us -> 173 us (0.966)
  the two profiles are of different devices: /device:TPU:123 before, /device:TPU:114 now
where the time goes in v8:
time: 173 us
  Pallas kernels  167 us (97%)
  local copies, waits for them, and re-layouts  5.74 us (3%)
    pallas_call x1, Pallas kernels, local_attn(): pl.pallas_call(layer_kernel, out_shape=jax.ShapeDtypeStruct((rows, d_mode...  167 us
    unnamed x2, local copies, waits for them, and re-layouts  5.74 us

profile of v8, /device:TPU:114, one launch (start us, length us, event | category | flops | bytes accessed | tf_op | source)
XLA Modules:
  0.0 172.8 jit_solution(10322454577782957449)
XLA Ops:
  0.0 3.4 %copy.8 = bf16[576,8,2,128]{3,1,2,0:T(8,128)(2,1)} copy(bf16[576,8,2,128]{3,2,1,0:T(2,128)(2,1)} %bitcast.8) | data formatting | bytes 4718592
  3.4 167.1 %layer.1 = bf16[128,4608]{1,0:T(8,128)(2,1)} custom-call(bf16[128,4608]{1,0:T(8,128)(2,1)} %x_hbm.1, bf16[4608,256]{1,0:T(8,128)(2,1)} %bitcast.7, bf16[4608,128]{1,0:T(8,128)(2,1)} %bitcast.10, bf16[4608,128]{1,0:T(8,128)(2,1)} %bitcast.11, bf16[4,64,4608]{2,1,0:T(8,128)(2,1)} %bitcast.9), custom_call_target="tpu_custom_call" | custom-call | tf_op jit(solution)/shard_map/layer/pallas_call | solution.py:601
  170.4 2.4 %copy.10 = bf16[128,4608]{1,0:T(8,128)(2,1)} copy(bf16[128,4608]{1,0:T(8,128)(2,1)} %layer.1) | data formatting | bytes 2359296

commit v9 on v8

--- a/solution.py
+++ b/solution.py
@@ -22,7 +22,7 @@
 
 
 def layer_kernel(x_hbm, wq_hbm, wk_hbm, wv_hbm, wo_hbm, y_hbm, xg, wq_v, wkv_v, q_v, kv_v, kv_st, wo_v, s_v, mx_v, mb_v, l_v, acc_v, o_st,
-                 og, yst, yv, x_sem, wl_sem, x_send, x_recv, w_send, w_recv, share_send, share_recv, a_send, a_recv,
+                 og, yst, raw_v, x_sem, wl_sem, x_send, x_recv, w_send, w_recv, share_send, share_recv, a_send, a_recv,
                  kv_send, kv_recv, wo_sem, wo_send, wo_recv, wy_send, wy_recv, sl_send, sl_recv, o_send, o_recv,
                  y_send, y_recv, y_sem):
     sp = lax.axis_index("sp")
@@ -45,7 +45,7 @@
     x_load.start()
     w_loads = (pltpu.make_async_copy(wk_hbm, wkv_v.at[my_z, :, 0:head], wl_sem.at[0]),
                pltpu.make_async_copy(wv_hbm, wkv_v.at[my_z, :, head:2 * head], wl_sem.at[1]),
-               pltpu.make_async_copy(wq_hbm, wq_v.at[my_z], wl_sem.at[2]))
+               pltpu.make_async_copy(wq_hbm.at[pl.ds(0, raw_v.shape[0])], raw_v, wl_sem.at[2]))
     for load in w_loads:
         load.start()
 
@@ -323,6 +323,24 @@
     def w_full(kind, z_src, slot):
         share_copy(kind, z_src, 1 - my_c, slot).wait_recv()
 
+    def split_heads():
+        size = mx_v.shape[0]
+        count = raw_v.shape[0] // size
+        for part_idx in range(2):
+            load = pltpu.make_async_copy(wq_hbm.at[pl.ds(part_idx * raw_v.shape[0], raw_v.shape[0])], raw_v, wl_sem.at[2])
+            if part_idx:
+                load.start()
+            load.wait()
+
+            def body(idx, carry, part_idx=part_idx):
+                mx_v[...] = raw_v[pl.ds(pl.multiple_of(idx * size, size), size), :].astype(jnp.float32)
+                at = pl.ds(pl.multiple_of((part_idx * count + idx) * (size // 2), size // 2), size // 2)
+                for sub in range(2):
+                    wq_v[my_z, at, sub * head:(sub + 1) * head] = mx_v[pl.ds(sub, size // 2, stride=2), :].astype(jnp.bfloat16)
+                return carry
+
+            lax.fori_loop(0, count, body, 0)
+
     x_load.wait()
     x_put(my_y, 0, 2, yp)
     x_put(my_y, 0, 2, ym)
@@ -332,7 +350,7 @@
     w_slices(0)
     w_own_rest(0)
     wo_z_start()
-    w_loads[2].wait()
+    split_heads()
     w_own_slice(1)
     w_far_slice(0)
     own_products([my_y])
@@ -356,7 +374,7 @@
         x_wait(yo, first, 1)
     own_products([yo])
     kv_own(my_z, start)
-    for slot, z_dst in enumerate((zo, zm, zp)):
+    for slot, z_dst in enumerate((zm, zp, zo)):
         w_full(0, z_dst, slot)
         products(0, z_dst, slot)
         a_start(0, z_dst, slot)
@@ -364,20 +382,20 @@
     w_ring(1, zo)
     wo_y_start()
     kv_direct(my_z, start, True)
-    for z_src in (zo, zm, zp):
+    for z_src in (zm, zp, zo):
         a_wait(0, z_src)
         kv_own(z_src, start)
     for slot, z_src in enumerate((zm, zp, zo)):
         w_share(1, z_src, slot)
     kv_relay(my_z, start, True)
-    for slot, z_dst in enumerate((zo, zm, zp)):
+    for slot, z_dst in enumerate((zm, zp, zo)):
         w_full(1, z_dst, slot)
         products(1, z_dst, slot)
         a_start(1, z_dst, slot)
         kv_direct(z_dst, start, True)
         if slot == 0:
             wo_y_pass()
-    for z_src in (zo, zm, zp):
+    for z_src in (zm, zp, zo):
         kv_relay(z_src, start, True)
     wo_first()
     for z_src in (zm, zp, zo):
@@ -482,8 +500,10 @@
 
     def y_copy(z_dst, z_src):
         return pltpu.make_async_remote_copy(
-            src_ref=yst.at[z_dst], dst_ref=yv.at[:, pl.ds(pl.multiple_of(z_src * cols, 128), cols)],
+            src_ref=yst.at[z_dst], dst_ref=y_hbm.at[:, pl.ds(pl.multiple_of(z_src * cols, 128), cols)],
             send_sem=y_send.at[z_dst], recv_sem=y_recv.at[z_src], device_id={"tp": NY * z_dst + my_y}, device_id_type=MESH)
+
+    y_own = pltpu.make_async_copy(yst.at[my_z], y_hbm.at[:, pl.ds(pl.multiple_of(my_z * cols, 128), cols)], y_sem)
 
     def out_product(first, count):
         for row in range(first, first + count):
@@ -506,7 +526,7 @@
 
             @pl.when(my_z == z_dst)
             def _(z_dst=z_dst):
-                yv[:, pl.ds(pl.multiple_of(my_z * cols, 128), cols)] = yst[z_dst]
+                y_own.start()
 
     def q_step(q_idx, carry):
         tiles = chunk // TQ
@@ -554,8 +574,6 @@
         @pl.when(my_z != z_src)
         def _(z_src=z_src):
             y_copy(z_src, z_src).wait_recv()
-    y_out = pltpu.make_async_copy(yv, y_hbm, y_sem)
-    y_out.start()
     for tile in range(n_tp):
         for z_dst in range(NY):
             mine = (tile % NY == my_y) & (my_z == z_dst)
@@ -582,7 +600,7 @@
         kv_own(z_idx, done)
         kv_direct(z_idx, done, False)
         kv_relay(z_idx, done, False)
-    y_out.wait()
+    y_own.wait()
 
 
 def solution(mesh):
@@ -619,14 +637,14 @@
                 pltpu.VMEM((seq_loc, two_head), bf16),
                 pltpu.VMEM((NY, n_tp, rows, two_head), bf16),
                 pltpu.VMEM((NY, rows, cols), bf16),
-                pltpu.VMEM((rows, d_model), bf16),
+                pltpu.VMEM((d_model, head), bf16),
                 dma, dma((3,)), dma((4,)), dma((NY, 2)), dma((40,)), dma((2, NY, NY + 1, 2)), dma((2, 3)), dma((2, NY)), dma((2, 3)), dma((2, NY)),
                 dma((NY, 6)), dma((2 * n_sp, 2)), dma, dma((NY,)), dma((NY,)), dma((4,)), dma((NY, 2)), dma((4,)), dma((NY, 2)),
                 dma((n_tp, NY)), dma((NY, n_tp)), dma((NY,)), dma((NY,)), dma,
             ],
             compiler_params=pltpu.CompilerParams(collective_id=1, has_side_effects=True, vmem_limit_bytes=67043328),
             name="layer",
-        )(x_part, w_query.reshape(d_model, two_head), w_key.reshape(d_model, head), w_value.reshape(d_model, head),
+        )(x_part, w_query.reshape(heads_loc * d_model, head), w_key.reshape(d_model, head), w_value.reshape(d_model, head),
           w_out.reshape(NY, wo_rows, d_model))
 
     return jax.shard_map(local_attn, mesh=mesh, in_specs=(P(("dp", "sp", "tp"), None), P(None, "tp", None), P(None, "tp", None), P(None, "tp", None), P("tp", None, None)), out_specs=P(("dp", "sp", "tp"), None), check_vma=False)

time: 173 us -> 167 us (0.965)
  the two profiles are of different devices: /device:TPU:114 before, /device:TPU:23 now
where the time goes in v9:
time: 167 us; the launch traced here: 166 us
  Pallas kernels  164 us (98%)
  local copies, waits for them, and re-layouts  2.36 us (1%)
    pallas_call x1, Pallas kernels, local_attn(): pl.pallas_call(layer_kernel, out_shape=jax.ShapeDtypeStruct((rows, d_mode...  164 us

profile of v9, /device:TPU:23, one launch (start us, length us, event | category | flops | bytes accessed | tf_op | source)
XLA Modules:
  0.0 166.4 jit_solution(15956797467852267712)
XLA Ops:
  0.0 164.0 %layer.1 = bf16[128,4608]{1,0:T(8,128)(2,1)} custom-call(bf16[128,4608]{1,0:T(8,128)(2,1)} %x_hbm.1, bf16[9216,128]{1,0:T(8,128)(2,1)} %bitcast.4, bf16[4608,128]{1,0:T(8,128)(2,1)} %bitcast.6, bf16[4608,128]{1,0:T(8,128)(2,1)} %bitcast.7, bf16[4,64,4608]{2,1,0:T(8,128)(2,1)} %bitcast.5), custom_call_target="tpu_custom_call" | custom-call | tf_op jit(solution)/shard_map/layer/pallas_call | solution.py:619
  164.0 2.4 %copy.7 = bf16[128,4608]{1,0:T(8,128)(2,1)} copy(bf16[128,4608]{1,0:T(8,128)(2,1)} %layer.1) | data formatting | bytes 2359296

commit v10 on v9

--- a/solution.py
+++ b/solution.py
@@ -13,7 +13,7 @@
 MESH = pl.DeviceIdType.MESH
 NY = 4
 TQ = 256
-WIDE = 768
+WIDE = 1280
 N_WIDE = (WINDOW - TQ) // WIDE
 
 

time: 167 us -> 165 us (0.988)
  no operation moved by 1% of the time
where the time goes in v10:
time: 165 us
  Pallas kernels  163 us (99%)
  local copies, waits for them, and re-layouts  2.36 us (1%)
    pallas_call x1, Pallas kernels, local_attn(): pl.pallas_call(layer_kernel, out_shape=jax.ShapeDtypeStruct((rows, d_mode...  163 us

profile of v10, /device:TPU:23, one launch (start us, length us, event | category | flops | bytes accessed | tf_op | source)
XLA Modules:
  0.0 165.1 jit_solution(11517094157244455938)
XLA Ops:
  0.0 162.7 %layer.1 = bf16[128,4608]{1,0:T(8,128)(2,1)} custom-call(bf16[128,4608]{1,0:T(8,128)(2,1)} %x_hbm.1, bf16[9216,128]{1,0:T(8,128)(2,1)} %bitcast.4, bf16[4608,128]{1,0:T(8,128)(2,1)} %bitcast.6, bf16[4608,128]{1,0:T(8,128)(2,1)} %bitcast.7, bf16[4,64,4608]{2,1,0:T(8,128)(2,1)} %bitcast.5), custom_call_target="tpu_custom_call" | custom-call | tf_op jit(solution)/shard_map/layer/pallas_call | solution.py:619
  162.7 2.4 %copy.7 = bf16[128,4608]{1,0:T(8,128)(2,1)} copy(bf16[128,4608]{1,0:T(8,128)(2,1)} %layer.1) | data formatting | bytes 2359296

commit v11 on v10

--- a/solution.py
+++ b/solution.py
@@ -555,7 +555,7 @@
             def _(tile=tile):
                 og[tile // NY, tp] = o_st[pl.ds(pl.multiple_of(tile * rows, rows), rows), :]
 
-        @pl.when(q_idx == 5)
+        @pl.when(q_idx == 6)
         def _():
             wo_second()
 

time: 165 us -> 166 us (level)
  the two profiles are of different devices: /device:TPU:23 before, /device:TPU:30 now
where the time goes in v11:
time: 166 us
  Pallas kernels  163 us (98%)
  local copies, waits for them, and re-layouts  2.36 us (1%)
    pallas_call x1, Pallas kernels, local_attn(): pl.pallas_call(layer_kernel, out_shape=jax.ShapeDtypeStruct((rows, d_mode...  163 us

profile of v11, /device:TPU:30, one launch (start us, length us, event | category | flops | bytes accessed | tf_op | source)
XLA Modules:
  0.0 165.5 jit_solution(4310852002451261185)
XLA Ops:
  0.0 163.1 %layer.1 = bf16[128,4608]{1,0:T(8,128)(2,1)} custom-call(bf16[128,4608]{1,0:T(8,128)(2,1)} %x_hbm.1, bf16[9216,128]{1,0:T(8,128)(2,1)} %bitcast.4, bf16[4608,128]{1,0:T(8,128)(2,1)} %bitcast.6, bf16[4608,128]{1,0:T(8,128)(2,1)} %bitcast.7, bf16[4,64,4608]{2,1,0:T(8,128)(2,1)} %bitcast.5), custom_call_target="tpu_custom_call" | custom-call | tf_op jit(solution)/shard_map/layer/pallas_call | solution.py:619
  163.1 2.4 %copy.7 = bf16[128,4608]{1,0:T(8,128)(2,1)} copy(bf16[128,4608]{1,0:T(8,128)(2,1)} %layer.1) | data formatting | bytes 2359296
